TPU v7x, 128 devices: a whole 4x4x4 slice. The times are simulated.
128 devices in a mesh: group: 4 (over z_lo, core), space: 32 (over z_hi, y, x).
Axes of the slice: x: 4, y: 4, z: 4 (z_hi: 2, z_lo: 2; z = z_hi * 2 + z_lo), core: 2. Of those that a mesh axis runs over, the one named last changes fastest.
Arguments:
- latents: bfloat16 [16, 64, 128, 256], P('group', 'space'), may hold values from -6 to 6
- first_kernel: bfloat16 [3, 3, 3, 256, 256], replicated, may hold values from -0.078125 to 0.078125
- second_kernel: bfloat16 [3, 3, 3, 256, 256], replicated, may hold values from -0.078125 to 0.078125
- upstream: bfloat16 [16, 64, 128, 256], P('group', 'space'), may hold values from -6 to 6
Outputs:
- decoded: bfloat16 [16, 64, 128, 256], P('group', 'space')
- latent_grad: bfloat16 [16, 64, 128, 256], P('group', 'space')
- first_grad: float32 [3, 3, 3, 256, 256], replicated
- second_grad: float32 [3, 3, 3, 256, 256], replicated
All inputs are finite; a program needn't handle non-finite values.
Results may differ from a plain program's by a relative error of at most 0.0054.
Values may be sent and summed in bfloat16 or wider, within the bound.
No kernel may reach another device: no remote copies, remote signals or barrier semaphores. Data moves between devices by JAX's collectives and lax.ppermute only.
A program may use at most 192 MiB of HBM per device.

v0:
```python
import functools

import jax
import jax.numpy as jnp
from jax import lax
from jax.experimental import pallas as pl
from jax.experimental.pallas import tpu as pltpu
from jax.sharding import Mesh, PartitionSpec as P

GROUP = ("zl", "co")
SPACE = ("zh", "y", "x")
CHIPS = ("zl", "zh", "y", "x")
C = 256
W = 128
FRAMES = 4
EXT = FRAMES + 2
TAPS = 27
BF = jnp.bfloat16
F32 = jnp.float32
PASS_FLOPS = 2 * FRAMES * 2 * W * TAPS * C * C


def fill_ext(ext_ref, own_ref, rows_ref, time_ref, first, which):
    other = 0 if first == 2 else FRAMES
    for f in range(FRAMES):
        ext_ref[first + f, 0:W] = rows_ref[0, which, f]
        for r in range(2):
            ext_ref[first + f, (r + 1) * W : (r + 2) * W] = own_ref[f, r]
        ext_ref[first + f, 3 * W : 4 * W] = rows_ref[1, which, f]
    for f in range(2):
        for r in range(4):
            ext_ref[other + f, r * W : (r + 1) * W] = time_ref[f, r]


def shifted(value, by):
    height = value.shape[0]
    turned = pltpu.roll(value, by % height, 0)
    column = lax.broadcasted_iota(jnp.int32, value.shape, 0) % W
    edge = 0 if by > 0 else W - 1
    return jnp.where(column == edge, 0.0, turned)


def conv_frame(ext_ref, kernel_ref, t, transposed):
    parts = []
    for i in range(3):
        for j in range(3):
            frame = t + (2 - i if transposed else i)
            row = 2 - j if transposed else j
            parts.append(ext_ref[frame, row * W : (row + 2) * W])
    lhs = jnp.concatenate(parts, axis=1)
    sums = []
    for k in range(3):
        taps = [kernel_ref[(i * 3 + j) * 3 + k] for i in range(3) for j in range(3)]
        if transposed:
            rhs = jnp.concatenate(taps, axis=1)
            dims = (((1,), (1,)), ((), ()))
        else:
            rhs = jnp.concatenate(taps, axis=0)
            dims = (((1,), (0,)), ((), ()))
        sums.append(lax.dot_general(lhs, rhs, dims, preferred_element_type=F32))
    if transposed:
        return sums[1] + shifted(sums[0], -1) + shifted(sums[2], 1)
    return sums[1] + shifted(sums[0], 1) + shifted(sums[2], -1)


def gate_grad(values):
    s = jax.nn.sigmoid(values)
    return s * (1.0 + values * (1.0 - s))


def split_rows(value):
    return value.reshape(2, W, C)


def hidden_kernel(own_ref, rows_ref, time_ref, kernel_ref, hidden_ref, active_ref, ext_ref):
    fill_ext(ext_ref, own_ref, rows_ref, time_ref, 2, 0)

    def body(t, carry):
        hidden = conv_frame(ext_ref, kernel_ref, t, False)
        hidden_ref[t] = hidden
        active_ref[t] = split_rows((hidden * jax.nn.sigmoid(hidden)).astype(BF))
        return carry

    lax.fori_loop(0, FRAMES, body, 0)


def hidden_grad_kernel(own_ref, rows_ref, time_ref, kernel_ref, hidden_ref, out_ref, ext_ref):
    fill_ext(ext_ref, own_ref, rows_ref, time_ref, 0, 1)

    def body(t, carry):
        grad = conv_frame(ext_ref, kernel_ref, t, True)
        out_ref[t] = split_rows((grad * gate_grad(hidden_ref[t])).astype(BF))
        return carry

    lax.fori_loop(0, FRAMES, body, 0)


def decoded_kernel(own_ref, rows_ref, time_ref, kernel_ref, latents_ref, out_ref, ext_ref):
    fill_ext(ext_ref, own_ref, rows_ref, time_ref, 2, 0)

    def body(t, carry):
        branch = split_rows(conv_frame(ext_ref, kernel_ref, t, False))
        out_ref[t] = (latents_ref[t].astype(F32) + branch).astype(BF)
        return carry

    lax.fori_loop(0, FRAMES, body, 0)


def latent_grad_kernel(
    own_ref, rows_ref, time_ref, kernel_ref, latents_ref, upstream_ref, out_ref, ext_ref
):
    fill_ext(ext_ref, own_ref, rows_ref, time_ref, 0, 1)

    def body(t, carry):
        inner = split_rows(conv_frame(ext_ref, kernel_ref, t, True))
        gate = gate_grad(latents_ref[t].astype(F32))
        out_ref[t] = (upstream_ref[t].astype(F32) + inner * gate).astype(BF)
        return carry

    lax.fori_loop(0, FRAMES, body, 0)


def keep_first(core, value):
    return jnp.where(core == 0, value, pltpu.roll(value, C // 2, 0))


def shift_copies(value):
    wide = value.astype(F32)
    return [shifted(wide, -1).astype(BF), value, shifted(wide, 1).astype(BF)]


def put_tap(keep_ref, send_ref, tap, product):
    for ref, low in ((keep_ref, 0), (send_ref, C // 2)):
        half = product[low : low + C // 2].astype(ref.dtype)
        for b in range(2):
            ref[:, b, tap] = half[:, b * 128 : (b + 1) * 128].reshape(16, 8, 128)


def second_grad_kernel(
    core_ref, active_ref, own_ref, rows_ref, time_ref, keep_ref, send_ref, ext_ref, across_ref, turn_ref
):
    core = core_ref[0]
    fill_ext(ext_ref, own_ref, rows_ref, time_ref, 0, 1)
    for f in range(EXT):
        for k, copy in enumerate(shift_copies(ext_ref[f])):
            across_ref[k, f] = copy
    for t in range(FRAMES):
        flat = active_ref[t].reshape(2 * W, C).astype(F32)
        turn_ref[:, t * 2 * W : (t + 1) * 2 * W] = keep_first(core, flat.T).astype(BF)

    def body(i, carry):
        for j in range(3):
            for k in range(3):
                rhs = jnp.concatenate(
                    [across_ref[k, t + 2 - i, (2 - j) * W : (4 - j) * W] for t in range(FRAMES)], axis=0
                )
                product = jnp.dot(turn_ref[...], rhs, preferred_element_type=F32)
                put_tap(keep_ref, send_ref, i * 9 + j * 3 + k, product)
        return carry

    lax.fori_loop(0, 3, body, 0)


def first_grad_kernel(
    core_ref, grad_ref, own_ref, rows_ref, time_ref, keep_ref, send_ref, ext_ref, across_ref, turn_ref
):
    core = core_ref[0]
    fill_ext(ext_ref, own_ref, rows_ref, time_ref, 2, 0)
    for t in range(FRAMES):
        for k, copy in enumerate(shift_copies(grad_ref[t].reshape(2 * W, C))):
            across_ref[k, t * 2 * W : (t + 1) * 2 * W] = copy
    for f in range(EXT):
        turn_ref[f] = keep_first(core, ext_ref[f].astype(F32).T).astype(BF)

    def body(i, carry):
        for j in range(3):
            lhs = jnp.concatenate(
                [turn_ref[t + i, :, j * W : (j + 2) * W] for t in range(FRAMES)], axis=1
            )
            for k in range(3):
                product = jnp.dot(lhs, across_ref[k], preferred_element_type=F32)
                put_tap(keep_ref, send_ref, i * 9 + j * 3 + k, product)
        return carry

    lax.fori_loop(0, 3, body, 0)


def cost(flops, moved):
    return pl.CostEstimate(flops=flops, bytes_accessed=moved, transcendentals=0)


def whole(kernel, outs, scratch, limit, name, smem=0):
    def call(*args):
        moved = sum(a.size * a.dtype.itemsize for a in args)
        moved += sum(o.size * o.dtype.itemsize for o in outs)
        specs = [
            pl.BlockSpec(memory_space=pltpu.SMEM if n < smem else pltpu.VMEM) for n in range(len(args))
        ]
        return pl.pallas_call(
            kernel,
            out_shape=outs,
            in_specs=specs,
            out_specs=[pl.BlockSpec(memory_space=pltpu.VMEM) for _ in outs],
            scratch_shapes=scratch,
            compiler_params=pltpu.CompilerParams(vmem_limit_bytes=limit << 20),
            cost_estimate=cost(PASS_FLOPS, moved),
            name=name,
        )(*args)

    return call


STEP = 3


def assemble_kernel(core_ref, own2_ref, own1_ref, far2_ref, far1_ref, first_ref, second_ref):
    core = core_ref[0]
    mine = pl.multiple_of(core * 128, 128)
    theirs = pl.multiple_of((1 - core) * 128, 128)
    for out, own, far in ((second_ref, own2_ref, far2_ref), (first_ref, own1_ref, far1_ref)):
        for p in range(STEP):
            for b in range(2):
                lanes = slice(b * 128, (b + 1) * 128)
                out[p, pl.ds(mine, 128), lanes] = own[0, :, b, p].astype(F32).reshape(128, 128)
                out[p, pl.ds(theirs, 128), lanes] = far[0, :, b, p].astype(F32).reshape(128, 128)


def assemble(core, own, far):
    own, far = (v.reshape(2, 16, 2, TAPS, 8, 128) for v in (own, far))
    block = (1, 16, 2, STEP, 8, 128)
    second = pl.BlockSpec(block, lambda p: (0, 0, 0, p, 0, 0))
    first = pl.BlockSpec(block, lambda p: (1, 0, 0, p, 0, 0))
    out = pl.BlockSpec((STEP, C, C), lambda p: (p, 0, 0))
    shape = jax.ShapeDtypeStruct((TAPS, C, C), F32)
    return pl.pallas_call(
        assemble_kernel,
        out_shape=(shape, shape),
        grid=(TAPS // STEP,),
        in_specs=[pl.BlockSpec(memory_space=pltpu.SMEM), second, first, second, first],
        out_specs=(out, out),
        compiler_params=pltpu.CompilerParams(vmem_limit_bytes=16 << 20),
        cost_estimate=cost(1 << 24, 28 << 20),
        name="assemble",
    )(core, own, own, far, far)


def total_kernel(parts_ref, out_ref):
    count = parts_ref.shape[0]

    def body(p, carry):
        total = parts_ref[0, p].astype(F32)
        for n in range(1, count):
            total = total + parts_ref[n, p].astype(F32)
        rounded = total.astype(BF)
        for n in range(count):
            out_ref[n, p] = rounded
        return carry

    lax.fori_loop(0, parts_ref.shape[1], body, 0)


def swap(value, axis, steps):
    count = lax.axis_size(axis)
    pairs = [(n, n + steps) for n in range(count) if 0 <= n + steps < count]
    return lax.ppermute(value, axis, pairs)


def edge_rows(one, two):
    to_above = jnp.stack([one[:, 0], two[:, 0]])
    to_below = jnp.stack([one[:, 1], two[:, 1]])
    return jnp.stack([swap(to_below, SPACE, 1), swap(to_above, SPACE, -1)])


def two_frames(own, rows, which, start):
    frames = slice(start, start + 2)
    return jnp.concatenate(
        [rows[0, which, frames][:, None], own[frames], rows[1, which, frames][:, None]], axis=1
    )


def local(latents, first_kernel, second_kernel, upstream):
    core = lax.axis_index("co").astype(jnp.int32).reshape(1)
    k1 = first_kernel.reshape(TAPS, C, C)
    k2 = second_kernel.reshape(TAPS, C, C)
    wide = latents.astype(F32)
    smooth = (wide * jax.nn.sigmoid(wide)).astype(BF)
    block = jax.ShapeDtypeStruct((FRAMES, 2, W, C), BF)
    ext = pltpu.VMEM((EXT, 4 * W, C), BF)

    rows = edge_rows(smooth, upstream)
    smooth_time = swap(two_frames(smooth, rows, 0, 2), GROUP, 1)
    up_time = swap(two_frames(upstream, rows, 1, 0), GROUP, -1)
    hidden, active = whole(
        hidden_kernel, (jax.ShapeDtypeStruct((FRAMES, 2 * W, C), F32), block), [ext], 24, "hidden"
    )(smooth, rows, smooth_time, k1)
    (hidden_grad,) = whole(hidden_grad_kernel, (block,), [ext], 24, "hidden_grad")(
        upstream, rows, up_time, k2, hidden
    )

    late = edge_rows(active, hidden_grad)
    active_time = swap(two_frames(active, late, 0, 2), GROUP, 1)
    grad_time = swap(two_frames(hidden_grad, late, 1, 0), GROUP, -1)

    half = (16, 2, TAPS, 8, 128)
    pair = (jax.ShapeDtypeStruct(half, F32), jax.ShapeDtypeStruct(half, BF))
    keep2, send2 = whole(
        second_grad_kernel,
        pair,
        [ext, pltpu.VMEM((3, EXT, 4 * W, C), BF), pltpu.VMEM((C, FRAMES * 2 * W), BF)],
        40,
        "second_grad",
        1,
    )(core, active, upstream, rows, up_time)
    keep1, send1 = whole(
        first_grad_kernel,
        pair,
        [ext, pltpu.VMEM((3, FRAMES * 2 * W, C), BF), pltpu.VMEM((EXT, C, 4 * W), BF)],
        40,
        "first_grad",
        1,
    )(core, hidden_grad, smooth, rows, smooth_time)

    across = [(0, 1), (1, 0)]
    got2 = lax.ppermute(send2, "co", across)
    got1 = lax.ppermute(send1, "co", across)
    chips = lax.axis_size(CHIPS)
    mine = jnp.stack([(keep2 + got2.astype(F32)).astype(BF), (keep1 + got1.astype(F32)).astype(BF)])
    mine = mine.reshape(chips, 64 // chips * TAPS, 8, 128)
    parts = lax.all_to_all(mine, CHIPS, 0, 0, tiled=False)
    (spread,) = whole(total_kernel, (jax.ShapeDtypeStruct(parts.shape, BF),), [], 16, "total")(parts)
    own = lax.all_to_all(spread, CHIPS, 0, 0, tiled=False)
    far = lax.ppermute(own, "co", across)

    (decoded,) = whole(decoded_kernel, (block,), [ext], 24, "decoded")(
        active, late, active_time, k2, latents
    )
    (latent_grad,) = whole(latent_grad_kernel, (block,), [ext], 24, "latent_grad")(
        hidden_grad, late, grad_time, k1, latents, upstream
    )
    first_grad, second_grad = assemble(core, own, far)
    shape = first_kernel.shape
    return (decoded, latent_grad, first_grad.reshape(shape), second_grad.reshape(shape))


def solution(mesh, sizes=(2, 2, 2, 4, 4)):
    fine = Mesh(mesh.devices.reshape(sizes), ("zl", "co", "zh", "y", "x"))
    placed = (P(GROUP, SPACE, None, None), P(), P(), P(GROUP, SPACE, None, None))
    return jax.shard_map(
        local,
        mesh=fine,
        in_specs=placed,
        out_specs=(P(GROUP, SPACE, None, None), P(GROUP, SPACE, None, None), P(), P()),
        check_vma=False,
    )
```

profile of v0, /device:TPU:96, one launch (start us, length us, event | category | flops | bytes accessed | tf_op | source)
XLA Modules:
  0.0 225.4 jit_solution(2021640014920989353)
XLA Ops:
  3.2 7.1 %collective-permute-start.1 = (bf16[2,4,128,256]{3,2,1,0:T(8,128)(2,1)S(1)}, bf16[2,4,128,256]{3,2,1,0:T(8,128)(2,1)S(1)}, u32[]{:S(2)}, u32[]{:S(2)}) collective-permute-start(bf16[2,4,128,256]{3,2,1,0:T(8,128)(2,1)S(1)} %pad_maximum_fusion.4), channel_id=1, source_target_pairs={{1,0},{2,1},{3,2},{4,3},{5,4},{6,5},{7,6},{8,7},{9,8},{10,9},{11,1... | collective-permute-start | bytes 1572872 | tf_op jit(solution)/shard_map/ppermute | solution.py:265
  10.4 1.9 collective-permute-start
  12.3 9.2 %collective-permute-done.1 = bf16[2,4,128,256]{3,2,1,0:T(8,128)(2,1)S(1)} collective-permute-done((bf16[2,4,128,256]{3,2,1,0:T(8,128)(2,1)S(1)}, bf16[2,4,128,256]{3,2,1,0:T(8,128)(2,1)S(1)}, u32[]{:S(2)}, u32[]{:S(2)}) %collective-permute-start.1) | collective-permute-done | bytes 524320 | tf_op jit(solution)/shard_map/ppermute | solution.py:265
  21.5 10.0 %collective-permute-done = bf16[2,4,128,256]{3,2,1,0:T(8,128)(2,1)S(1)} collective-permute-done((bf16[2,4,128,256]{3,2,1,0:T(8,128)(2,1)S(1)}, bf16[2,4,128,256]{3,2,1,0:T(8,128)(2,1)S(1)}, u32[]{:S(2)}, u32[]{:S(2)}) %collective-permute-start) | collective-permute-done | bytes 524320 | tf_op jit(solution)/shard_map/ppermute | solution.py:265
  34.3 3.6 %collective-permute-start.3 = (bf16[2,4,128,256]{3,2,1,0:T(8,128)(2,1)}, bf16[2,4,128,256]{3,2,1,0:T(8,128)(2,1)S(1)}, u32[]{:S(2)}, u32[]{:S(2)}) collective-permute-start(bf16[2,4,128,256]{3,2,1,0:T(8,128)(2,1)} %pad_maximum_fusion.6), channel_id=1, source_target_pairs={{32,0},{64,32},{96,64},{33,1},{65,33},{97,65},{34,2},{66,34},{98,6... | collective-permute-start | bytes 1572872 | tf_op jit(solution)/shard_map/ppermute | solution.py:265
  38.1 3.9 %collective-permute-done.2.time_ref = bf16[2,4,128,256]{3,2,1,0:T(8,128)(2,1)S(1)} collective-permute-done((bf16[2,4,128,256]{3,2,1,0:T(8,128)(2,1)S(1)}, bf16[2,4,128,256]{3,2,1,0:T(8,128)(2,1)S(1)}, u32[]{:S(2)}, u32[]{:S(2)}) %collective-permute-start.2) | collective-permute-done | bytes 524320 | tf_op jit(solution)/shard_map/ppermute | solution.py:265
  42.0 2.0 copy-done.3
  44.0 4.5 %hidden.1 = (f32[4,256,256]{2,1,0:T(8,128)S(1)}, bf16[4,2,128,256]{3,2,1,0:T(8,128)(2,1)S(1)}) custom-call(bf16[4,2,128,256]{3,2,1,0:T(8,128)(2,1)S(1)} %copy.13.own_ref, bf16[2,2,4,128,256]{4,3,2,1,0:T(8,128)(2,1)S(1)} %pad_maximum_fusion.1.rows_ref, bf16[2,4,128,256]{3,2,1,0:T(8,128)(2,1)S(1)} %collective-permute-done.2.time_ref, ...), custom_call_target="tpu_custom_call" | custom-call | flops 3623878656 | bytes 7208960 | tf_op jit(solution)/shard_map/hidden/pallas_call | solution.py:199
  48.6 4.6 %hidden_grad.1.own_ref.grad_ref = bf16[4,2,128,256]{3,2,1,0:T(8,128)(2,1)S(1)} custom-call(bf16[4,2,128,256]{3,2,1,0:T(8,128)(2,1)S(1)} %copy-done, bf16[2,2,4,128,256]{4,3,2,1,0:T(8,128)(2,1)S(1)} %pad_maximum_fusion.1.rows_ref, bf16[2,4,128,256]{3,2,1,0:T(8,128)(2,1)S(1)} %collective-permute-done.3.time_ref, bf16[27,256,256]{2,1,0:T(8,128)(2,1)S(1)} %bitcast.72, ...), custom_call_target="tpu_custom_call" | custom-call | flops 3623878656 | bytes 7208960 | tf_op jit(solution)/shard_map/hidden_grad/pallas_call | solution.py:199
  53.2 5.0 %first_grad.1 = (f32[16,2,27,8,128]{4,3,2,1,0:T(8,128)S(1)}, bf16[16,2,27,8,128]{4,3,2,1,0:T(8,128)(2,1)S(1)}) custom-call(s32[1]{0:T(128)} %bitcast.28.core_ref, bf16[4,2,128,256]{3,2,1,0:T(8,128)(2,1)S(1)} %hidden_grad.1.own_ref.grad_ref, bf16[4,2,128,256]{3,2,1,0:T(8,128)(2,1)S(1)} %copy.13.own_ref, ...), custom_call_target="tpu_custom_call" | custom-call | flops 3623878656 | bytes 7929860 | tf_op jit(solution)/shard_map/first_grad/pallas_call | solution.py:199
  58.3 5.6 %second_grad.1 = (f32[16,2,27,8,128]{4,3,2,1,0:T(8,128)S(1)}, bf16[16,2,27,8,128]{4,3,2,1,0:T(8,128)(2,1)S(1)}) custom-call(s32[1]{0:T(128)} %bitcast.28.core_ref, bf16[4,2,128,256]{3,2,1,0:T(8,128)(2,1)S(1)} %get-tuple-element.12.own_ref.active_ref, bf16[4,2,128,256]{3,2,1,0:T(8,128)(2,1)S(1)} %copy-done, ...), custom_call_target="tpu_custom_call" | custom-call | flops 3623878656 | bytes 7929860 | tf_op jit(solution)/shard_map/second_grad/pallas_call | solution.py:199
  64.8 2.9 %collective-permute-done.8 = bf16[16,2,27,8,128]{4,3,2,1,0:T(8,128)(2,1)S(1)} collective-permute-done((bf16[16,2,27,8,128]{4,3,2,1,0:T(8,128)(2,1)S(1)}, bf16[16,2,27,8,128]{4,3,2,1,0:T(8,128)(2,1)S(1)}, u32[]{:S(2)}, u32[]{:S(2)}) %collective-permute-start.8) | collective-permute-done | bytes 1769504 | tf_op jit(solution)/shard_map/ppermute | solution.py:324
  68.5 49.5 %all_to_all.10.parts_ref = bf16[64,27,8,128]{3,2,1,0:T(8,128)(2,1)S(1)} all-to-all(bf16[64,27,8,128]{3,2,1,0:T(8,128)(2,1)S(1)} %bitcast.76), channel_id=1, replica_groups=mesh['zl'=2,'co'=2,'zh'=2,'y'=4,'x'=4] {'zl','zh','y','x'}, dimensions={0} | all-to-all | bytes 7077888 | tf_op jit(solution)/shard_map/all_to_all | solution.py:329
  118.0 2.3 %total.1 = bf16[64,27,8,128]{3,2,1,0:T(8,128)(2,1)S(1)} custom-call(bf16[64,27,8,128]{3,2,1,0:T(8,128)(2,1)S(1)} %all_to_all.10.parts_ref), custom_call_target="tpu_custom_call" | custom-call | flops 3623878656 | bytes 7077888 | tf_op jit(solution)/shard_map/total/pallas_call | solution.py:199
  120.3 50.0 %all_to_all.11 = bf16[64,27,8,128]{3,2,1,0:T(8,128)(2,1)S(1)} all-to-all(bf16[64,27,8,128]{3,2,1,0:T(8,128)(2,1)S(1)} %total.1), channel_id=1, replica_groups=mesh['zl'=2,'co'=2,'zh'=2,'y'=4,'x'=4] {'zl','zh','y','x'}, dimensions={0} | all-to-all | bytes 7077888 | tf_op jit(solution)/shard_map/all_to_all | solution.py:331
  170.5 4.9 %collective-permute-start.5 = (bf16[2,4,128,256]{3,2,1,0:T(8,128)(2,1)S(1)}, bf16[2,4,128,256]{3,2,1,0:T(8,128)(2,1)S(1)}, u32[]{:S(2)}, u32[]{:S(2)}) collective-permute-start(bf16[2,4,128,256]{3,2,1,0:T(8,128)(2,1)S(1)} %pad_maximum_fusion.8), channel_id=1, source_target_pairs={{1,0},{2,1},{3,2},{4,3},{5,4},{6,5},{7,6},{8,7},{9,8},{10,9},{11,1... | collective-permute-start | bytes 1572872 | tf_op jit(solution)/shard_map/ppermute | solution.py:265
  175.5 2.1 collective-permute-start.4
  177.6 9.6 %collective-permute-done.5 = bf16[2,4,128,256]{3,2,1,0:T(8,128)(2,1)S(1)} collective-permute-done((bf16[2,4,128,256]{3,2,1,0:T(8,128)(2,1)S(1)}, bf16[2,4,128,256]{3,2,1,0:T(8,128)(2,1)S(1)}, u32[]{:S(2)}, u32[]{:S(2)}) %collective-permute-start.5) | collective-permute-done | bytes 524320 | tf_op jit(solution)/shard_map/ppermute | solution.py:265
  187.3 10.1 %collective-permute-done.4 = bf16[2,4,128,256]{3,2,1,0:T(8,128)(2,1)S(1)} collective-permute-done((bf16[2,4,128,256]{3,2,1,0:T(8,128)(2,1)S(1)}, bf16[2,4,128,256]{3,2,1,0:T(8,128)(2,1)S(1)}, u32[]{:S(2)}, u32[]{:S(2)}) %collective-permute-start.4) | collective-permute-done | bytes 524320 | tf_op jit(solution)/shard_map/ppermute | solution.py:265
  199.5 3.6 %collective-permute-start.7 = (bf16[2,4,128,256]{3,2,1,0:T(8,128)(2,1)S(1)}, bf16[2,4,128,256]{3,2,1,0:T(8,128)(2,1)S(1)}, u32[]{:S(2)}, u32[]{:S(2)}) collective-permute-start(bf16[2,4,128,256]{3,2,1,0:T(8,128)(2,1)S(1)} %pad_maximum_fusion.10), channel_id=1, source_target_pairs={{32,0},{64,32},{96,64},{33,1},{65,33},{97,65},{34,2},{66,34},{98,6... | collective-permute-start | bytes 1572872 | tf_op jit(solution)/shard_map/ppermute | solution.py:265
  203.3 4.7 %collective-permute-done.6.time_ref = bf16[2,4,128,256]{3,2,1,0:T(8,128)(2,1)S(1)} collective-permute-done((bf16[2,4,128,256]{3,2,1,0:T(8,128)(2,1)S(1)}, bf16[2,4,128,256]{3,2,1,0:T(8,128)(2,1)S(1)}, u32[]{:S(2)}, u32[]{:S(2)}) %collective-permute-start.6) | collective-permute-done | bytes 524320 | tf_op jit(solution)/shard_map/ppermute | solution.py:265
  208.0 5.3 %decoded.1 = bf16[4,2,128,256]{3,2,1,0:T(8,128)(2,1)} custom-call(bf16[4,2,128,256]{3,2,1,0:T(8,128)(2,1)S(1)} %get-tuple-element.12.own_ref.active_ref, bf16[2,2,4,128,256]{4,3,2,1,0:T(8,128)(2,1)S(1)} %pad_maximum_fusion.2.rows_ref, bf16[2,4,128,256]{3,2,1,0:T(8,128)(2,1)S(1)} %collective-permute-done.6.time_ref, bf16[27,256,256]{2,1,0:T(8,128)(2,1)S(1)} %bitcast.73, ...), custom_call_target="tpu_custom_call" | custom-call | flops 3623878656 | bytes 6684672 | tf_op jit(solution)/shard_map/decoded/pallas_call | solution.py:199
  213.3 5.5 %latent_grad.1 = bf16[4,2,128,256]{3,2,1,0:T(8,128)(2,1)} custom-call(bf16[4,2,128,256]{3,2,1,0:T(8,128)(2,1)S(1)} %hidden_grad.1.own_ref.grad_ref, bf16[2,2,4,128,256]{4,3,2,1,0:T(8,128)(2,1)S(1)} %pad_maximum_fusion.2.rows_ref, bf16[2,4,128,256]{3,2,1,0:T(8,128)(2,1)S(1)} %collective-permute-done.7.time_ref, bf16[27,256,256]{2,1,0:T(8,128)(2,1)S(1)} %bitcast.75, ...), custom_call_target="tpu_custom_call" | custom-call | flops 3623878656 | bytes 7208960 | tf_op jit(solution)/shard_map/latent_grad/pallas_call | solution.py:199
  218.8 6.6 %assemble.1 = (f32[27,256,256]{2,1,0:T(8,128)}, f32[27,256,256]{2,1,0:T(8,128)}) custom-call(s32[1]{0:T(128)} %bitcast.28.core_ref, bf16[2,16,2,27,8,128]{5,4,3,2,1,0:T(8,128)(2,1)S(1)} %bitcast.68, bf16[2,16,2,27,8,128]{5,4,3,2,1,0:T(8,128)(2,1)S(1)} %bitcast.69, bf16[2,16,2,27,8,128]{5,4,3,2,1,0:T(8,128)(2,1)S(1)} %bitcast.70, ...), custom_call_target="tpu_custom_call" | custom-call | flops 16777216 | bytes 29360128 | tf_op jit(solution)/shard_map/assemble/pallas_call | solution.py:235
  (45 shorter events, 9.8 us)
Async XLA Ops:
  2.0 31.5 %slice-start = ((bf16[4,2,128,256]{3,2,1,0:T(8,128)(2,1)}), bf16[2,2,128,256]{3,2,1,0:T(8,128)(2,1)S(1)}, s32[]{:S(2)}) async-start(bf16[4,2,128,256]{3,2,1,0:T(8,128)(2,1)} %own_ref.3), calls=%async_computation.2 | async-start | bytes 524288 | tf_op jit(solution)/shard_map/slice | solution.py:277
  3.2 18.3 %collective-permute-start.1 = (bf16[2,4,128,256]{3,2,1,0:T(8,128)(2,1)S(1)}, bf16[2,4,128,256]{3,2,1,0:T(8,128)(2,1)S(1)}, u32[]{:S(2)}, u32[]{:S(2)}) collective-permute-start(bf16[2,4,128,256]{3,2,1,0:T(8,128)(2,1)S(1)} %pad_maximum_fusion.4), channel_id=1, source_target_pairs={{1,0},{2,1},{3,2},{4,3},{5,4},{6,5},{7,6},{8,7},{9,8},{10,9},{11,1... | collective-permute-start | bytes 1572872 | tf_op jit(solution)/shard_map/ppermute | solution.py:265
  10.4 21.1 %collective-permute-start = (bf16[2,4,128,256]{3,2,1,0:T(8,128)(2,1)S(1)}, bf16[2,4,128,256]{3,2,1,0:T(8,128)(2,1)S(1)}, u32[]{:S(2)}, u32[]{:S(2)}) collective-permute-start(bf16[2,4,128,256]{3,2,1,0:T(8,128)(2,1)S(1)} %pad_maximum_fusion.3), channel_id=1, source_target_pairs={{0,1},{1,2},{2,3},{3,4},{4,5},{5,6},{6,7},{7,8},{8,9},{9,10},{10,1... | collective-permute-start | bytes 1572872 | tf_op jit(solution)/shard_map/ppermute | solution.py:265
  31.5 10.5 %collective-permute-start.2 = (bf16[2,4,128,256]{3,2,1,0:T(8,128)(2,1)S(1)}, bf16[2,4,128,256]{3,2,1,0:T(8,128)(2,1)S(1)}, u32[]{:S(2)}, u32[]{:S(2)}) collective-permute-start(bf16[2,4,128,256]{3,2,1,0:T(8,128)(2,1)S(1)} %pad_maximum_fusion.5), channel_id=1, source_target_pairs={{0,32},{32,64},{64,96},{1,33},{33,65},{65,97},{2,34},{34,66},{66,9... | collective-permute-start | bytes 1572872 | tf_op jit(solution)/shard_map/ppermute | solution.py:265
  34.3 14.2 %collective-permute-start.3 = (bf16[2,4,128,256]{3,2,1,0:T(8,128)(2,1)}, bf16[2,4,128,256]{3,2,1,0:T(8,128)(2,1)S(1)}, u32[]{:S(2)}, u32[]{:S(2)}) collective-permute-start(bf16[2,4,128,256]{3,2,1,0:T(8,128)(2,1)} %pad_maximum_fusion.6), channel_id=1, source_target_pairs={{32,0},{64,32},{96,64},{33,1},{65,33},{97,65},{34,2},{66,34},{98,6... | collective-permute-start | bytes 1572872 | tf_op jit(solution)/shard_map/ppermute | solution.py:265
  42.0 2.0 copy-start.3
  44.0 4.5 %copy-start = (bf16[4,2,128,256]{3,2,1,0:T(8,128)(2,1)S(1)}, bf16[4,2,128,256]{3,2,1,0:T(8,128)(2,1)}, u32[]{:S(2)}) copy-start(bf16[4,2,128,256]{3,2,1,0:T(8,128)(2,1)} %own_ref.3) | copy-start | bytes 1572868
  44.0 4.5 %copy-start.2 = (bf16[3,3,3,256,256]{4,3,2,1,0:T(8,128)(2,1)S(1)}, bf16[3,3,3,256,256]{4,3,2,1,0:T(8,128)(2,1)}, u32[]{:S(2)}) copy-start(bf16[3,3,3,256,256]{4,3,2,1,0:T(8,128)(2,1)} %param.6) | copy-start | bytes 10616836
  58.2 6.2 %collective-permute-start.9 = (bf16[16,2,27,8,128]{4,3,2,1,0:T(8,128)(2,1)S(1)}, bf16[16,2,27,8,128]{4,3,2,1,0:T(8,128)(2,1)S(1)}, u32[]{:S(2)}, u32[]{:S(2)}) collective-permute-start(bf16[16,2,27,8,128]{4,3,2,1,0:T(8,128)(2,1)S(1)} %get-tuple-element.17), channel_id=1, source_target_pairs={{0,32},{32,0},{1,33},{33,1},{2,34},{34,2},{3,35},{35,3},{4,36},{36... | collective-permute-start | bytes 5308424 | tf_op jit(solution)/shard_map/ppermute | solution.py:325
  63.9 3.9 %collective-permute-start.8 = (bf16[16,2,27,8,128]{4,3,2,1,0:T(8,128)(2,1)S(1)}, bf16[16,2,27,8,128]{4,3,2,1,0:T(8,128)(2,1)S(1)}, u32[]{:S(2)}, u32[]{:S(2)}) collective-permute-start(bf16[16,2,27,8,128]{4,3,2,1,0:T(8,128)(2,1)S(1)} %get-tuple-element.15), channel_id=1, source_target_pairs={{0,32},{32,0},{1,33},{33,1},{2,34},{34,2},{3,35},{35,3},{4,36},{36... | collective-permute-start | bytes 5308424 | tf_op jit(solution)/shard_map/ppermute | solution.py:324
  170.4 48.5 %collective-permute-start.10 = (bf16[64,27,8,128]{3,2,1,0:T(8,128)(2,1)S(1)}, bf16[64,27,8,128]{3,2,1,0:T(8,128)(2,1)S(1)}, u32[]{:S(2)}, u32[]{:S(2)}) collective-permute-start(bf16[64,27,8,128]{3,2,1,0:T(8,128)(2,1)S(1)} %all_to_all.11), channel_id=1, source_target_pairs={{0,32},{32,0},{1,33},{33,1},{2,34},{34,2},{3,35},{35,3},{4,36},{36... | collective-permute-start | bytes 10616840 | tf_op jit(solution)/shard_map/ppermute | solution.py:332
  170.5 16.7 %collective-permute-start.5 = (bf16[2,4,128,256]{3,2,1,0:T(8,128)(2,1)S(1)}, bf16[2,4,128,256]{3,2,1,0:T(8,128)(2,1)S(1)}, u32[]{:S(2)}, u32[]{:S(2)}) collective-permute-start(bf16[2,4,128,256]{3,2,1,0:T(8,128)(2,1)S(1)} %pad_maximum_fusion.8), channel_id=1, source_target_pairs={{1,0},{2,1},{3,2},{4,3},{5,4},{6,5},{7,6},{8,7},{9,8},{10,9},{11,1... | collective-permute-start | bytes 1572872 | tf_op jit(solution)/shard_map/ppermute | solution.py:265
  175.4 32.6 %copy-start.1 = (bf16[4,2,128,256]{3,2,1,0:T(8,128)(2,1)S(1)}, bf16[4,2,128,256]{3,2,1,0:T(8,128)(2,1)}, u32[]{:S(2)}) copy-start(bf16[4,2,128,256]{3,2,1,0:T(8,128)(2,1)} %latents_ref.3) | copy-start | bytes 1572868
  175.5 21.9 %collective-permute-start.4 = (bf16[2,4,128,256]{3,2,1,0:T(8,128)(2,1)S(1)}, bf16[2,4,128,256]{3,2,1,0:T(8,128)(2,1)S(1)}, u32[]{:S(2)}, u32[]{:S(2)}) collective-permute-start(bf16[2,4,128,256]{3,2,1,0:T(8,128)(2,1)S(1)} %pad_maximum_fusion.7), channel_id=1, source_target_pairs={{0,1},{1,2},{2,3},{3,4},{4,5},{5,6},{6,7},{7,8},{8,9},{9,10},{10,1... | collective-permute-start | bytes 1572872 | tf_op jit(solution)/shard_map/ppermute | solution.py:265
  197.5 10.5 %collective-permute-start.6 = (bf16[2,4,128,256]{3,2,1,0:T(8,128)(2,1)S(1)}, bf16[2,4,128,256]{3,2,1,0:T(8,128)(2,1)S(1)}, u32[]{:S(2)}, u32[]{:S(2)}) collective-permute-start(bf16[2,4,128,256]{3,2,1,0:T(8,128)(2,1)S(1)} %pad_maximum_fusion.9), channel_id=1, source_target_pairs={{0,32},{32,64},{64,96},{1,33},{33,65},{65,97},{2,34},{34,66},{66,9... | collective-permute-start | bytes 1572872 | tf_op jit(solution)/shard_map/ppermute | solution.py:265
  199.5 13.8 %collective-permute-start.7 = (bf16[2,4,128,256]{3,2,1,0:T(8,128)(2,1)S(1)}, bf16[2,4,128,256]{3,2,1,0:T(8,128)(2,1)S(1)}, u32[]{:S(2)}, u32[]{:S(2)}) collective-permute-start(bf16[2,4,128,256]{3,2,1,0:T(8,128)(2,1)S(1)} %pad_maximum_fusion.10), channel_id=1, source_target_pairs={{32,0},{64,32},{96,64},{33,1},{65,33},{97,65},{34,2},{66,34},{98,6... | collective-permute-start | bytes 1572872 | tf_op jit(solution)/shard_map/ppermute | solution.py:265
  203.3 10.0 %copy-start.4 = (bf16[3,3,3,256,256]{4,3,2,1,0:T(8,128)(2,1)S(1)}, bf16[3,3,3,256,256]{4,3,2,1,0:T(8,128)(2,1)}, u32[]{:S(2)}) copy-start(bf16[3,3,3,256,256]{4,3,2,1,0:T(8,128)(2,1)} %param.5) | copy-start | bytes 10616836
where the time goes:
time: 226 us; the launch traced here: 225 us
  blocking collectives  99.5 us (44%)
  waiting for transfers between devices  50.4 us (22%)
  Pallas kernels  39.4 us (17%)
  starting transfers between devices  27.8 us (12%)
  other arithmetic  3.9 us (2%)
  local copies, waits for them, and re-layouts  3.39 us (2%)
    all_to_all x1, blocking collectives, local(): own = lax.all_to_all(spread, CHIPS, 0, 0, tiled=False)  50 us
    all_to_all x1, blocking collectives, local(): parts = lax.all_to_all(mine, CHIPS, 0, 0, tiled=False)  49.5 us
    ppermute x8, waiting for transfers between devices, swap(): return lax.ppermute(value, axis, pairs)  47.5 us
    pallas_call x7, Pallas kernels, call(): pl.pallas_call(kernel, out_shape=outs, in_specs=specs, out_specs=[pl.Bloc...  32.8 us
    ppermute x8, starting transfers between devices, swap(): return lax.ppermute(value, axis, pairs)  27.1 us
    pallas_call x1, Pallas kernels, assemble(): pl.pallas_call(assemble_kernel, out_shape=(shape, shape), grid=(TAPS // S...  6.59 us
  transfers between devices with their start and end apart: 11, of which 7 were waited for; matrix products, arithmetic and copies ran while one was open for 1% of the time, Pallas kernels for 9%

commit v1 on v0

v1 whole, which is shorter than its diff:
```python
import jax
import jax.numpy as jnp
from jax import lax
from jax.experimental import pallas as pl
from jax.experimental.pallas import tpu as pltpu
from jax.sharding import Mesh, PartitionSpec as P


GROUP = ("zl", "co")
SPACE = ("zh", "y", "x")
CHIPS = ("zl", "zh", "y", "x")
C = 256
W = 128
FRAMES = 4
EXT = FRAMES + 2
TAPS = 27
SLOTS = 28
BF = jnp.bfloat16
F32 = jnp.float32
PASS_FLOPS = 2 * FRAMES * 2 * W * TAPS * C * C


def fill_ext(ext_ref, own_ref, above_ref, below_ref, time_ref, first):
    other = 0 if first == 2 else FRAMES
    for f in range(FRAMES):
        ext_ref[first + f, 0:W] = above_ref[f]
        for r in range(2):
            ext_ref[first + f, (r + 1) * W : (r + 2) * W] = own_ref[f, r]
        ext_ref[first + f, 3 * W : 4 * W] = below_ref[f]
    for f in range(2):
        for r in range(4):
            ext_ref[other + f, r * W : (r + 1) * W] = time_ref[f, r]


def shifted(value, by):
    height = value.shape[0]
    turned = pltpu.roll(value, by % height, 0)
    column = lax.broadcasted_iota(jnp.int32, value.shape, 0) % W
    edge = 0 if by > 0 else W - 1
    return jnp.where(column == edge, 0.0, turned)


def conv_frame(ext_ref, kernel_ref, t, transposed):
    parts = []
    for i in range(3):
        for j in range(3):
            frame = t + (2 - i if transposed else i)
            row = 2 - j if transposed else j
            parts.append(ext_ref[frame, row * W : (row + 2) * W])
    lhs = jnp.concatenate(parts, axis=1)
    sums = []
    for k in range(3):
        taps = [kernel_ref[(i * 3 + j) * 3 + k] for i in range(3) for j in range(3)]
        if transposed:
            rhs = jnp.concatenate(taps, axis=1)
            dims = (((1,), (1,)), ((), ()))
        else:
            rhs = jnp.concatenate(taps, axis=0)
            dims = (((1,), (0,)), ((), ()))
        sums.append(lax.dot_general(lhs, rhs, dims, preferred_element_type=F32))
    if transposed:
        return sums[1] + shifted(sums[0], -1) + shifted(sums[2], 1)
    return sums[1] + shifted(sums[0], 1) + shifted(sums[2], -1)


def gate_grad(values):
    s = jax.nn.sigmoid(values)
    return s * (1.0 + values * (1.0 - s))


def split_rows(value):
    return value.reshape(2, W, C)


def hidden_kernel(own_ref, above_ref, below_ref, time_ref, kernel_ref, hidden_ref, active_ref, ext_ref):
    fill_ext(ext_ref, own_ref, above_ref, below_ref, time_ref, 2)

    def body(t, carry):
        hidden = conv_frame(ext_ref, kernel_ref, t, False)
        hidden_ref[t] = hidden
        active_ref[t] = split_rows((hidden * jax.nn.sigmoid(hidden)).astype(BF))
        return carry

    lax.fori_loop(0, FRAMES, body, 0)


def hidden_grad_kernel(own_ref, above_ref, below_ref, time_ref, kernel_ref, hidden_ref, out_ref, ext_ref):
    fill_ext(ext_ref, own_ref, above_ref, below_ref, time_ref, 0)

    def body(t, carry):
        grad = conv_frame(ext_ref, kernel_ref, t, True)
        out_ref[t] = split_rows((grad * gate_grad(hidden_ref[t])).astype(BF))
        return carry

    lax.fori_loop(0, FRAMES, body, 0)


def decoded_kernel(own_ref, above_ref, below_ref, time_ref, kernel_ref, latents_ref, out_ref, ext_ref):
    fill_ext(ext_ref, own_ref, above_ref, below_ref, time_ref, 2)

    def body(t, carry):
        branch = split_rows(conv_frame(ext_ref, kernel_ref, t, False))
        out_ref[t] = (latents_ref[t].astype(F32) + branch).astype(BF)
        return carry

    lax.fori_loop(0, FRAMES, body, 0)


def latent_grad_kernel(
    own_ref, above_ref, below_ref, time_ref, kernel_ref, latents_ref, upstream_ref, out_ref, ext_ref
):
    fill_ext(ext_ref, own_ref, above_ref, below_ref, time_ref, 0)

    def body(t, carry):
        inner = split_rows(conv_frame(ext_ref, kernel_ref, t, True))
        gate = gate_grad(latents_ref[t].astype(F32))
        out_ref[t] = (upstream_ref[t].astype(F32) + inner * gate).astype(BF)
        return carry

    lax.fori_loop(0, FRAMES, body, 0)


def keep_first(core, value):
    return jnp.where(core == 0, value, pltpu.roll(value, C // 2, 0))


def shift_copies(value):
    wide = value.astype(F32)
    return [shifted(wide, -1).astype(BF), value, shifted(wide, 1).astype(BF)]


def put_tap(keep_ref, send_ref, tap, product):
    for ref, low in ((keep_ref, 0), (send_ref, C // 2)):
        half = product[low : low + C // 2].astype(ref.dtype)
        for b in range(2):
            ref[:, b, tap] = half[:, b * 128 : (b + 1) * 128].reshape(16, 8, 128)


def clear_slot(keep_ref, send_ref):
    for ref in (keep_ref, send_ref):
        ref[:, :, TAPS] = jnp.zeros((16, 2, 8, 128), ref.dtype)


def second_grad_kernel(
    core_ref, active_ref, own_ref, above_ref, below_ref, time_ref, keep_ref, send_ref, ext_ref, across_ref, turn_ref
):
    core = core_ref[0]
    fill_ext(ext_ref, own_ref, above_ref, below_ref, time_ref, 0)
    for f in range(EXT):
        for k, copy in enumerate(shift_copies(ext_ref[f])):
            across_ref[k, f] = copy
    for t in range(FRAMES):
        flat = active_ref[t].reshape(2 * W, C).astype(F32)
        turn_ref[:, t * 2 * W : (t + 1) * 2 * W] = keep_first(core, flat.T).astype(BF)

    def body(i, carry):
        for j in range(3):
            for k in range(3):
                rhs = jnp.concatenate(
                    [across_ref[k, t + 2 - i, (2 - j) * W : (4 - j) * W] for t in range(FRAMES)], axis=0
                )
                product = jnp.dot(turn_ref[...], rhs, preferred_element_type=F32)
                put_tap(keep_ref, send_ref, i * 9 + j * 3 + k, product)
        return carry

    lax.fori_loop(0, 3, body, 0)
    clear_slot(keep_ref, send_ref)


def first_grad_kernel(
    core_ref, grad_ref, own_ref, above_ref, below_ref, time_ref, keep_ref, send_ref, ext_ref, across_ref, turn_ref
):
    core = core_ref[0]
    fill_ext(ext_ref, own_ref, above_ref, below_ref, time_ref, 2)
    for t in range(FRAMES):
        for k, copy in enumerate(shift_copies(grad_ref[t].reshape(2 * W, C))):
            across_ref[k, t * 2 * W : (t + 1) * 2 * W] = copy
    for f in range(EXT):
        turn_ref[f] = keep_first(core, ext_ref[f].astype(F32).T).astype(BF)

    def body(i, carry):
        for j in range(3):
            lhs = jnp.concatenate(
                [turn_ref[t + i, :, j * W : (j + 2) * W] for t in range(FRAMES)], axis=1
            )
            for k in range(3):
                product = jnp.dot(lhs, across_ref[k], preferred_element_type=F32)
                put_tap(keep_ref, send_ref, i * 9 + j * 3 + k, product)
        return carry

    lax.fori_loop(0, 3, body, 0)
    clear_slot(keep_ref, send_ref)


def cost(flops, moved):
    return pl.CostEstimate(flops=flops, bytes_accessed=moved, transcendentals=0)


def whole(kernel, outs, scratch, limit, smem=0, flops=PASS_FLOPS):
    def call(*args):
        moved = sum(a.size * a.dtype.itemsize for a in args)
        moved += sum(o.size * o.dtype.itemsize for o in outs)
        specs = [
            pl.BlockSpec(memory_space=pltpu.SMEM if n < smem else pltpu.VMEM) for n in range(len(args))
        ]
        return pl.pallas_call(
            kernel,
            out_shape=outs,
            in_specs=specs,
            out_specs=[pl.BlockSpec(memory_space=pltpu.VMEM) for _ in outs],
            scratch_shapes=scratch,
            compiler_params=pltpu.CompilerParams(vmem_limit_bytes=limit << 20),
            cost_estimate=cost(flops, moved),
        )(*args)

    return call


def tie(value, *after):
    return lax.optimization_barrier((value, *after))[0]


STEP = 3


def assemble_kernel(core_ref, own_ref, far_ref, out_ref):
    core = core_ref[0]
    mine = pl.multiple_of(core * 128, 128)
    theirs = pl.multiple_of((1 - core) * 128, 128)
    for p in range(STEP):
        for b in range(2):
            lanes = slice(b * 128, (b + 1) * 128)
            out_ref[p, pl.ds(mine, 128), lanes] = own_ref[:, b, p].astype(F32).reshape(128, 128)
            out_ref[p, pl.ds(theirs, 128), lanes] = far_ref[:, b, p].astype(F32).reshape(128, 128)


def assemble(core, own, far):
    own, far = (v.reshape(HALF) for v in (own, far))
    part = pl.BlockSpec((16, 2, STEP, 8, 128), lambda p: (0, 0, p, 0, 0))
    return pl.pallas_call(
        assemble_kernel,
        out_shape=jax.ShapeDtypeStruct((TAPS, C, C), F32),
        grid=(TAPS // STEP,),
        in_specs=[pl.BlockSpec(memory_space=pltpu.SMEM), part, part],
        out_specs=pl.BlockSpec((STEP, C, C), lambda p: (p, 0, 0)),
        compiler_params=pltpu.CompilerParams(vmem_limit_bytes=16 << 20),
        cost_estimate=cost(1 << 24, 11 << 20),
        name="assemble",
    )(core, own, far)


def total_kernel(parts_ref, out_ref):
    count = parts_ref.shape[0]

    def body(p, carry):
        total = parts_ref[0, p].astype(F32)
        for n in range(1, count):
            total = total + parts_ref[n, p].astype(F32)
        rounded = total.astype(BF)
        for n in range(count):
            out_ref[n, p] = rounded
        return carry

    lax.fori_loop(0, parts_ref.shape[1], body, 0)


def add_kernel(keep_ref, got_ref, out_ref):
    for b in range(2):

        def body(p, carry):
            both = keep_ref[:, b, p] + got_ref[:, b, p].astype(F32)
            out_ref[:, b, p] = both.astype(BF)
            return carry

        lax.fori_loop(0, SLOTS, body, 0)


def swap(value, axis, steps):
    count = lax.axis_size(axis)
    pairs = [(n, n + steps) for n in range(count) if 0 <= n + steps < count]
    return lax.ppermute(value, axis, pairs)


def edge_rows(own):
    return (swap(own[:, 1], SPACE, 1), swap(own[:, 0], SPACE, -1))


def two_frames(own, rows, start):
    frames = slice(start, start + 2)
    above, below = rows
    return jnp.concatenate([above[frames][:, None], own[frames], below[frames][:, None]], axis=1)


HALF = (16, 2, SLOTS, 8, 128)
PAIR = (jax.ShapeDtypeStruct(HALF, F32), jax.ShapeDtypeStruct(HALF, BF))
ACROSS = [(0, 1), (1, 0)]


def add_pair(keep, got):
    shape = jax.ShapeDtypeStruct(HALF, BF)
    (mine,) = whole(add_kernel, (shape,), [], 16, flops=1 << 28)(keep, got)
    chips = lax.axis_size(CHIPS)
    return mine.reshape(chips, 64 // chips * 14, 8, 128)


def total(parts):
    (spread,) = whole(total_kernel, (jax.ShapeDtypeStruct(parts.shape, BF),), [], 16, flops=1 << 28)(parts)
    return spread


def exchange(value):
    return lax.all_to_all(value, CHIPS, 0, 0, tiled=False)


def step(latents, first_kernel, second_kernel, upstream):
    core = lax.axis_index("co").astype(jnp.int32).reshape(1)
    k1 = first_kernel.reshape(TAPS, C, C)
    k2 = second_kernel.reshape(TAPS, C, C)
    wide = latents.astype(F32)
    smooth = (wide * jax.nn.sigmoid(wide)).astype(BF)
    block = jax.ShapeDtypeStruct((FRAMES, 2, W, C), BF)
    ext = pltpu.VMEM((EXT, 4 * W, C), BF)

    rows = edge_rows(smooth)
    up_rows = edge_rows(upstream)
    smooth_time = swap(two_frames(smooth, rows, 2), GROUP, 1)
    up_time = swap(two_frames(upstream, up_rows, 0), GROUP, -1)
    hidden, active = whole(
        hidden_kernel, (jax.ShapeDtypeStruct((FRAMES, 2 * W, C), F32), block), [ext], 24
    )(smooth, *rows, smooth_time, k1)
    keep2, send2 = whole(
        second_grad_kernel, PAIR, [ext, pltpu.VMEM((3, EXT, 4 * W, C), BF), pltpu.VMEM((C, FRAMES * 2 * W), BF)], 40, 1
    )(core, active, upstream, *up_rows, up_time)
    (hidden_grad,) = whole(hidden_grad_kernel, (block,), [ext], 24)(upstream, *up_rows, up_time, k2, hidden)
    got2 = lax.ppermute(send2, "co", ACROSS)
    mine2 = add_pair(keep2, tie(got2, hidden_grad))
    parts2 = exchange(mine2)
    keep1, send1 = whole(
        first_grad_kernel, PAIR, [ext, pltpu.VMEM((3, FRAMES * 2 * W, C), BF), pltpu.VMEM((EXT, C, 4 * W), BF)], 40, 1
    )(core, tie(hidden_grad, mine2), smooth, *rows, smooth_time)
    got1 = lax.ppermute(send1, "co", ACROSS)

    active_rows = edge_rows(active)
    grad_rows = edge_rows(hidden_grad)
    active_time = swap(two_frames(active, active_rows, 2), GROUP, 1)
    grad_time = swap(two_frames(hidden_grad, grad_rows, 0), GROUP, -1)
    parts1 = exchange(add_pair(keep1, tie(got1, *grad_rows, active_time)))
    (decoded,) = whole(decoded_kernel, (block,), [ext], 24)(
        active, *active_rows, active_time, k2, latents
    )
    (latent_grad,) = whole(latent_grad_kernel, (block,), [ext], 24)(
        hidden_grad, *grad_rows, grad_time, k1, latents, upstream
    )
    own2 = exchange(total(tie(parts2, decoded)))
    own1 = exchange(total(tie(parts1, latent_grad)))
    far2 = lax.ppermute(own2, "co", ACROSS)
    far1 = lax.ppermute(own1, "co", ACROSS)
    second_grad = assemble(core, own2, far2)
    first_grad = assemble(core, own1, far1)
    shape = first_kernel.shape
    return (decoded, latent_grad, first_grad.reshape(shape), second_grad.reshape(shape))


def solution(mesh, sizes=(2, 2, 2, 4, 4)):
    fine = Mesh(mesh.devices.reshape(sizes), ("zl", "co", "zh", "y", "x"))
    placed = (P(GROUP, SPACE, None, None), P(), P(), P(GROUP, SPACE, None, None))
    return jax.shard_map(
        step,
        mesh=fine,
        in_specs=placed,
        out_specs=(P(GROUP, SPACE, None, None), P(GROUP, SPACE, None, None), P(), P()),
        check_vma=False,
    )
```

time: 226 us -> 269 us (1.19)
  the two profiles are of different devices: /device:TPU:96 before, /device:TPU:1 now
where the time goes in v1:
time: 269 us; the launch traced here: 268 us
  waiting for transfers between devices  95.4 us (35%)
  starting transfers between devices  88.5 us (33%)
  Pallas kernels  60.3 us (22%)
  local copies, waits for them, and re-layouts  19.3 us (7%)
  other arithmetic  3.21 us (1%)
    ppermute x12, waiting for transfers between devices, swap(): return lax.ppermute(value, axis, pairs)  56.3 us
    all_to_all x4, starting transfers between devices, exchange(): return lax.all_to_all(value, CHIPS, 0, 0, tiled=False)  49.9 us
    pallas_call x10, Pallas kernels, call(): pl.pallas_call(kernel, out_shape=outs, in_specs=specs, out_specs=[pl.Bloc...  46.1 us
    all_to_all x4, waiting for transfers between devices, exchange(): return lax.all_to_all(value, CHIPS, 0, 0, tiled=False)  39 us
    ppermute x12, starting transfers between devices, swap(): return lax.ppermute(value, axis, pairs)  37.8 us
    unnamed x38, local copies, waits for them, and re-layouts  17.1 us
    pallas_call x2, Pallas kernels, assemble(): pl.pallas_call(assemble_kernel, out_shape=jax.ShapeDtypeStruct((TAPS, C,...  14.1 us
  transfers between devices with their start and end apart: 20, of which 7 were waited for; matrix products, arithmetic and copies ran while one was open for 1% of the time, Pallas kernels for 14%

profile of v1, /device:TPU:1, one launch (start us, length us, event | category | flops | bytes accessed | tf_op | source)
XLA Modules:
  0.0 267.7 jit_solution(3502302118756546962)
XLA Ops:
  3.4 4.7 %collective-permute-start = (bf16[4,128,256]{2,1,0:T(8,128)(2,1)S(1)}, bf16[4,128,256]{2,1,0:T(8,128)(2,1)S(1)}, u32[]{:S(2)}, u32[]{:S(2)}) collective-permute-start(bf16[4,128,256]{2,1,0:T(8,128)(2,1)S(1)} %get-tuple-element.33), channel_id=1, source_target_pairs={{0,1},{1,2},{2,3},{3,4},{4,5},{5,6},{6,7},{7,8},{8,9},{9,10},{10,1... | collective-permute-start | bytes 786440 | tf_op jit(solution)/shard_map/ppermute | solution.py:281
  9.5 4.0 %collective-permute-start.6 = (bf16[4,128,256]{2,1,0:T(8,128)(2,1)S(1)}, bf16[4,128,256]{2,1,0:T(8,128)(2,1)S(1)}, u32[]{:S(2)}, u32[]{:S(2)}) collective-permute-start(bf16[4,128,256]{2,1,0:T(8,128)(2,1)S(1)} %get-tuple-element.29), channel_id=1, source_target_pairs={{0,1},{1,2},{2,3},{3,4},{4,5},{5,6},{6,7},{7,8},{8,9},{9,10},{10,1... | collective-permute-start | bytes 786440 | tf_op jit(solution)/shard_map/ppermute | solution.py:281
  14.4 5.5 %collective-permute-start.2 = (bf16[2,4,128,256]{3,2,1,0:T(8,128)(2,1)}, bf16[2,4,128,256]{3,2,1,0:T(8,128)(2,1)S(1)}, u32[]{:S(2)}, u32[]{:S(2)}) collective-permute-start(bf16[2,4,128,256]{3,2,1,0:T(8,128)(2,1)} %pad_maximum_fusion), channel_id=1, source_target_pairs={{0,32},{32,64},{64,96},{1,33},{33,65},{65,97},{2,34},{34,66},{66,9... | collective-permute-start | bytes 1572872 | tf_op jit(solution)/shard_map/ppermute | solution.py:281
  23.1 7.5 %collective-permute-done.2.time_ref = bf16[2,4,128,256]{3,2,1,0:T(8,128)(2,1)S(1)} collective-permute-done((bf16[2,4,128,256]{3,2,1,0:T(8,128)(2,1)}, bf16[2,4,128,256]{3,2,1,0:T(8,128)(2,1)S(1)}, u32[]{:S(2)}, u32[]{:S(2)}) %collective-permute-start.2) | collective-permute-done | bytes 524320 | tf_op jit(solution)/shard_map/ppermute | solution.py:281
  34.4 4.5 %shard_map.75 = (f32[4,256,256]{2,1,0:T(8,128)S(1)}, bf16[4,2,128,256]{3,2,1,0:T(8,128)(2,1)S(1)}) custom-call(bf16[4,2,128,256]{3,2,1,0:T(8,128)(2,1)S(1)} %copy.11.own_ref, bf16[4,128,256]{2,1,0:T(8,128)(2,1)S(1)} %collective-permute-done.above_ref, bf16[4,128,256]{2,1,0:T(8,128)(2,1)S(1)} %collective-permute-done.1.below_ref, ...), custom_call_target="tpu_custom_call" | custom-call | flops 3623878656 | bytes 6684672 | tf_op jit(solution)/shard_map/pallas_call | solution.py:206
  39.0 6.8 %shard_map.79 = (f32[16,2,28,8,128]{4,3,2,1,0:T(8,128)S(1)}, bf16[16,2,28,8,128]{4,3,2,1,0:T(8,128)(2,1)S(1)}) custom-call(s32[1]{0:T(128)} %bitcast.19.core_ref, bf16[4,2,128,256]{3,2,1,0:T(8,128)(2,1)S(1)} %get-tuple-element.15.own_ref.active_ref, bf16[4,2,128,256]{3,2,1,0:T(8,128)(2,1)S(1)} %copy-done.3, ...), custom_call_target="tpu_custom_call" | custom-call | flops 3623878656 | bytes 7602180 | tf_op jit(solution)/shard_map/pallas_call | solution.py:206
  45.9 5.7 %shard_map.77.own_ref.grad_ref = bf16[4,2,128,256]{3,2,1,0:T(8,128)(2,1)S(1)} custom-call(bf16[4,2,128,256]{3,2,1,0:T(8,128)(2,1)S(1)} %copy-done.3, bf16[4,128,256]{2,1,0:T(8,128)(2,1)S(1)} %collective-permute-done.6.above_ref, bf16[4,128,256]{2,1,0:T(8,128)(2,1)S(1)} %collective-permute-done.7.below_ref, ...), custom_call_target="tpu_custom_call" | custom-call | flops 3623878656 | bytes 6684672 | tf_op jit(solution)/shard_map/pallas_call | solution.py:206
  53.9 6.2 %shard_map.81 = (f32[16,2,28,8,128]{4,3,2,1,0:T(8,128)S(1)}, bf16[16,2,28,8,128]{4,3,2,1,0:T(8,128)(2,1)}) custom-call(s32[1]{0:T(128)} %bitcast.19.core_ref, bf16[4,2,128,256]{3,2,1,0:T(8,128)(2,1)S(1)} %shard_map.77.own_ref.grad_ref, bf16[4,2,128,256]{3,2,1,0:T(8,128)(2,1)S(1)} %copy.11.own_ref, bf16[4,128,256]{2,1,0:T(8,128)(2,1)S(1)} %collective-permute-done.above_ref, ...), custom_call_target="tpu_custom_call" | custom-call | flops 3623878656 | bytes 7602180 | tf_op jit(solution)/shard_map/pallas_call | solution.py:206
  62.4 16.5 %all-to-all-start.2 = ((bf16[64,14,8,128]{3,2,1,0:T(8,128)(2,1)}), bf16[64,14,8,128]{3,2,1,0:T(8,128)(2,1)S(1)}, u32[]{:S(2)}, u32[]{:S(2)}) async-start(bf16[64,14,8,128]{3,2,1,0:T(8,128)(2,1)} %bitcast.20), calls=%async_computation.2 | async-start | bytes 3670016 | tf_op jit(solution)/shard_map/all_to_all | solution.py:312
  80.5 4.0 %collective-permute-start.3 = (bf16[4,128,256]{2,1,0:T(8,128)(2,1)S(1)}, bf16[4,128,256]{2,1,0:T(8,128)(2,1)S(1)}, u32[]{:S(2)}, u32[]{:S(2)}) collective-permute-start(bf16[4,128,256]{2,1,0:T(8,128)(2,1)S(1)} %get-tuple-element.31), channel_id=1, source_target_pairs={{0,1},{1,2},{2,3},{3,4},{4,5},{5,6},{6,7},{7,8},{8,9},{9,10},{10,1... | collective-permute-start | bytes 786440 | tf_op jit(solution)/shard_map/ppermute | solution.py:281
  84.6 20.9 %collective-permute-done.4.below_ref = bf16[4,128,256]{2,1,0:T(8,128)(2,1)S(1)} collective-permute-done((bf16[4,128,256]{2,1,0:T(8,128)(2,1)S(1)}, bf16[4,128,256]{2,1,0:T(8,128)(2,1)S(1)}, u32[]{:S(2)}, u32[]{:S(2)}) %collective-permute-start.4) | collective-permute-done | bytes 262176 | tf_op jit(solution)/shard_map/ppermute | solution.py:281
  107.0 4.3 %collective-permute-start.5 = (bf16[2,4,128,256]{3,2,1,0:T(8,128)(2,1)S(1)}, bf16[2,4,128,256]{3,2,1,0:T(8,128)(2,1)S(1)}, u32[]{:S(2)}, u32[]{:S(2)}) collective-permute-start(bf16[2,4,128,256]{3,2,1,0:T(8,128)(2,1)S(1)} %pad_maximum_fusion.1), channel_id=1, source_target_pairs={{0,32},{32,64},{64,96},{1,33},{33,65},{65,97},{2,34},{34,66},{66,9... | collective-permute-start | bytes 1572872 | tf_op jit(solution)/shard_map/ppermute | solution.py:281
  112.6 4.7 %collective-permute-start.9 = (bf16[4,128,256]{2,1,0:T(8,128)(2,1)S(1)}, bf16[4,128,256]{2,1,0:T(8,128)(2,1)}, u32[]{:S(2)}, u32[]{:S(2)}) collective-permute-start(bf16[4,128,256]{2,1,0:T(8,128)(2,1)S(1)} %get-tuple-element.27), channel_id=1, source_target_pairs={{0,1},{1,2},{2,3},{3,4},{4,5},{5,6},{6,7},{7,8},{8,9},{9,10},{10,1... | collective-permute-start | bytes 786440 | tf_op jit(solution)/shard_map/ppermute | solution.py:281
  126.3 18.7 %all-to-all-start = ((bf16[64,14,8,128]{3,2,1,0:T(8,128)(2,1)}), bf16[64,14,8,128]{3,2,1,0:T(8,128)(2,1)}, u32[]{:S(2)}, u32[]{:S(2)}) async-start(bf16[64,14,8,128]{3,2,1,0:T(8,128)(2,1)} %bitcast.21), calls=%async_computation | async-start | bytes 3670016 | tf_op jit(solution)/shard_map/all_to_all | solution.py:312
  150.9 5.3 %shard_map.76 = bf16[4,2,128,256]{3,2,1,0:T(8,128)(2,1)} custom-call(bf16[4,2,128,256]{3,2,1,0:T(8,128)(2,1)S(1)} %get-tuple-element.15.own_ref.active_ref, bf16[4,128,256]{2,1,0:T(8,128)(2,1)S(1)} %copy-done.9, bf16[4,128,256]{2,1,0:T(8,128)(2,1)S(1)} %copy-done.7, bf16[2,4,128,256]{3,2,1,0:T(8,128)(2,1)S(1)} %copy-done.18, ...), custom_call_target="tpu_custom_call" | custom-call | flops 3623878656 | bytes 6160384 | tf_op jit(solution)/shard_map/pallas_call | solution.py:206
  158.6 12.3 %all-to-all-done.parts_ref = bf16[64,14,8,128]{3,2,1,0:T(8,128)(2,1)} async-done(((bf16[64,14,8,128]{3,2,1,0:T(8,128)(2,1)}), bf16[64,14,8,128]{3,2,1,0:T(8,128)(2,1)}, u32[]{:S(2)}, u32[]{:S(2)}) %all-to-all-start) | async-done | bytes 1835040 | tf_op jit(solution)/shard_map/all_to_all | solution.py:312
  170.9 6.1 %all-to-all-start.3 = ((bf16[64,14,8,128]{3,2,1,0:T(8,128)(2,1)}), bf16[64,14,8,128]{3,2,1,0:T(8,128)(2,1)S(1)}, u32[]{:S(2)}, u32[]{:S(2)}) async-start(bf16[64,14,8,128]{3,2,1,0:T(8,128)(2,1)} %copy-done), calls=%async_computation.3 | async-start | bytes 3670016 | tf_op jit(solution)/shard_map/all_to_all | solution.py:312
  182.0 23.4 %collective-permute-done.11.time_ref = bf16[2,4,128,256]{3,2,1,0:T(8,128)(2,1)S(1)} collective-permute-done((bf16[2,4,128,256]{3,2,1,0:T(8,128)(2,1)S(1)}, bf16[2,4,128,256]{3,2,1,0:T(8,128)(2,1)S(1)}, u32[]{:S(2)}, u32[]{:S(2)}) %collective-permute-start.11) | collective-permute-done | bytes 524320 | tf_op jit(solution)/shard_map/ppermute | solution.py:281
  207.4 6.5 %shard_map.78 = bf16[4,2,128,256]{3,2,1,0:T(8,128)(2,1)} custom-call(bf16[4,2,128,256]{3,2,1,0:T(8,128)(2,1)S(1)} %shard_map.77.own_ref.grad_ref, bf16[4,128,256]{2,1,0:T(8,128)(2,1)} %collective-permute-done.9.above_ref, bf16[4,128,256]{2,1,0:T(8,128)(2,1)} %collective-permute-done.10.below_ref, ...), custom_call_target="tpu_custom_call" | custom-call | flops 3623878656 | bytes 6684672 | tf_op jit(solution)/shard_map/pallas_call | solution.py:206
  214.0 3.9 %shard_map.83 = bf16[64,14,8,128]{3,2,1,0:T(8,128)(2,1)} custom-call(bf16[64,14,8,128]{3,2,1,0:T(8,128)(2,1)} %all-to-all-done.parts_ref), custom_call_target="tpu_custom_call" | custom-call | flops 268435456 | bytes 3670016 | tf_op jit(solution)/shard_map/pallas_call | solution.py:206
  217.9 8.7 %all-to-all-start.1 = ((bf16[64,14,8,128]{3,2,1,0:T(8,128)(2,1)}), bf16[64,14,8,128]{3,2,1,0:T(8,128)(2,1)}, u32[]{:S(2)}, u32[]{:S(2)}) async-start(bf16[64,14,8,128]{3,2,1,0:T(8,128)(2,1)} %shard_map.83), calls=%async_computation.1 | async-start | bytes 3670016 | tf_op jit(solution)/shard_map/all_to_all | solution.py:312
  226.7 26.7 %all-to-all-done.1 = bf16[64,14,8,128]{3,2,1,0:T(8,128)(2,1)} async-done(((bf16[64,14,8,128]{3,2,1,0:T(8,128)(2,1)}), bf16[64,14,8,128]{3,2,1,0:T(8,128)(2,1)}, u32[]{:S(2)}, u32[]{:S(2)}) %all-to-all-start.1) | async-done | bytes 1835040 | tf_op jit(solution)/shard_map/all_to_all | solution.py:312
  253.6 7.1 %assemble.3 = f32[27,256,256]{2,1,0:T(8,128)} custom-call(s32[1]{0:T(128)} %bitcast.19.core_ref, bf16[16,2,28,8,128]{4,3,2,1,0:T(8,128)(2,1)S(1)} %bitcast.53, bf16[16,2,28,8,128]{4,3,2,1,0:T(8,128)(2,1)} %bitcast.26.far_ref), custom_call_target="tpu_custom_call" | custom-call | flops 16777216 | bytes 11534336 | tf_op jit(solution)/shard_map/assemble/pallas_call | solution.py:240
  260.7 7.0 %assemble.2 = f32[27,256,256]{2,1,0:T(8,128)} custom-call(s32[1]{0:T(128)} %bitcast.19.core_ref, bf16[16,2,28,8,128]{4,3,2,1,0:T(8,128)(2,1)} %bitcast.22.own_ref, bf16[16,2,28,8,128]{4,3,2,1,0:T(8,128)(2,1)S(1)} %bitcast.54), custom_call_target="tpu_custom_call" | custom-call | flops 16777216 | bytes 11534336 | tf_op jit(solution)/shard_map/assemble/pallas_call | solution.py:240
  (88 shorter events, 45.6 us)
Async XLA Ops:
  0.6 7.5 %copy-start.3 = (bf16[4,2,128,256]{3,2,1,0:T(8,128)(2,1)S(1)}, bf16[4,2,128,256]{3,2,1,0:T(8,128)(2,1)}, u32[]{:S(2)}) copy-start(bf16[4,2,128,256]{3,2,1,0:T(8,128)(2,1)} %own_ref.3) | copy-start | bytes 1572868
  2.1 11.4 %collective-permute-start.1 = (bf16[4,128,256]{2,1,0:T(8,128)(2,1)S(1)}, bf16[4,128,256]{2,1,0:T(8,128)(2,1)S(1)}, u32[]{:S(2)}, u32[]{:S(2)}) collective-permute-start(bf16[4,128,256]{2,1,0:T(8,128)(2,1)S(1)} %get-tuple-element.32), channel_id=1, source_target_pairs={{1,0},{2,1},{3,2},{4,3},{5,4},{6,5},{7,6},{8,7},{9,8},{10,9},{11,1... | collective-permute-start | bytes 786440 | tf_op jit(solution)/shard_map/ppermute | solution.py:281
  3.4 16.5 %slice-start = ((bf16[4,2,128,256]{3,2,1,0:T(8,128)(2,1)}), bf16[2,2,128,256]{3,2,1,0:T(8,128)(2,1)S(1)}, s32[]{:S(2)}) async-start(bf16[4,2,128,256]{3,2,1,0:T(8,128)(2,1)} %own_ref.3), calls=%async_computation.4 | async-start | bytes 524288 | tf_op jit(solution)/shard_map/slice | solution.py:291
  3.4 10.1 %collective-permute-start = (bf16[4,128,256]{2,1,0:T(8,128)(2,1)S(1)}, bf16[4,128,256]{2,1,0:T(8,128)(2,1)S(1)}, u32[]{:S(2)}, u32[]{:S(2)}) collective-permute-start(bf16[4,128,256]{2,1,0:T(8,128)(2,1)S(1)} %get-tuple-element.33), channel_id=1, source_target_pairs={{0,1},{1,2},{2,3},{3,4},{4,5},{5,6},{6,7},{7,8},{8,9},{9,10},{10,1... | collective-permute-start | bytes 786440 | tf_op jit(solution)/shard_map/ppermute | solution.py:281
  8.2 11.7 %collective-permute-start.7 = (bf16[4,128,256]{2,1,0:T(8,128)(2,1)S(1)}, bf16[4,128,256]{2,1,0:T(8,128)(2,1)S(1)}, u32[]{:S(2)}, u32[]{:S(2)}) collective-permute-start(bf16[4,128,256]{2,1,0:T(8,128)(2,1)S(1)} %get-tuple-element.28), channel_id=1, source_target_pairs={{1,0},{2,1},{3,2},{4,3},{5,4},{6,5},{7,6},{8,7},{9,8},{10,9},{11,1... | collective-permute-start | bytes 786440 | tf_op jit(solution)/shard_map/ppermute | solution.py:281
  9.5 10.4 %collective-permute-start.6 = (bf16[4,128,256]{2,1,0:T(8,128)(2,1)S(1)}, bf16[4,128,256]{2,1,0:T(8,128)(2,1)S(1)}, u32[]{:S(2)}, u32[]{:S(2)}) collective-permute-start(bf16[4,128,256]{2,1,0:T(8,128)(2,1)S(1)} %get-tuple-element.29), channel_id=1, source_target_pairs={{0,1},{1,2},{2,3},{3,4},{4,5},{5,6},{6,7},{7,8},{8,9},{9,10},{10,1... | collective-permute-start | bytes 786440 | tf_op jit(solution)/shard_map/ppermute | solution.py:281
  14.4 16.2 %collective-permute-start.2 = (bf16[2,4,128,256]{3,2,1,0:T(8,128)(2,1)}, bf16[2,4,128,256]{3,2,1,0:T(8,128)(2,1)S(1)}, u32[]{:S(2)}, u32[]{:S(2)}) collective-permute-start(bf16[2,4,128,256]{3,2,1,0:T(8,128)(2,1)} %pad_maximum_fusion), channel_id=1, source_target_pairs={{0,32},{32,64},{64,96},{1,33},{33,65},{65,97},{2,34},{34,66},{66,9... | collective-permute-start | bytes 1572872 | tf_op jit(solution)/shard_map/ppermute | solution.py:281
  20.8 18.2 %collective-permute-start.8 = (bf16[2,4,128,256]{3,2,1,0:T(8,128)(2,1)}, bf16[2,4,128,256]{3,2,1,0:T(8,128)(2,1)}, u32[]{:S(2)}, u32[]{:S(2)}) collective-permute-start(bf16[2,4,128,256]{3,2,1,0:T(8,128)(2,1)} %pad_maximum_fusion.2), channel_id=1, source_target_pairs={{32,0},{64,32},{96,64},{33,1},{65,33},{97,65},{34,2},{66,34},{98,6... | collective-permute-start | bytes 1572872 | tf_op jit(solution)/shard_map/ppermute | solution.py:281
  45.8 5.8 %collective-permute-start.12 = (bf16[16,2,28,8,128]{4,3,2,1,0:T(8,128)(2,1)S(1)}, bf16[16,2,28,8,128]{4,3,2,1,0:T(8,128)(2,1)S(1)}, u32[]{:S(2)}, u32[]{:S(2)}) collective-permute-start(bf16[16,2,28,8,128]{4,3,2,1,0:T(8,128)(2,1)S(1)} %get-tuple-element.18), channel_id=1, source_target_pairs={{0,32},{32,0},{1,33},{33,1},{2,34},{34,2},{3,35},{35,3},{4,36},{36... | collective-permute-start | bytes 5505032 | tf_op jit(solution)/shard_map/ppermute | solution.py:335
  61.9 60.6 %collective-permute-start.13 = (bf16[16,2,28,8,128]{4,3,2,1,0:T(8,128)(2,1)}, bf16[16,2,28,8,128]{4,3,2,1,0:T(8,128)(2,1)}, u32[]{:S(2)}, u32[]{:S(2)}) collective-permute-start(bf16[16,2,28,8,128]{4,3,2,1,0:T(8,128)(2,1)} %get-tuple-element.22), channel_id=1, source_target_pairs={{0,32},{32,0},{1,33},{33,1},{2,34},{34,2},{3,35},{35,3},{4,36},{36... | collective-permute-start | bytes 5505032 | tf_op jit(solution)/shard_map/ppermute | solution.py:341
  62.4 63.8 %all-to-all-start.2 = ((bf16[64,14,8,128]{3,2,1,0:T(8,128)(2,1)}), bf16[64,14,8,128]{3,2,1,0:T(8,128)(2,1)S(1)}, u32[]{:S(2)}, u32[]{:S(2)}) async-start(bf16[64,14,8,128]{3,2,1,0:T(8,128)(2,1)} %bitcast.20), calls=%async_computation.2 | async-start | bytes 3670016 | tf_op jit(solution)/shard_map/all_to_all | solution.py:312
  78.9 43.6 %copy-start.2 = (f32[16,2,28,8,128]{4,3,2,1,0:T(8,128)S(1)}, f32[16,2,28,8,128]{4,3,2,1,0:T(8,128)}, u32[]{:S(2)}) copy-start(f32[16,2,28,8,128]{4,3,2,1,0:T(8,128)} %copy-done.1) | copy-start | bytes 11010052
  79.0 26.5 %collective-permute-start.4 = (bf16[4,128,256]{2,1,0:T(8,128)(2,1)S(1)}, bf16[4,128,256]{2,1,0:T(8,128)(2,1)S(1)}, u32[]{:S(2)}, u32[]{:S(2)}) collective-permute-start(bf16[4,128,256]{2,1,0:T(8,128)(2,1)S(1)} %get-tuple-element.30), channel_id=1, source_target_pairs={{1,0},{2,1},{3,2},{4,3},{5,4},{6,5},{7,6},{8,7},{9,8},{10,9},{11,1... | collective-permute-start | bytes 786440 | tf_op jit(solution)/shard_map/ppermute | solution.py:281
  80.5 25.7 %collective-permute-start.3 = (bf16[4,128,256]{2,1,0:T(8,128)(2,1)S(1)}, bf16[4,128,256]{2,1,0:T(8,128)(2,1)S(1)}, u32[]{:S(2)}, u32[]{:S(2)}) collective-permute-start(bf16[4,128,256]{2,1,0:T(8,128)(2,1)S(1)} %get-tuple-element.31), channel_id=1, source_target_pairs={{0,1},{1,2},{2,3},{3,4},{4,5},{5,6},{6,7},{7,8},{8,9},{9,10},{10,1... | collective-permute-start | bytes 786440 | tf_op jit(solution)/shard_map/ppermute | solution.py:281
  107.0 14.7 %collective-permute-start.5 = (bf16[2,4,128,256]{3,2,1,0:T(8,128)(2,1)S(1)}, bf16[2,4,128,256]{3,2,1,0:T(8,128)(2,1)S(1)}, u32[]{:S(2)}, u32[]{:S(2)}) collective-permute-start(bf16[2,4,128,256]{3,2,1,0:T(8,128)(2,1)S(1)} %pad_maximum_fusion.1), channel_id=1, source_target_pairs={{0,32},{32,64},{64,96},{1,33},{33,65},{65,97},{2,34},{34,66},{66,9... | collective-permute-start | bytes 1572872 | tf_op jit(solution)/shard_map/ppermute | solution.py:281
  111.3 8.7 %collective-permute-start.10 = (bf16[4,128,256]{2,1,0:T(8,128)(2,1)S(1)}, bf16[4,128,256]{2,1,0:T(8,128)(2,1)}, u32[]{:S(2)}, u32[]{:S(2)}) collective-permute-start(bf16[4,128,256]{2,1,0:T(8,128)(2,1)S(1)} %get-tuple-element.26), channel_id=1, source_target_pairs={{1,0},{2,1},{3,2},{4,3},{5,4},{6,5},{7,6},{8,7},{9,8},{10,9},{11,1... | collective-permute-start | bytes 786440 | tf_op jit(solution)/shard_map/ppermute | solution.py:281
  112.6 9.1 %collective-permute-start.9 = (bf16[4,128,256]{2,1,0:T(8,128)(2,1)S(1)}, bf16[4,128,256]{2,1,0:T(8,128)(2,1)}, u32[]{:S(2)}, u32[]{:S(2)}) collective-permute-start(bf16[4,128,256]{2,1,0:T(8,128)(2,1)S(1)} %get-tuple-element.27), channel_id=1, source_target_pairs={{0,1},{1,2},{2,3},{3,4},{4,5},{5,6},{6,7},{7,8},{8,9},{9,10},{10,1... | collective-permute-start | bytes 786440 | tf_op jit(solution)/shard_map/ppermute | solution.py:281
  126.3 44.6 %all-to-all-start = ((bf16[64,14,8,128]{3,2,1,0:T(8,128)(2,1)}), bf16[64,14,8,128]{3,2,1,0:T(8,128)(2,1)}, u32[]{:S(2)}, u32[]{:S(2)}) async-start(bf16[64,14,8,128]{3,2,1,0:T(8,128)(2,1)} %bitcast.21), calls=%async_computation | async-start | bytes 3670016 | tf_op jit(solution)/shard_map/all_to_all | solution.py:312
  170.9 47.0 %all-to-all-start.3 = ((bf16[64,14,8,128]{3,2,1,0:T(8,128)(2,1)}), bf16[64,14,8,128]{3,2,1,0:T(8,128)(2,1)S(1)}, u32[]{:S(2)}, u32[]{:S(2)}) async-start(bf16[64,14,8,128]{3,2,1,0:T(8,128)(2,1)} %copy-done), calls=%async_computation.3 | async-start | bytes 3670016 | tf_op jit(solution)/shard_map/all_to_all | solution.py:312
  177.0 28.4 %copy-start.5 = (bf16[4,2,128,256]{3,2,1,0:T(8,128)(2,1)S(1)}, bf16[4,2,128,256]{3,2,1,0:T(8,128)(2,1)}, u32[]{:S(2)}) copy-start(bf16[4,2,128,256]{3,2,1,0:T(8,128)(2,1)} %latents_ref.3) | copy-start | bytes 1572868
  179.0 26.4 %collective-permute-start.11 = (bf16[2,4,128,256]{3,2,1,0:T(8,128)(2,1)S(1)}, bf16[2,4,128,256]{3,2,1,0:T(8,128)(2,1)S(1)}, u32[]{:S(2)}, u32[]{:S(2)}) collective-permute-start(bf16[2,4,128,256]{3,2,1,0:T(8,128)(2,1)S(1)} %pad_maximum_fusion.3), channel_id=1, source_target_pairs={{32,0},{64,32},{96,64},{33,1},{65,33},{97,65},{34,2},{66,34},{98,6... | collective-permute-start | bytes 1572872 | tf_op jit(solution)/shard_map/ppermute | solution.py:281
  217.9 35.5 %all-to-all-start.1 = ((bf16[64,14,8,128]{3,2,1,0:T(8,128)(2,1)}), bf16[64,14,8,128]{3,2,1,0:T(8,128)(2,1)}, u32[]{:S(2)}, u32[]{:S(2)}) async-start(bf16[64,14,8,128]{3,2,1,0:T(8,128)(2,1)} %shard_map.83), calls=%async_computation.1 | async-start | bytes 3670016 | tf_op jit(solution)/shard_map/all_to_all | solution.py:312
  226.6 27.0 %collective-permute-start.15 = (bf16[64,14,8,128]{3,2,1,0:T(8,128)(2,1)S(1)}, bf16[64,14,8,128]{3,2,1,0:T(8,128)(2,1)}, u32[]{:S(2)}, u32[]{:S(2)}) collective-permute-start(bf16[64,14,8,128]{3,2,1,0:T(8,128)(2,1)S(1)} %all-to-all-done.3), channel_id=1, source_target_pairs={{0,32},{32,0},{1,33},{33,1},{2,34},{34,2},{3,35},{35,3},{4,36},{36... | collective-permute-start | bytes 5505032 | tf_op jit(solution)/shard_map/ppermute | solution.py:356
  253.4 7.3 %collective-permute-start.14 = (bf16[64,14,8,128]{3,2,1,0:T(8,128)(2,1)}, bf16[64,14,8,128]{3,2,1,0:T(8,128)(2,1)S(1)}, u32[]{:S(2)}, u32[]{:S(2)}) collective-permute-start(bf16[64,14,8,128]{3,2,1,0:T(8,128)(2,1)} %all-to-all-done.1), channel_id=1, source_target_pairs={{0,32},{32,0},{1,33},{33,1},{2,34},{34,2},{3,35},{35,3},{4,36},{36... | collective-permute-start | bytes 5505032 | tf_op jit(solution)/shard_map/ppermute | solution.py:357
  (16 other events, 26.3 us)

commit v2 on v0

--- a/solution.py
+++ b/solution.py
@@ -1,11 +1,10 @@
-import functools
-
 import jax
 import jax.numpy as jnp
 from jax import lax
 from jax.experimental import pallas as pl
 from jax.experimental.pallas import tpu as pltpu
 from jax.sharding import Mesh, PartitionSpec as P
+
 
 GROUP = ("zl", "co")
 SPACE = ("zh", "y", "x")
@@ -50,7 +49,7 @@
     lhs = jnp.concatenate(parts, axis=1)
     sums = []
     for k in range(3):
-        taps = [kernel_ref[(i * 3 + j) * 3 + k] for i in range(3) for j in range(3)]
+        taps = [kernel_ref[k, n] for n in range(9)]
         if transposed:
             rhs = jnp.concatenate(taps, axis=1)
             dims = (((1,), (1,)), ((), ()))
@@ -68,12 +67,24 @@
     return s * (1.0 + values * (1.0 - s))
 
 
+def load_taps(source_ref, kernel_ref, sem):
+    copies = [
+        pltpu.make_async_copy(source_ref.at[:, k], kernel_ref.at[k], sem.at[k]) for k in range(3)
+    ]
+    for copy in copies:
+        copy.start()
+    return copies
+
+
 def split_rows(value):
     return value.reshape(2, W, C)
 
 
-def hidden_kernel(own_ref, rows_ref, time_ref, kernel_ref, hidden_ref, active_ref, ext_ref):
+def hidden_kernel(own_ref, rows_ref, time_ref, source_ref, hidden_ref, active_ref, ext_ref, kernel_ref, sem):
+    copies = load_taps(source_ref, kernel_ref, sem)
     fill_ext(ext_ref, own_ref, rows_ref, time_ref, 2, 0)
+    for copy in copies:
+        copy.wait()
 
     def body(t, carry):
         hidden = conv_frame(ext_ref, kernel_ref, t, False)
@@ -84,8 +95,11 @@
     lax.fori_loop(0, FRAMES, body, 0)
 
 
-def hidden_grad_kernel(own_ref, rows_ref, time_ref, kernel_ref, hidden_ref, out_ref, ext_ref):
+def hidden_grad_kernel(own_ref, rows_ref, time_ref, source_ref, hidden_ref, out_ref, ext_ref, kernel_ref, sem):
+    copies = load_taps(source_ref, kernel_ref, sem)
     fill_ext(ext_ref, own_ref, rows_ref, time_ref, 0, 1)
+    for copy in copies:
+        copy.wait()
 
     def body(t, carry):
         grad = conv_frame(ext_ref, kernel_ref, t, True)
@@ -95,8 +109,11 @@
     lax.fori_loop(0, FRAMES, body, 0)
 
 
-def decoded_kernel(own_ref, rows_ref, time_ref, kernel_ref, latents_ref, out_ref, ext_ref):
+def decoded_kernel(own_ref, rows_ref, time_ref, source_ref, latents_ref, out_ref, ext_ref, kernel_ref, sem):
+    copies = load_taps(source_ref, kernel_ref, sem)
     fill_ext(ext_ref, own_ref, rows_ref, time_ref, 2, 0)
+    for copy in copies:
+        copy.wait()
 
     def body(t, carry):
         branch = split_rows(conv_frame(ext_ref, kernel_ref, t, False))
@@ -107,9 +124,12 @@
 
 
 def latent_grad_kernel(
-    own_ref, rows_ref, time_ref, kernel_ref, latents_ref, upstream_ref, out_ref, ext_ref
+    own_ref, rows_ref, time_ref, source_ref, latents_ref, upstream_ref, out_ref, ext_ref, kernel_ref, sem
 ):
+    copies = load_taps(source_ref, kernel_ref, sem)
     fill_ext(ext_ref, own_ref, rows_ref, time_ref, 0, 1)
+    for copy in copies:
+        copy.wait()
 
     def body(t, carry):
         inner = split_rows(conv_frame(ext_ref, kernel_ref, t, True))
@@ -189,25 +209,33 @@
     return pl.CostEstimate(flops=flops, bytes_accessed=moved, transcendentals=0)
 
 
-def whole(kernel, outs, scratch, limit, name, smem=0):
+def whole(kernel, outs, scratch, limit, smem=0, hbm=(), flops=PASS_FLOPS):
     def call(*args):
         moved = sum(a.size * a.dtype.itemsize for a in args)
         moved += sum(o.size * o.dtype.itemsize for o in outs)
-        specs = [
-            pl.BlockSpec(memory_space=pltpu.SMEM if n < smem else pltpu.VMEM) for n in range(len(args))
+        spaces = [
+            pltpu.SMEM if n < smem else pltpu.HBM if n in hbm else pltpu.VMEM for n in range(len(args))
         ]
         return pl.pallas_call(
             kernel,
             out_shape=outs,
-            in_specs=specs,
+            in_specs=[pl.BlockSpec(memory_space=space) for space in spaces],
             out_specs=[pl.BlockSpec(memory_space=pltpu.VMEM) for _ in outs],
             scratch_shapes=scratch,
             compiler_params=pltpu.CompilerParams(vmem_limit_bytes=limit << 20),
-            cost_estimate=cost(PASS_FLOPS, moved),
-            name=name,
+            cost_estimate=cost(flops, moved),
         )(*args)
 
     return call
+
+
+def convolution(kernel, outs):
+    scratch = [
+        pltpu.VMEM((EXT, 4 * W, C), BF),
+        pltpu.VMEM((3, 9, C, C), BF),
+        pltpu.SemaphoreType.DMA((3,)),
+    ]
+    return whole(kernel, outs, scratch, 24, hbm=(3,))
 
 
 STEP = 3
@@ -268,7 +296,9 @@
 def edge_rows(one, two):
     to_above = jnp.stack([one[:, 0], two[:, 0]])
     to_below = jnp.stack([one[:, 1], two[:, 1]])
-    return jnp.stack([swap(to_below, SPACE, 1), swap(to_above, SPACE, -1)])
+    above = swap(to_below, SPACE, 1)
+    below = swap(to_above, SPACE, -1)
+    return jnp.stack([above, below])
 
 
 def two_frames(own, rows, which, start):
@@ -278,10 +308,10 @@
     )
 
 
-def local(latents, first_kernel, second_kernel, upstream):
+def step(latents, first_kernel, second_kernel, upstream):
     core = lax.axis_index("co").astype(jnp.int32).reshape(1)
-    k1 = first_kernel.reshape(TAPS, C, C)
-    k2 = second_kernel.reshape(TAPS, C, C)
+    k1 = first_kernel.reshape(9, 3, C, C)
+    k2 = second_kernel.reshape(9, 3, C, C)
     wide = latents.astype(F32)
     smooth = (wide * jax.nn.sigmoid(wide)).astype(BF)
     block = jax.ShapeDtypeStruct((FRAMES, 2, W, C), BF)
@@ -290,10 +320,10 @@
     rows = edge_rows(smooth, upstream)
     smooth_time = swap(two_frames(smooth, rows, 0, 2), GROUP, 1)
     up_time = swap(two_frames(upstream, rows, 1, 0), GROUP, -1)
-    hidden, active = whole(
-        hidden_kernel, (jax.ShapeDtypeStruct((FRAMES, 2 * W, C), F32), block), [ext], 24, "hidden"
+    hidden, active = convolution(
+        hidden_kernel, (jax.ShapeDtypeStruct((FRAMES, 2 * W, C), F32), block)
     )(smooth, rows, smooth_time, k1)
-    (hidden_grad,) = whole(hidden_grad_kernel, (block,), [ext], 24, "hidden_grad")(
+    (hidden_grad,) = convolution(hidden_grad_kernel, (block,))(
         upstream, rows, up_time, k2, hidden
     )
 
@@ -304,20 +334,10 @@
     half = (16, 2, TAPS, 8, 128)
     pair = (jax.ShapeDtypeStruct(half, F32), jax.ShapeDtypeStruct(half, BF))
     keep2, send2 = whole(
-        second_grad_kernel,
-        pair,
-        [ext, pltpu.VMEM((3, EXT, 4 * W, C), BF), pltpu.VMEM((C, FRAMES * 2 * W), BF)],
-        40,
-        "second_grad",
-        1,
+        second_grad_kernel, pair, [ext, pltpu.VMEM((3, EXT, 4 * W, C), BF), pltpu.VMEM((C, FRAMES * 2 * W), BF)], 40, 1
     )(core, active, upstream, rows, up_time)
     keep1, send1 = whole(
-        first_grad_kernel,
-        pair,
-        [ext, pltpu.VMEM((3, FRAMES * 2 * W, C), BF), pltpu.VMEM((EXT, C, 4 * W), BF)],
-        40,
-        "first_grad",
-        1,
+        first_grad_kernel, pair, [ext, pltpu.VMEM((3, FRAMES * 2 * W, C), BF), pltpu.VMEM((EXT, C, 4 * W), BF)], 40, 1
     )(core, hidden_grad, smooth, rows, smooth_time)
 
     across = [(0, 1), (1, 0)]
@@ -327,16 +347,14 @@
     mine = jnp.stack([(keep2 + got2.astype(F32)).astype(BF), (keep1 + got1.astype(F32)).astype(BF)])
     mine = mine.reshape(chips, 64 // chips * TAPS, 8, 128)
     parts = lax.all_to_all(mine, CHIPS, 0, 0, tiled=False)
-    (spread,) = whole(total_kernel, (jax.ShapeDtypeStruct(parts.shape, BF),), [], 16, "total")(parts)
+    (spread,) = whole(total_kernel, (jax.ShapeDtypeStruct(parts.shape, BF),), [], 16, flops=1 << 28)(parts)
     own = lax.all_to_all(spread, CHIPS, 0, 0, tiled=False)
     far = lax.ppermute(own, "co", across)
 
-    (decoded,) = whole(decoded_kernel, (block,), [ext], 24, "decoded")(
+    (decoded,) = convolution(decoded_kernel, (block,))(
         active, late, active_time, k2, latents
     )
-    (latent_grad,) = whole(latent_grad_kernel, (block,), [ext], 24, "latent_grad")(
-        hidden_grad, late, grad_time, k1, latents, upstream
-    )
+    (latent_grad,) = convolution(latent_grad_kernel, (block,))(hidden_grad, late, grad_time, k1, latents, upstream)
     first_grad, second_grad = assemble(core, own, far)
     shape = first_kernel.shape
     return (decoded, latent_grad, first_grad.reshape(shape), second_grad.reshape(shape))
@@ -346,7 +364,7 @@
     fine = Mesh(mesh.devices.reshape(sizes), ("zl", "co", "zh", "y", "x"))
     placed = (P(GROUP, SPACE, None, None), P(), P(), P(GROUP, SPACE, None, None))
     return jax.shard_map(
-        local,
+        step,
         mesh=fine,
         in_specs=placed,
         out_specs=(P(GROUP, SPACE, None, None), P(GROUP, SPACE, None, None), P(), P()),

time: 226 us -> 227 us (level)
  transfers between devices with their start and end apart: 11 -> 11, of which waited for: 7 -> 7; matrix products, arithmetic and copies ran while one was open for 1% -> 1% of each run, Pallas kernels for 9% -> 10%
where the time goes in v2:
time: 227 us
  blocking collectives  99.5 us (44%)
  waiting for transfers between devices  50.4 us (22%)
  Pallas kernels  40.4 us (18%)
  starting transfers between devices  27.9 us (12%)
  other arithmetic  3.9 us (2%)
  local copies, waits for them, and re-layouts  3.39 us (1%)
    all_to_all x1, blocking collectives, step(): own = lax.all_to_all(spread, CHIPS, 0, 0, tiled=False)  50 us
    all_to_all x1, blocking collectives, step(): parts = lax.all_to_all(mine, CHIPS, 0, 0, tiled=False)  49.5 us
    ppermute x8, waiting for transfers between devices, swap(): return lax.ppermute(value, axis, pairs)  47.5 us
    pallas_call x7, Pallas kernels, call(): pl.pallas_call(kernel, out_shape=outs, in_specs=[pl.BlockSpec(memory_spac...  33.8 us
    ppermute x8, starting transfers between devices, swap(): return lax.ppermute(value, axis, pairs)  27.3 us
    pallas_call x1, Pallas kernels, assemble(): pl.pallas_call(assemble_kernel, out_shape=(shape, shape), grid=(TAPS // S...  6.61 us
  transfers between devices with their start and end apart: 11, of which 7 were waited for; matrix products, arithmetic and copies ran while one was open for 1% of the time, Pallas kernels for 10%

profile of v2, /device:TPU:96, one launch (start us, length us, event | category | flops | bytes accessed | tf_op | source)
XLA Modules:
  0.0 226.6 jit_solution(9243405987435266748)
XLA Ops:
  3.2 7.1 %collective-permute-start.1 = (bf16[2,4,128,256]{3,2,1,0:T(8,128)(2,1)S(1)}, bf16[2,4,128,256]{3,2,1,0:T(8,128)(2,1)S(1)}, u32[]{:S(2)}, u32[]{:S(2)}) collective-permute-start(bf16[2,4,128,256]{3,2,1,0:T(8,128)(2,1)S(1)} %pad_maximum_fusion.4), channel_id=1, source_target_pairs={{1,0},{2,1},{3,2},{4,3},{5,4},{6,5},{7,6},{8,7},{9,8},{10,9},{11,1... | collective-permute-start | bytes 1572872 | tf_op jit(solution)/shard_map/ppermute | solution.py:293
  12.3 9.2 %collective-permute-done.1 = bf16[2,4,128,256]{3,2,1,0:T(8,128)(2,1)S(1)} collective-permute-done((bf16[2,4,128,256]{3,2,1,0:T(8,128)(2,1)S(1)}, bf16[2,4,128,256]{3,2,1,0:T(8,128)(2,1)S(1)}, u32[]{:S(2)}, u32[]{:S(2)}) %collective-permute-start.1) | collective-permute-done | bytes 524320 | tf_op jit(solution)/shard_map/ppermute | solution.py:293
  21.5 10.0 %collective-permute-done = bf16[2,4,128,256]{3,2,1,0:T(8,128)(2,1)S(1)} collective-permute-done((bf16[2,4,128,256]{3,2,1,0:T(8,128)(2,1)S(1)}, bf16[2,4,128,256]{3,2,1,0:T(8,128)(2,1)S(1)}, u32[]{:S(2)}, u32[]{:S(2)}) %collective-permute-start) | collective-permute-done | bytes 524320 | tf_op jit(solution)/shard_map/ppermute | solution.py:293
  34.3 3.6 %collective-permute-start.3 = (bf16[2,4,128,256]{3,2,1,0:T(8,128)(2,1)}, bf16[2,4,128,256]{3,2,1,0:T(8,128)(2,1)S(1)}, u32[]{:S(2)}, u32[]{:S(2)}) collective-permute-start(bf16[2,4,128,256]{3,2,1,0:T(8,128)(2,1)} %pad_maximum_fusion.6), channel_id=1, source_target_pairs={{32,0},{64,32},{96,64},{33,1},{65,33},{97,65},{34,2},{66,34},{98,6... | collective-permute-start | bytes 1572872 | tf_op jit(solution)/shard_map/ppermute | solution.py:293
  38.1 3.9 %collective-permute-done.2.time_ref = bf16[2,4,128,256]{3,2,1,0:T(8,128)(2,1)S(1)} collective-permute-done((bf16[2,4,128,256]{3,2,1,0:T(8,128)(2,1)S(1)}, bf16[2,4,128,256]{3,2,1,0:T(8,128)(2,1)S(1)}, u32[]{:S(2)}, u32[]{:S(2)}) %collective-permute-start.2) | collective-permute-done | bytes 524320 | tf_op jit(solution)/shard_map/ppermute | solution.py:293
  42.0 2.0 copy-done.3
  44.0 4.8 %shard_map.75 = (f32[4,256,256]{2,1,0:T(8,128)S(1)}, bf16[4,2,128,256]{3,2,1,0:T(8,128)(2,1)S(1)}) custom-call(bf16[4,2,128,256]{3,2,1,0:T(8,128)(2,1)S(1)} %copy.13.own_ref, bf16[2,2,4,128,256]{4,3,2,1,0:T(8,128)(2,1)S(1)} %pad_maximum_fusion.1.rows_ref, bf16[2,4,128,256]{3,2,1,0:T(8,128)(2,1)S(1)} %collective-permute-done.2.time_ref, ...), custom_call_target="tpu_custom_call" | custom-call | flops 3623878656 | bytes 7208960 | tf_op jit(solution)/shard_map/pallas_call | solution.py:219
  48.9 4.9 %shard_map.76.own_ref.grad_ref = bf16[4,2,128,256]{3,2,1,0:T(8,128)(2,1)S(1)} custom-call(bf16[4,2,128,256]{3,2,1,0:T(8,128)(2,1)S(1)} %copy-done, bf16[2,2,4,128,256]{4,3,2,1,0:T(8,128)(2,1)S(1)} %pad_maximum_fusion.1.rows_ref, bf16[2,4,128,256]{3,2,1,0:T(8,128)(2,1)S(1)} %collective-permute-done.3.time_ref, bf16[9,3,256,256]{3,2,1,0:T(8,128)(2,1)S(1)} %bitcast.72, ...), custom_call_target="tpu_custom_call" | custom-call | flops 3623878656 | bytes 7208960 | tf_op jit(solution)/shard_map/pallas_call | solution.py:219
  53.8 5.0 %shard_map.80 = (f32[16,2,27,8,128]{4,3,2,1,0:T(8,128)S(1)}, bf16[16,2,27,8,128]{4,3,2,1,0:T(8,128)(2,1)S(1)}) custom-call(s32[1]{0:T(128)} %bitcast.28.core_ref, bf16[4,2,128,256]{3,2,1,0:T(8,128)(2,1)S(1)} %shard_map.76.own_ref.grad_ref, bf16[4,2,128,256]{3,2,1,0:T(8,128)(2,1)S(1)} %copy.13.own_ref, ...), custom_call_target="tpu_custom_call" | custom-call | flops 3623878656 | bytes 7929860 | tf_op jit(solution)/shard_map/pallas_call | solution.py:219
  58.8 5.6 %shard_map.79 = (f32[16,2,27,8,128]{4,3,2,1,0:T(8,128)S(1)}, bf16[16,2,27,8,128]{4,3,2,1,0:T(8,128)(2,1)S(1)}) custom-call(s32[1]{0:T(128)} %bitcast.28.core_ref, bf16[4,2,128,256]{3,2,1,0:T(8,128)(2,1)S(1)} %get-tuple-element.12.own_ref.active_ref, bf16[4,2,128,256]{3,2,1,0:T(8,128)(2,1)S(1)} %copy-done, ...), custom_call_target="tpu_custom_call" | custom-call | flops 3623878656 | bytes 7929860 | tf_op jit(solution)/shard_map/pallas_call | solution.py:219
  65.4 2.9 %collective-permute-done.8 = bf16[16,2,27,8,128]{4,3,2,1,0:T(8,128)(2,1)S(1)} collective-permute-done((bf16[16,2,27,8,128]{4,3,2,1,0:T(8,128)(2,1)S(1)}, bf16[16,2,27,8,128]{4,3,2,1,0:T(8,128)(2,1)S(1)}, u32[]{:S(2)}, u32[]{:S(2)}) %collective-permute-start.8) | collective-permute-done | bytes 1769504 | tf_op jit(solution)/shard_map/ppermute | solution.py:344
  69.0 49.5 %all_to_all.10.parts_ref = bf16[64,27,8,128]{3,2,1,0:T(8,128)(2,1)S(1)} all-to-all(bf16[64,27,8,128]{3,2,1,0:T(8,128)(2,1)S(1)} %bitcast.76), channel_id=1, replica_groups=mesh['zl'=2,'co'=2,'zh'=2,'y'=4,'x'=4] {'zl','zh','y','x'}, dimensions={0} | all-to-all | bytes 7077888 | tf_op jit(solution)/shard_map/all_to_all | solution.py:349
  118.5 2.3 %shard_map.81 = bf16[64,27,8,128]{3,2,1,0:T(8,128)(2,1)S(1)} custom-call(bf16[64,27,8,128]{3,2,1,0:T(8,128)(2,1)S(1)} %all_to_all.10.parts_ref), custom_call_target="tpu_custom_call" | custom-call | flops 268435456 | bytes 7077888 | tf_op jit(solution)/shard_map/pallas_call | solution.py:219
  120.8 50.0 %all_to_all.11 = bf16[64,27,8,128]{3,2,1,0:T(8,128)(2,1)S(1)} all-to-all(bf16[64,27,8,128]{3,2,1,0:T(8,128)(2,1)S(1)} %shard_map.81), channel_id=1, replica_groups=mesh['zl'=2,'co'=2,'zh'=2,'y'=4,'x'=4] {'zl','zh','y','x'}, dimensions={0} | all-to-all | bytes 7077888 | tf_op jit(solution)/shard_map/all_to_all | solution.py:351
  171.0 5.1 %collective-permute-start.5 = (bf16[2,4,128,256]{3,2,1,0:T(8,128)(2,1)S(1)}, bf16[2,4,128,256]{3,2,1,0:T(8,128)(2,1)S(1)}, u32[]{:S(2)}, u32[]{:S(2)}) collective-permute-start(bf16[2,4,128,256]{3,2,1,0:T(8,128)(2,1)S(1)} %pad_maximum_fusion.8), channel_id=1, source_target_pairs={{1,0},{2,1},{3,2},{4,3},{5,4},{6,5},{7,6},{8,7},{9,8},{10,9},{11,1... | collective-permute-start | bytes 1572872 | tf_op jit(solution)/shard_map/ppermute | solution.py:293
  176.2 2.1 collective-permute-start.4
  178.3 9.5 %collective-permute-done.5 = bf16[2,4,128,256]{3,2,1,0:T(8,128)(2,1)S(1)} collective-permute-done((bf16[2,4,128,256]{3,2,1,0:T(8,128)(2,1)S(1)}, bf16[2,4,128,256]{3,2,1,0:T(8,128)(2,1)S(1)}, u32[]{:S(2)}, u32[]{:S(2)}) %collective-permute-start.5) | collective-permute-done | bytes 524320 | tf_op jit(solution)/shard_map/ppermute | solution.py:293
  187.8 10.3 %collective-permute-done.4 = bf16[2,4,128,256]{3,2,1,0:T(8,128)(2,1)S(1)} collective-permute-done((bf16[2,4,128,256]{3,2,1,0:T(8,128)(2,1)S(1)}, bf16[2,4,128,256]{3,2,1,0:T(8,128)(2,1)S(1)}, u32[]{:S(2)}, u32[]{:S(2)}) %collective-permute-start.4) | collective-permute-done | bytes 524320 | tf_op jit(solution)/shard_map/ppermute | solution.py:293
  198.1 1.9 collective-permute-start.6
  200.2 3.6 %collective-permute-start.7 = (bf16[2,4,128,256]{3,2,1,0:T(8,128)(2,1)S(1)}, bf16[2,4,128,256]{3,2,1,0:T(8,128)(2,1)S(1)}, u32[]{:S(2)}, u32[]{:S(2)}) collective-permute-start(bf16[2,4,128,256]{3,2,1,0:T(8,128)(2,1)S(1)} %pad_maximum_fusion.10), channel_id=1, source_target_pairs={{32,0},{64,32},{96,64},{33,1},{65,33},{97,65},{34,2},{66,34},{98,6... | collective-permute-start | bytes 1572872 | tf_op jit(solution)/shard_map/ppermute | solution.py:293
  203.9 4.7 %collective-permute-done.6.time_ref = bf16[2,4,128,256]{3,2,1,0:T(8,128)(2,1)S(1)} collective-permute-done((bf16[2,4,128,256]{3,2,1,0:T(8,128)(2,1)S(1)}, bf16[2,4,128,256]{3,2,1,0:T(8,128)(2,1)S(1)}, u32[]{:S(2)}, u32[]{:S(2)}) %collective-permute-start.6) | collective-permute-done | bytes 524320 | tf_op jit(solution)/shard_map/ppermute | solution.py:293
  208.6 5.5 %shard_map.77 = bf16[4,2,128,256]{3,2,1,0:T(8,128)(2,1)} custom-call(bf16[4,2,128,256]{3,2,1,0:T(8,128)(2,1)S(1)} %get-tuple-element.12.own_ref.active_ref, bf16[2,2,4,128,256]{4,3,2,1,0:T(8,128)(2,1)S(1)} %pad_maximum_fusion.2.rows_ref, bf16[2,4,128,256]{3,2,1,0:T(8,128)(2,1)S(1)} %collective-permute-done.6.time_ref, bf16[9,3,256,256]{3,2,1,0:T(8,128)(2,1)S(1)} %bitcast.73, ...), custom_call_target="tpu_custom_call" | custom-call | flops 3623878656 | bytes 6684672 | tf_op jit(solution)/shard_map/pallas_call | solution.py:219
  214.2 5.8 %shard_map.78 = bf16[4,2,128,256]{3,2,1,0:T(8,128)(2,1)} custom-call(bf16[4,2,128,256]{3,2,1,0:T(8,128)(2,1)S(1)} %shard_map.76.own_ref.grad_ref, bf16[2,2,4,128,256]{4,3,2,1,0:T(8,128)(2,1)S(1)} %pad_maximum_fusion.2.rows_ref, bf16[2,4,128,256]{3,2,1,0:T(8,128)(2,1)S(1)} %collective-permute-done.7.time_ref, bf16[9,3,256,256]{3,2,1,0:T(8,128)(2,1)S(1)} %bitcast.75, ...), custom_call_target="tpu_custom_call" | custom-call | flops 3623878656 | bytes 7208960 | tf_op jit(solution)/shard_map/pallas_call | solution.py:219
  220.0 6.6 %assemble.1 = (f32[27,256,256]{2,1,0:T(8,128)}, f32[27,256,256]{2,1,0:T(8,128)}) custom-call(s32[1]{0:T(128)} %bitcast.28.core_ref, bf16[2,16,2,27,8,128]{5,4,3,2,1,0:T(8,128)(2,1)S(1)} %bitcast.68, bf16[2,16,2,27,8,128]{5,4,3,2,1,0:T(8,128)(2,1)S(1)} %bitcast.69, bf16[2,16,2,27,8,128]{5,4,3,2,1,0:T(8,128)(2,1)S(1)} %bitcast.70, ...), custom_call_target="tpu_custom_call" | custom-call | flops 16777216 | bytes 29360128 | tf_op jit(solution)/shard_map/assemble/pallas_call | solution.py:263
  (45 shorter events, 9.8 us)
Async XLA Ops:
  2.0 31.5 %slice-start = ((bf16[4,2,128,256]{3,2,1,0:T(8,128)(2,1)}), bf16[2,2,128,256]{3,2,1,0:T(8,128)(2,1)S(1)}, s32[]{:S(2)}) async-start(bf16[4,2,128,256]{3,2,1,0:T(8,128)(2,1)} %own_ref.3), calls=%async_computation.2 | async-start | bytes 524288 | tf_op jit(solution)/shard_map/slice | solution.py:307
  3.2 18.3 %collective-permute-start.1 = (bf16[2,4,128,256]{3,2,1,0:T(8,128)(2,1)S(1)}, bf16[2,4,128,256]{3,2,1,0:T(8,128)(2,1)S(1)}, u32[]{:S(2)}, u32[]{:S(2)}) collective-permute-start(bf16[2,4,128,256]{3,2,1,0:T(8,128)(2,1)S(1)} %pad_maximum_fusion.4), channel_id=1, source_target_pairs={{1,0},{2,1},{3,2},{4,3},{5,4},{6,5},{7,6},{8,7},{9,8},{10,9},{11,1... | collective-permute-start | bytes 1572872 | tf_op jit(solution)/shard_map/ppermute | solution.py:293
  10.4 21.1 %collective-permute-start = (bf16[2,4,128,256]{3,2,1,0:T(8,128)(2,1)S(1)}, bf16[2,4,128,256]{3,2,1,0:T(8,128)(2,1)S(1)}, u32[]{:S(2)}, u32[]{:S(2)}) collective-permute-start(bf16[2,4,128,256]{3,2,1,0:T(8,128)(2,1)S(1)} %pad_maximum_fusion.3), channel_id=1, source_target_pairs={{0,1},{1,2},{2,3},{3,4},{4,5},{5,6},{6,7},{7,8},{8,9},{9,10},{10,1... | collective-permute-start | bytes 1572872 | tf_op jit(solution)/shard_map/ppermute | solution.py:293
  31.5 10.5 %collective-permute-start.2 = (bf16[2,4,128,256]{3,2,1,0:T(8,128)(2,1)S(1)}, bf16[2,4,128,256]{3,2,1,0:T(8,128)(2,1)S(1)}, u32[]{:S(2)}, u32[]{:S(2)}) collective-permute-start(bf16[2,4,128,256]{3,2,1,0:T(8,128)(2,1)S(1)} %pad_maximum_fusion.5), channel_id=1, source_target_pairs={{0,32},{32,64},{64,96},{1,33},{33,65},{65,97},{2,34},{34,66},{66,9... | collective-permute-start | bytes 1572872 | tf_op jit(solution)/shard_map/ppermute | solution.py:293
  34.3 14.5 %collective-permute-start.3 = (bf16[2,4,128,256]{3,2,1,0:T(8,128)(2,1)}, bf16[2,4,128,256]{3,2,1,0:T(8,128)(2,1)S(1)}, u32[]{:S(2)}, u32[]{:S(2)}) collective-permute-start(bf16[2,4,128,256]{3,2,1,0:T(8,128)(2,1)} %pad_maximum_fusion.6), channel_id=1, source_target_pairs={{32,0},{64,32},{96,64},{33,1},{65,33},{97,65},{34,2},{66,34},{98,6... | collective-permute-start | bytes 1572872 | tf_op jit(solution)/shard_map/ppermute | solution.py:293
  42.0 2.0 copy-start.3
  44.0 4.8 %copy-start = (bf16[4,2,128,256]{3,2,1,0:T(8,128)(2,1)S(1)}, bf16[4,2,128,256]{3,2,1,0:T(8,128)(2,1)}, u32[]{:S(2)}) copy-start(bf16[4,2,128,256]{3,2,1,0:T(8,128)(2,1)} %own_ref.3) | copy-start | bytes 1572868
  44.0 4.8 %copy-start.2 = (bf16[3,3,3,256,256]{4,3,2,1,0:T(8,128)(2,1)S(1)}, bf16[3,3,3,256,256]{4,3,2,1,0:T(8,128)(2,1)}, u32[]{:S(2)}) copy-start(bf16[3,3,3,256,256]{4,3,2,1,0:T(8,128)(2,1)} %param.6) | copy-start | bytes 10616836
  58.7 6.2 %collective-permute-start.9 = (bf16[16,2,27,8,128]{4,3,2,1,0:T(8,128)(2,1)S(1)}, bf16[16,2,27,8,128]{4,3,2,1,0:T(8,128)(2,1)S(1)}, u32[]{:S(2)}, u32[]{:S(2)}) collective-permute-start(bf16[16,2,27,8,128]{4,3,2,1,0:T(8,128)(2,1)S(1)} %get-tuple-element.17), channel_id=1, source_target_pairs={{0,32},{32,0},{1,33},{33,1},{2,34},{34,2},{3,35},{35,3},{4,36},{36... | collective-permute-start | bytes 5308424 | tf_op jit(solution)/shard_map/ppermute | solution.py:345
  64.4 3.9 %collective-permute-start.8 = (bf16[16,2,27,8,128]{4,3,2,1,0:T(8,128)(2,1)S(1)}, bf16[16,2,27,8,128]{4,3,2,1,0:T(8,128)(2,1)S(1)}, u32[]{:S(2)}, u32[]{:S(2)}) collective-permute-start(bf16[16,2,27,8,128]{4,3,2,1,0:T(8,128)(2,1)S(1)} %get-tuple-element.15), channel_id=1, source_target_pairs={{0,32},{32,0},{1,33},{33,1},{2,34},{34,2},{3,35},{35,3},{4,36},{36... | collective-permute-start | bytes 5308424 | tf_op jit(solution)/shard_map/ppermute | solution.py:344
  170.9 49.1 %collective-permute-start.10 = (bf16[64,27,8,128]{3,2,1,0:T(8,128)(2,1)S(1)}, bf16[64,27,8,128]{3,2,1,0:T(8,128)(2,1)S(1)}, u32[]{:S(2)}, u32[]{:S(2)}) collective-permute-start(bf16[64,27,8,128]{3,2,1,0:T(8,128)(2,1)S(1)} %all_to_all.11), channel_id=1, source_target_pairs={{0,32},{32,0},{1,33},{33,1},{2,34},{34,2},{3,35},{35,3},{4,36},{36... | collective-permute-start | bytes 10616840 | tf_op jit(solution)/shard_map/ppermute | solution.py:352
  171.0 16.7 %collective-permute-start.5 = (bf16[2,4,128,256]{3,2,1,0:T(8,128)(2,1)S(1)}, bf16[2,4,128,256]{3,2,1,0:T(8,128)(2,1)S(1)}, u32[]{:S(2)}, u32[]{:S(2)}) collective-permute-start(bf16[2,4,128,256]{3,2,1,0:T(8,128)(2,1)S(1)} %pad_maximum_fusion.8), channel_id=1, source_target_pairs={{1,0},{2,1},{3,2},{4,3},{5,4},{6,5},{7,6},{8,7},{9,8},{10,9},{11,1... | collective-permute-start | bytes 1572872 | tf_op jit(solution)/shard_map/ppermute | solution.py:293
  176.1 32.5 %copy-start.1 = (bf16[4,2,128,256]{3,2,1,0:T(8,128)(2,1)S(1)}, bf16[4,2,128,256]{3,2,1,0:T(8,128)(2,1)}, u32[]{:S(2)}) copy-start(bf16[4,2,128,256]{3,2,1,0:T(8,128)(2,1)} %latents_ref.3) | copy-start | bytes 1572868
  176.2 21.9 %collective-permute-start.4 = (bf16[2,4,128,256]{3,2,1,0:T(8,128)(2,1)S(1)}, bf16[2,4,128,256]{3,2,1,0:T(8,128)(2,1)S(1)}, u32[]{:S(2)}, u32[]{:S(2)}) collective-permute-start(bf16[2,4,128,256]{3,2,1,0:T(8,128)(2,1)S(1)} %pad_maximum_fusion.7), channel_id=1, source_target_pairs={{0,1},{1,2},{2,3},{3,4},{4,5},{5,6},{6,7},{7,8},{8,9},{9,10},{10,1... | collective-permute-start | bytes 1572872 | tf_op jit(solution)/shard_map/ppermute | solution.py:293
  198.1 10.5 %collective-permute-start.6 = (bf16[2,4,128,256]{3,2,1,0:T(8,128)(2,1)S(1)}, bf16[2,4,128,256]{3,2,1,0:T(8,128)(2,1)S(1)}, u32[]{:S(2)}, u32[]{:S(2)}) collective-permute-start(bf16[2,4,128,256]{3,2,1,0:T(8,128)(2,1)S(1)} %pad_maximum_fusion.9), channel_id=1, source_target_pairs={{0,32},{32,64},{64,96},{1,33},{33,65},{65,97},{2,34},{34,66},{66,9... | collective-permute-start | bytes 1572872 | tf_op jit(solution)/shard_map/ppermute | solution.py:293
  200.2 14.0 %collective-permute-start.7 = (bf16[2,4,128,256]{3,2,1,0:T(8,128)(2,1)S(1)}, bf16[2,4,128,256]{3,2,1,0:T(8,128)(2,1)S(1)}, u32[]{:S(2)}, u32[]{:S(2)}) collective-permute-start(bf16[2,4,128,256]{3,2,1,0:T(8,128)(2,1)S(1)} %pad_maximum_fusion.10), channel_id=1, source_target_pairs={{32,0},{64,32},{96,64},{33,1},{65,33},{97,65},{34,2},{66,34},{98,6... | collective-permute-start | bytes 1572872 | tf_op jit(solution)/shard_map/ppermute | solution.py:293
  203.9 10.3 %copy-start.4 = (bf16[3,3,3,256,256]{4,3,2,1,0:T(8,128)(2,1)S(1)}, bf16[3,3,3,256,256]{4,3,2,1,0:T(8,128)(2,1)}, u32[]{:S(2)}) copy-start(bf16[3,3,3,256,256]{4,3,2,1,0:T(8,128)(2,1)} %param.5) | copy-start | bytes 10616836

commit v3 on v2

--- a/solution.py
+++ b/solution.py
@@ -1,5 +1,8 @@
+import math
+
 import jax
 import jax.numpy as jnp
+import numpy as np
 from jax import lax
 from jax.experimental import pallas as pl
 from jax.experimental.pallas import tpu as pltpu
@@ -8,7 +11,7 @@
 
 GROUP = ("zl", "co")
 SPACE = ("zh", "y", "x")
-CHIPS = ("zl", "zh", "y", "x")
+ALL = ("zl", "co", "zh", "y", "x")
 C = 256
 W = 128
 FRAMES = 4
@@ -273,18 +276,37 @@
 
 
 def total_kernel(parts_ref, out_ref):
-    count = parts_ref.shape[0]
-
-    def body(p, carry):
-        total = parts_ref[0, p].astype(F32)
-        for n in range(1, count):
-            total = total + parts_ref[n, p].astype(F32)
-        rounded = total.astype(BF)
-        for n in range(count):
-            out_ref[n, p] = rounded
+    def body(q, carry):
+        value = parts_ref[0, q].astype(F32)
+        for n in range(1, parts_ref.shape[0]):
+            value = value + parts_ref[n, q].astype(F32)
+        rounded = value.astype(BF)
+        for n in range(out_ref.shape[0]):
+            out_ref[n, q] = rounded
         return carry
 
     lax.fori_loop(0, parts_ref.shape[1], body, 0)
+
+
+def total(parts, copies):
+    shape = jax.ShapeDtypeStruct((copies, *parts.shape[1:]), BF)
+    return whole(total_kernel, (shape,), [], 16, flops=1 << 28)(parts)[0]
+
+
+def stage_groups():
+    sizes = [lax.axis_size(axis) for axis in ALL]
+    grid = np.arange(math.prod(sizes)).reshape(sizes)
+    near, rest = ([], [])
+    for core, axis in ((0, 3), (1, 2)):
+        chips = np.moveaxis(grid[:, core], axis, -1)
+        lines = chips.reshape(-1, chips.shape[-1])
+        near += lines.tolist()
+        rest += lines.T.tolist()
+    return near, rest
+
+
+def exchange(value, groups):
+    return lax.all_to_all(value, ALL, 0, 0, axis_index_groups=groups, tiled=False)
 
 
 def swap(value, axis, steps):
@@ -343,12 +365,16 @@
     across = [(0, 1), (1, 0)]
     got2 = lax.ppermute(send2, "co", across)
     got1 = lax.ppermute(send1, "co", across)
-    chips = lax.axis_size(CHIPS)
     mine = jnp.stack([(keep2 + got2.astype(F32)).astype(BF), (keep1 + got1.astype(F32)).astype(BF)])
-    mine = mine.reshape(chips, 64 // chips * TAPS, 8, 128)
-    parts = lax.all_to_all(mine, CHIPS, 0, 0, tiled=False)
-    (spread,) = whole(total_kernel, (jax.ShapeDtypeStruct(parts.shape, BF),), [], 16, flops=1 << 28)(parts)
-    own = lax.all_to_all(spread, CHIPS, 0, 0, tiled=False)
+    near, rest = stage_groups()
+    first, second = (len(near[0]), len(rest[0]))
+    block_rows = 64 // (first * second) * TAPS
+    parts = exchange(mine.reshape(first, second, block_rows, 8, 128), near)
+    quarter = total(parts, 1)
+    parts = exchange(quarter.reshape(second, block_rows, 8, 128), rest)
+    spread = total(parts[:, None], second)
+    quarter = exchange(spread.reshape(second, block_rows, 8, 128), rest)
+    own = exchange(jnp.broadcast_to(quarter[None], (first, *quarter.shape)), near)
     far = lax.ppermute(own, "co", across)
 
     (decoded,) = convolution(decoded_kernel, (block,))(

time: 227 us -> 214 us (0.943)
  blocking collectives: 99.5 us -> 86.8 us
    all_to_all x2 -> x4, blocking collectives: 99.5 us -> 86.8 us  [exchange(): lax.all_to_all(value, ALL, 0, 0, axis_index_groups=groups, tiled=False)]
    pallas_call x7 -> x8, Pallas kernels: 33.8 us -> 32.2 us  [call(): pl.pallas_call(kernel, out_shape=outs, in_specs=[pl.BlockSpec(memory_spac...]
where the time goes in v3:
time: 214 us; the launch traced here: 213 us
  blocking collectives  86.8 us (41%)
  waiting for transfers between devices  50.2 us (23%)
  Pallas kernels  38.8 us (18%)
  starting transfers between devices  28.6 us (13%)
  other arithmetic  3.9 us (2%)
  local copies, waits for them, and re-layouts  3.84 us (2%)
    all_to_all x4, blocking collectives, exchange(): lax.all_to_all(value, ALL, 0, 0, axis_index_groups=groups, tiled=False)  86.8 us
    ppermute x8, waiting for transfers between devices, swap(): return lax.ppermute(value, axis, pairs)  47.3 us
    pallas_call x8, Pallas kernels, call(): pl.pallas_call(kernel, out_shape=outs, in_specs=[pl.BlockSpec(memory_spac...  32.2 us
    ppermute x8, starting transfers between devices, swap(): return lax.ppermute(value, axis, pairs)  27.9 us
    pallas_call x1, Pallas kernels, assemble(): pl.pallas_call(assemble_kernel, out_shape=(shape, shape), grid=(TAPS // S...  6.61 us
  transfers between devices with their start and end apart: 11, of which 7 were waited for; matrix products, arithmetic and copies ran while one was open for 1% of the time, Pallas kernels for 10%

profile of v3, /device:TPU:96, one launch (start us, length us, event | category | flops | bytes accessed | tf_op | source)
XLA Modules:
  0.0 213.1 jit_solution(1948502635564378)
XLA Ops:
  3.2 7.1 %collective-permute-start.1 = (bf16[2,4,128,256]{3,2,1,0:T(8,128)(2,1)S(1)}, bf16[2,4,128,256]{3,2,1,0:T(8,128)(2,1)S(1)}, u32[]{:S(2)}, u32[]{:S(2)}) collective-permute-start(bf16[2,4,128,256]{3,2,1,0:T(8,128)(2,1)S(1)} %pad_maximum_fusion.4), channel_id=1, source_target_pairs={{1,0},{2,1},{3,2},{4,3},{5,4},{6,5},{7,6},{8,7},{9,8},{10,9},{11,1... | collective-permute-start | bytes 1572872 | tf_op jit(solution)/shard_map/ppermute | solution.py:315
  12.3 9.2 %collective-permute-done.1 = bf16[2,4,128,256]{3,2,1,0:T(8,128)(2,1)S(1)} collective-permute-done((bf16[2,4,128,256]{3,2,1,0:T(8,128)(2,1)S(1)}, bf16[2,4,128,256]{3,2,1,0:T(8,128)(2,1)S(1)}, u32[]{:S(2)}, u32[]{:S(2)}) %collective-permute-start.1) | collective-permute-done | bytes 524320 | tf_op jit(solution)/shard_map/ppermute | solution.py:315
  21.5 10.0 %collective-permute-done = bf16[2,4,128,256]{3,2,1,0:T(8,128)(2,1)S(1)} collective-permute-done((bf16[2,4,128,256]{3,2,1,0:T(8,128)(2,1)S(1)}, bf16[2,4,128,256]{3,2,1,0:T(8,128)(2,1)S(1)}, u32[]{:S(2)}, u32[]{:S(2)}) %collective-permute-start) | collective-permute-done | bytes 524320 | tf_op jit(solution)/shard_map/ppermute | solution.py:315
  34.3 3.6 %collective-permute-start.3 = (bf16[2,4,128,256]{3,2,1,0:T(8,128)(2,1)}, bf16[2,4,128,256]{3,2,1,0:T(8,128)(2,1)S(1)}, u32[]{:S(2)}, u32[]{:S(2)}) collective-permute-start(bf16[2,4,128,256]{3,2,1,0:T(8,128)(2,1)} %pad_maximum_fusion.6), channel_id=1, source_target_pairs={{32,0},{64,32},{96,64},{33,1},{65,33},{97,65},{34,2},{66,34},{98,6... | collective-permute-start | bytes 1572872 | tf_op jit(solution)/shard_map/ppermute | solution.py:315
  38.1 3.9 %collective-permute-done.2.time_ref = bf16[2,4,128,256]{3,2,1,0:T(8,128)(2,1)S(1)} collective-permute-done((bf16[2,4,128,256]{3,2,1,0:T(8,128)(2,1)S(1)}, bf16[2,4,128,256]{3,2,1,0:T(8,128)(2,1)S(1)}, u32[]{:S(2)}, u32[]{:S(2)}) %collective-permute-start.2) | collective-permute-done | bytes 524320 | tf_op jit(solution)/shard_map/ppermute | solution.py:315
  44.0 4.8 %shard_map.75 = (f32[4,256,256]{2,1,0:T(8,128)S(1)}, bf16[4,2,128,256]{3,2,1,0:T(8,128)(2,1)S(1)}) custom-call(bf16[4,2,128,256]{3,2,1,0:T(8,128)(2,1)S(1)} %copy.13.own_ref, bf16[2,2,4,128,256]{4,3,2,1,0:T(8,128)(2,1)S(1)} %pad_maximum_fusion.1.rows_ref, bf16[2,4,128,256]{3,2,1,0:T(8,128)(2,1)S(1)} %collective-permute-done.2.time_ref, ...), custom_call_target="tpu_custom_call" | custom-call | flops 3623878656 | bytes 7208960 | tf_op jit(solution)/shard_map/pallas_call | solution.py:222
  48.9 4.9 %shard_map.76.own_ref.grad_ref = bf16[4,2,128,256]{3,2,1,0:T(8,128)(2,1)S(1)} custom-call(bf16[4,2,128,256]{3,2,1,0:T(8,128)(2,1)S(1)} %copy-done, bf16[2,2,4,128,256]{4,3,2,1,0:T(8,128)(2,1)S(1)} %pad_maximum_fusion.1.rows_ref, bf16[2,4,128,256]{3,2,1,0:T(8,128)(2,1)S(1)} %collective-permute-done.3.time_ref, bf16[9,3,256,256]{3,2,1,0:T(8,128)(2,1)S(1)} %bitcast.78, ...), custom_call_target="tpu_custom_call" | custom-call | flops 3623878656 | bytes 7208960 | tf_op jit(solution)/shard_map/pallas_call | solution.py:222
  53.8 5.0 %shard_map.80 = (f32[16,2,27,8,128]{4,3,2,1,0:T(8,128)S(1)}, bf16[16,2,27,8,128]{4,3,2,1,0:T(8,128)(2,1)S(1)}) custom-call(s32[1]{0:T(128)} %bitcast.28.core_ref, bf16[4,2,128,256]{3,2,1,0:T(8,128)(2,1)S(1)} %shard_map.76.own_ref.grad_ref, bf16[4,2,128,256]{3,2,1,0:T(8,128)(2,1)S(1)} %copy.13.own_ref, ...), custom_call_target="tpu_custom_call" | custom-call | flops 3623878656 | bytes 7929860 | tf_op jit(solution)/shard_map/pallas_call | solution.py:222
  58.8 5.6 %shard_map.79 = (f32[16,2,27,8,128]{4,3,2,1,0:T(8,128)S(1)}, bf16[16,2,27,8,128]{4,3,2,1,0:T(8,128)(2,1)S(1)}) custom-call(s32[1]{0:T(128)} %bitcast.28.core_ref, bf16[4,2,128,256]{3,2,1,0:T(8,128)(2,1)S(1)} %get-tuple-element.12.own_ref.active_ref, bf16[4,2,128,256]{3,2,1,0:T(8,128)(2,1)S(1)} %copy-done, ...), custom_call_target="tpu_custom_call" | custom-call | flops 3623878656 | bytes 7929860 | tf_op jit(solution)/shard_map/pallas_call | solution.py:222
  65.4 2.9 %collective-permute-done.8 = bf16[16,2,27,8,128]{4,3,2,1,0:T(8,128)(2,1)S(1)} collective-permute-done((bf16[16,2,27,8,128]{4,3,2,1,0:T(8,128)(2,1)S(1)}, bf16[16,2,27,8,128]{4,3,2,1,0:T(8,128)(2,1)S(1)}, u32[]{:S(2)}, u32[]{:S(2)}) %collective-permute-start.8) | collective-permute-done | bytes 1769504 | tf_op jit(solution)/shard_map/ppermute | solution.py:366
  69.0 26.8 %all_to_all.20.parts_ref = bf16[4,16,27,8,128]{4,3,2,1,0:T(8,128)(2,1)S(1)} all-to-all(bf16[4,16,27,8,128]{4,3,2,1,0:T(8,128)(2,1)S(1)} %bitcast.82), channel_id=1, replica_groups={{0,1,2,3},{4,5,6,7},{8,9,10,11},{12,13,14,15},{16,17,18,19},{20,21,22,2..., dimensions={0} | all-to-all | bytes 7077888 | tf_op jit(solution)/shard_map/all_to_all | solution.py:309
  96.3 15.6 %all_to_all.21 = bf16[16,27,8,128]{3,2,1,0:T(8,128)(2,1)S(1)} all-to-all(bf16[16,27,8,128]{3,2,1,0:T(8,128)(2,1)S(1)} %bitcast.77), channel_id=1, replica_groups={{0,4,8,12,16,20,24,28,64,68,72,76,80,84,88,92},{1,5,9,13,17,21,25,29,65..., dimensions={0} | all-to-all | bytes 1769472 | tf_op jit(solution)/shard_map/all_to_all | solution.py:309
  112.1 17.2 %all_to_all.22 = bf16[16,27,8,128]{3,2,1,0:T(8,128)(2,1)S(1)} all-to-all(bf16[16,27,8,128]{3,2,1,0:T(8,128)(2,1)S(1)} %bitcast.76), channel_id=1, replica_groups={{0,4,8,12,16,20,24,28,64,68,72,76,80,84,88,92},{1,5,9,13,17,21,25,29,65..., dimensions={0} | all-to-all | bytes 1769472 | tf_op jit(solution)/shard_map/all_to_all | solution.py:309
  129.8 27.2 %all_to_all.23 = bf16[4,16,27,8,128]{4,3,2,1,0:T(8,128)(2,1)S(1)} all-to-all(bf16[4,16,27,8,128]{4,3,2,1,0:T(8,128)(2,1)S(1)} %broadcast_in_dim.10), channel_id=1, replica_groups={{0,1,2,3},{4,5,6,7},{8,9,10,11},{12,13,14,15},{16,17,18,19},{20,21,22,2..., dimensions={0} | all-to-all | bytes 7077888 | tf_op jit(solution)/shard_map/all_to_all | solution.py:309
  157.1 5.5 %collective-permute-start.5 = (bf16[2,4,128,256]{3,2,1,0:T(8,128)(2,1)S(1)}, bf16[2,4,128,256]{3,2,1,0:T(8,128)(2,1)S(1)}, u32[]{:S(2)}, u32[]{:S(2)}) collective-permute-start(bf16[2,4,128,256]{3,2,1,0:T(8,128)(2,1)S(1)} %pad_maximum_fusion.8), channel_id=1, source_target_pairs={{1,0},{2,1},{3,2},{4,3},{5,4},{6,5},{7,6},{8,7},{9,8},{10,9},{11,1... | collective-permute-start | bytes 1572872 | tf_op jit(solution)/shard_map/ppermute | solution.py:315
  162.7 2.1 collective-permute-start.4
  164.8 9.7 %collective-permute-done.5 = bf16[2,4,128,256]{3,2,1,0:T(8,128)(2,1)S(1)} collective-permute-done((bf16[2,4,128,256]{3,2,1,0:T(8,128)(2,1)S(1)}, bf16[2,4,128,256]{3,2,1,0:T(8,128)(2,1)S(1)}, u32[]{:S(2)}, u32[]{:S(2)}) %collective-permute-start.5) | collective-permute-done | bytes 524320 | tf_op jit(solution)/shard_map/ppermute | solution.py:315
  174.5 10.0 %collective-permute-done.4 = bf16[2,4,128,256]{3,2,1,0:T(8,128)(2,1)S(1)} collective-permute-done((bf16[2,4,128,256]{3,2,1,0:T(8,128)(2,1)S(1)}, bf16[2,4,128,256]{3,2,1,0:T(8,128)(2,1)S(1)}, u32[]{:S(2)}, u32[]{:S(2)}) %collective-permute-start.4) | collective-permute-done | bytes 524320 | tf_op jit(solution)/shard_map/ppermute | solution.py:315
  184.6 2.1 collective-permute-start.6
  186.8 3.6 %collective-permute-start.7 = (bf16[2,4,128,256]{3,2,1,0:T(8,128)(2,1)S(1)}, bf16[2,4,128,256]{3,2,1,0:T(8,128)(2,1)S(1)}, u32[]{:S(2)}, u32[]{:S(2)}) collective-permute-start(bf16[2,4,128,256]{3,2,1,0:T(8,128)(2,1)S(1)} %pad_maximum_fusion.10), channel_id=1, source_target_pairs={{32,0},{64,32},{96,64},{33,1},{65,33},{97,65},{34,2},{66,34},{98,6... | collective-permute-start | bytes 1572872 | tf_op jit(solution)/shard_map/ppermute | solution.py:315
  190.6 4.5 %collective-permute-done.6.time_ref = bf16[2,4,128,256]{3,2,1,0:T(8,128)(2,1)S(1)} collective-permute-done((bf16[2,4,128,256]{3,2,1,0:T(8,128)(2,1)S(1)}, bf16[2,4,128,256]{3,2,1,0:T(8,128)(2,1)S(1)}, u32[]{:S(2)}, u32[]{:S(2)}) %collective-permute-start.6) | collective-permute-done | bytes 524320 | tf_op jit(solution)/shard_map/ppermute | solution.py:315
  195.1 5.5 %shard_map.77 = bf16[4,2,128,256]{3,2,1,0:T(8,128)(2,1)} custom-call(bf16[4,2,128,256]{3,2,1,0:T(8,128)(2,1)S(1)} %get-tuple-element.12.own_ref.active_ref, bf16[2,2,4,128,256]{4,3,2,1,0:T(8,128)(2,1)S(1)} %pad_maximum_fusion.2.rows_ref, bf16[2,4,128,256]{3,2,1,0:T(8,128)(2,1)S(1)} %collective-permute-done.6.time_ref, bf16[9,3,256,256]{3,2,1,0:T(8,128)(2,1)S(1)} %bitcast.79, ...), custom_call_target="tpu_custom_call" | custom-call | flops 3623878656 | bytes 6684672 | tf_op jit(solution)/shard_map/pallas_call | solution.py:222
  200.7 5.8 %shard_map.78 = bf16[4,2,128,256]{3,2,1,0:T(8,128)(2,1)} custom-call(bf16[4,2,128,256]{3,2,1,0:T(8,128)(2,1)S(1)} %shard_map.76.own_ref.grad_ref, bf16[2,2,4,128,256]{4,3,2,1,0:T(8,128)(2,1)S(1)} %pad_maximum_fusion.2.rows_ref, bf16[2,4,128,256]{3,2,1,0:T(8,128)(2,1)S(1)} %collective-permute-done.7.time_ref, bf16[9,3,256,256]{3,2,1,0:T(8,128)(2,1)S(1)} %bitcast.81, ...), custom_call_target="tpu_custom_call" | custom-call | flops 3623878656 | bytes 7208960 | tf_op jit(solution)/shard_map/pallas_call | solution.py:222
  206.5 6.6 %assemble.1 = (f32[27,256,256]{2,1,0:T(8,128)}, f32[27,256,256]{2,1,0:T(8,128)}) custom-call(s32[1]{0:T(128)} %bitcast.28.core_ref, bf16[2,16,2,27,8,128]{5,4,3,2,1,0:T(8,128)(2,1)S(1)} %bitcast.71, bf16[2,16,2,27,8,128]{5,4,3,2,1,0:T(8,128)(2,1)S(1)} %bitcast.72, bf16[2,16,2,27,8,128]{5,4,3,2,1,0:T(8,128)(2,1)S(1)} %bitcast.73, ...), custom_call_target="tpu_custom_call" | custom-call | flops 16777216 | bytes 29360128 | tf_op jit(solution)/shard_map/assemble/pallas_call | solution.py:266
  (49 shorter events, 12.9 us)
Async XLA Ops:
  2.0 31.5 %slice-start = ((bf16[4,2,128,256]{3,2,1,0:T(8,128)(2,1)}), bf16[2,2,128,256]{3,2,1,0:T(8,128)(2,1)S(1)}, s32[]{:S(2)}) async-start(bf16[4,2,128,256]{3,2,1,0:T(8,128)(2,1)} %own_ref.3), calls=%async_computation.4 | async-start | bytes 524288 | tf_op jit(solution)/shard_map/slice | solution.py:329
  3.2 18.3 %collective-permute-start.1 = (bf16[2,4,128,256]{3,2,1,0:T(8,128)(2,1)S(1)}, bf16[2,4,128,256]{3,2,1,0:T(8,128)(2,1)S(1)}, u32[]{:S(2)}, u32[]{:S(2)}) collective-permute-start(bf16[2,4,128,256]{3,2,1,0:T(8,128)(2,1)S(1)} %pad_maximum_fusion.4), channel_id=1, source_target_pairs={{1,0},{2,1},{3,2},{4,3},{5,4},{6,5},{7,6},{8,7},{9,8},{10,9},{11,1... | collective-permute-start | bytes 1572872 | tf_op jit(solution)/shard_map/ppermute | solution.py:315
  10.4 21.1 %collective-permute-start = (bf16[2,4,128,256]{3,2,1,0:T(8,128)(2,1)S(1)}, bf16[2,4,128,256]{3,2,1,0:T(8,128)(2,1)S(1)}, u32[]{:S(2)}, u32[]{:S(2)}) collective-permute-start(bf16[2,4,128,256]{3,2,1,0:T(8,128)(2,1)S(1)} %pad_maximum_fusion.3), channel_id=1, source_target_pairs={{0,1},{1,2},{2,3},{3,4},{4,5},{5,6},{6,7},{7,8},{8,9},{9,10},{10,1... | collective-permute-start | bytes 1572872 | tf_op jit(solution)/shard_map/ppermute | solution.py:315
  31.5 10.5 %collective-permute-start.2 = (bf16[2,4,128,256]{3,2,1,0:T(8,128)(2,1)S(1)}, bf16[2,4,128,256]{3,2,1,0:T(8,128)(2,1)S(1)}, u32[]{:S(2)}, u32[]{:S(2)}) collective-permute-start(bf16[2,4,128,256]{3,2,1,0:T(8,128)(2,1)S(1)} %pad_maximum_fusion.5), channel_id=1, source_target_pairs={{0,32},{32,64},{64,96},{1,33},{33,65},{65,97},{2,34},{34,66},{66,9... | collective-permute-start | bytes 1572872 | tf_op jit(solution)/shard_map/ppermute | solution.py:315
  34.3 14.5 %collective-permute-start.3 = (bf16[2,4,128,256]{3,2,1,0:T(8,128)(2,1)}, bf16[2,4,128,256]{3,2,1,0:T(8,128)(2,1)S(1)}, u32[]{:S(2)}, u32[]{:S(2)}) collective-permute-start(bf16[2,4,128,256]{3,2,1,0:T(8,128)(2,1)} %pad_maximum_fusion.6), channel_id=1, source_target_pairs={{32,0},{64,32},{96,64},{33,1},{65,33},{97,65},{34,2},{66,34},{98,6... | collective-permute-start | bytes 1572872 | tf_op jit(solution)/shard_map/ppermute | solution.py:315
  42.0 2.0 copy-start.3
  44.0 4.8 %copy-start = (bf16[4,2,128,256]{3,2,1,0:T(8,128)(2,1)S(1)}, bf16[4,2,128,256]{3,2,1,0:T(8,128)(2,1)}, u32[]{:S(2)}) copy-start(bf16[4,2,128,256]{3,2,1,0:T(8,128)(2,1)} %own_ref.3) | copy-start | bytes 1572868
  44.0 4.8 %copy-start.2 = (bf16[3,3,3,256,256]{4,3,2,1,0:T(8,128)(2,1)S(1)}, bf16[3,3,3,256,256]{4,3,2,1,0:T(8,128)(2,1)}, u32[]{:S(2)}) copy-start(bf16[3,3,3,256,256]{4,3,2,1,0:T(8,128)(2,1)} %param.6) | copy-start | bytes 10616836
  58.7 6.2 %collective-permute-start.9 = (bf16[16,2,27,8,128]{4,3,2,1,0:T(8,128)(2,1)S(1)}, bf16[16,2,27,8,128]{4,3,2,1,0:T(8,128)(2,1)S(1)}, u32[]{:S(2)}, u32[]{:S(2)}) collective-permute-start(bf16[16,2,27,8,128]{4,3,2,1,0:T(8,128)(2,1)S(1)} %get-tuple-element.17), channel_id=1, source_target_pairs={{0,32},{32,0},{1,33},{33,1},{2,34},{34,2},{3,35},{35,3},{4,36},{36... | collective-permute-start | bytes 5308424 | tf_op jit(solution)/shard_map/ppermute | solution.py:367
  64.4 3.9 %collective-permute-start.8 = (bf16[16,2,27,8,128]{4,3,2,1,0:T(8,128)(2,1)S(1)}, bf16[16,2,27,8,128]{4,3,2,1,0:T(8,128)(2,1)S(1)}, u32[]{:S(2)}, u32[]{:S(2)}) collective-permute-start(bf16[16,2,27,8,128]{4,3,2,1,0:T(8,128)(2,1)S(1)} %get-tuple-element.15), channel_id=1, source_target_pairs={{0,32},{32,0},{1,33},{33,1},{2,34},{34,2},{3,35},{35,3},{4,36},{36... | collective-permute-start | bytes 5308424 | tf_op jit(solution)/shard_map/ppermute | solution.py:366
  156.9 49.5 %collective-permute-start.10 = (bf16[4,16,27,8,128]{4,3,2,1,0:T(8,128)(2,1)S(1)}, bf16[4,16,27,8,128]{4,3,2,1,0:T(8,128)(2,1)S(1)}, u32[]{:S(2)}, u32[]{:S(2)}) collective-permute-start(bf16[4,16,27,8,128]{4,3,2,1,0:T(8,128)(2,1)S(1)} %all_to_all.23), channel_id=1, source_target_pairs={{0,32},{32,0},{1,33},{33,1},{2,34},{34,2},{3,35},{35,3},{4,36},{36... | collective-permute-start | bytes 10616840 | tf_op jit(solution)/shard_map/ppermute | solution.py:378
  157.1 17.4 %collective-permute-start.5 = (bf16[2,4,128,256]{3,2,1,0:T(8,128)(2,1)S(1)}, bf16[2,4,128,256]{3,2,1,0:T(8,128)(2,1)S(1)}, u32[]{:S(2)}, u32[]{:S(2)}) collective-permute-start(bf16[2,4,128,256]{3,2,1,0:T(8,128)(2,1)S(1)} %pad_maximum_fusion.8), channel_id=1, source_target_pairs={{1,0},{2,1},{3,2},{4,3},{5,4},{6,5},{7,6},{8,7},{9,8},{10,9},{11,1... | collective-permute-start | bytes 1572872 | tf_op jit(solution)/shard_map/ppermute | solution.py:315
  162.6 32.5 %copy-start.1 = (bf16[4,2,128,256]{3,2,1,0:T(8,128)(2,1)S(1)}, bf16[4,2,128,256]{3,2,1,0:T(8,128)(2,1)}, u32[]{:S(2)}) copy-start(bf16[4,2,128,256]{3,2,1,0:T(8,128)(2,1)} %latents_ref.3) | copy-start | bytes 1572868
  162.7 21.8 %collective-permute-start.4 = (bf16[2,4,128,256]{3,2,1,0:T(8,128)(2,1)S(1)}, bf16[2,4,128,256]{3,2,1,0:T(8,128)(2,1)S(1)}, u32[]{:S(2)}, u32[]{:S(2)}) collective-permute-start(bf16[2,4,128,256]{3,2,1,0:T(8,128)(2,1)S(1)} %pad_maximum_fusion.7), channel_id=1, source_target_pairs={{0,1},{1,2},{2,3},{3,4},{4,5},{5,6},{6,7},{7,8},{8,9},{9,10},{10,1... | collective-permute-start | bytes 1572872 | tf_op jit(solution)/shard_map/ppermute | solution.py:315
  184.6 10.5 %collective-permute-start.6 = (bf16[2,4,128,256]{3,2,1,0:T(8,128)(2,1)S(1)}, bf16[2,4,128,256]{3,2,1,0:T(8,128)(2,1)S(1)}, u32[]{:S(2)}, u32[]{:S(2)}) collective-permute-start(bf16[2,4,128,256]{3,2,1,0:T(8,128)(2,1)S(1)} %pad_maximum_fusion.9), channel_id=1, source_target_pairs={{0,32},{32,64},{64,96},{1,33},{33,65},{65,97},{2,34},{34,66},{66,9... | collective-permute-start | bytes 1572872 | tf_op jit(solution)/shard_map/ppermute | solution.py:315
  186.8 13.8 %collective-permute-start.7 = (bf16[2,4,128,256]{3,2,1,0:T(8,128)(2,1)S(1)}, bf16[2,4,128,256]{3,2,1,0:T(8,128)(2,1)S(1)}, u32[]{:S(2)}, u32[]{:S(2)}) collective-permute-start(bf16[2,4,128,256]{3,2,1,0:T(8,128)(2,1)S(1)} %pad_maximum_fusion.10), channel_id=1, source_target_pairs={{32,0},{64,32},{96,64},{33,1},{65,33},{97,65},{34,2},{66,34},{98,6... | collective-permute-start | bytes 1572872 | tf_op jit(solution)/shard_map/ppermute | solution.py:315
  190.6 10.1 %copy-start.4 = (bf16[3,3,3,256,256]{4,3,2,1,0:T(8,128)(2,1)S(1)}, bf16[3,3,3,256,256]{4,3,2,1,0:T(8,128)(2,1)}, u32[]{:S(2)}) copy-start(bf16[3,3,3,256,256]{4,3,2,1,0:T(8,128)(2,1)} %param.5) | copy-start | bytes 10616836

commit v4 on v3

--- a/solution.py
+++ b/solution.py
@@ -244,35 +244,35 @@
 STEP = 3
 
 
-def assemble_kernel(core_ref, own2_ref, own1_ref, far2_ref, far1_ref, first_ref, second_ref):
+def assemble_kernel(core_ref, own_ref, far_ref, first_ref, second_ref):
     core = core_ref[0]
+    start = pl.program_id(0) * STEP
     mine = pl.multiple_of(core * 128, 128)
     theirs = pl.multiple_of((1 - core) * 128, 128)
-    for out, own, far in ((second_ref, own2_ref, far2_ref), (first_ref, own1_ref, far1_ref)):
+    for grad, out in ((0, second_ref), (1, first_ref)):
         for p in range(STEP):
             for b in range(2):
                 lanes = slice(b * 128, (b + 1) * 128)
-                out[p, pl.ds(mine, 128), lanes] = own[0, :, b, p].astype(F32).reshape(128, 128)
-                out[p, pl.ds(theirs, 128), lanes] = far[0, :, b, p].astype(F32).reshape(128, 128)
+                for rows, ref in ((mine, own_ref), (theirs, far_ref)):
+                    half = ref[grad, :, b, start + p].astype(F32)
+                    out[p, pl.ds(rows, 128), lanes] = half.reshape(128, 128)
 
 
 def assemble(core, own, far):
     own, far = (v.reshape(2, 16, 2, TAPS, 8, 128) for v in (own, far))
-    block = (1, 16, 2, STEP, 8, 128)
-    second = pl.BlockSpec(block, lambda p: (0, 0, 0, p, 0, 0))
-    first = pl.BlockSpec(block, lambda p: (1, 0, 0, p, 0, 0))
     out = pl.BlockSpec((STEP, C, C), lambda p: (p, 0, 0))
     shape = jax.ShapeDtypeStruct((TAPS, C, C), F32)
+    whole_array = pl.BlockSpec(memory_space=pltpu.VMEM)
     return pl.pallas_call(
         assemble_kernel,
         out_shape=(shape, shape),
         grid=(TAPS // STEP,),
-        in_specs=[pl.BlockSpec(memory_space=pltpu.SMEM), second, first, second, first],
+        in_specs=[pl.BlockSpec(memory_space=pltpu.SMEM), whole_array, whole_array],
         out_specs=(out, out),
-        compiler_params=pltpu.CompilerParams(vmem_limit_bytes=16 << 20),
+        compiler_params=pltpu.CompilerParams(vmem_limit_bytes=24 << 20),
         cost_estimate=cost(1 << 24, 28 << 20),
         name="assemble",
-    )(core, own, own, far, far)
+    )(core, own, far)
 
 
 def total_kernel(parts_ref, out_ref):
@@ -296,13 +296,19 @@
 def stage_groups():
     sizes = [lax.axis_size(axis) for axis in ALL]
     grid = np.arange(math.prod(sizes)).reshape(sizes)
-    near, rest = ([], [])
-    for core, axis in ((0, 3), (1, 2)):
-        chips = np.moveaxis(grid[:, core], axis, -1)
-        lines = chips.reshape(-1, chips.shape[-1])
-        near += lines.tolist()
-        rest += lines.T.tolist()
-    return near, rest
+    stages = []
+    for order in ("xy", "yz", "zx"):
+        groups = []
+        for core, axis in enumerate(order):
+            chips = grid[:, core]
+            chips = {
+                "x": chips,
+                "y": np.moveaxis(chips, 2, -1),
+                "z": np.moveaxis(chips, (0, 1), (-2, -1)),
+            }[axis]
+            groups += chips.reshape(-1, 4).tolist()
+        stages.append(groups)
+    return stages
 
 
 def exchange(value, groups):
@@ -366,15 +372,16 @@
     got2 = lax.ppermute(send2, "co", across)
     got1 = lax.ppermute(send1, "co", across)
     mine = jnp.stack([(keep2 + got2.astype(F32)).astype(BF), (keep1 + got1.astype(F32)).astype(BF)])
-    near, rest = stage_groups()
-    first, second = (len(near[0]), len(rest[0]))
-    block_rows = 64 // (first * second) * TAPS
-    parts = exchange(mine.reshape(first, second, block_rows, 8, 128), near)
-    quarter = total(parts, 1)
-    parts = exchange(quarter.reshape(second, block_rows, 8, 128), rest)
-    spread = total(parts[:, None], second)
-    quarter = exchange(spread.reshape(second, block_rows, 8, 128), rest)
-    own = exchange(jnp.broadcast_to(quarter[None], (first, *quarter.shape)), near)
+    stages = stage_groups()
+    parts = exchange(mine.reshape(4, 16, TAPS, 8, 128), stages[0])
+    held = total(parts, 1)
+    parts = exchange(held.reshape(4, 4, TAPS, 8, 128), stages[1])
+    parts = exchange(total(parts, 1).reshape(4, 1, TAPS, 8, 128), stages[2])
+    held = exchange(total(parts, 4), stages[2])
+    for groups in stages[1::-1]:
+        spread = jnp.broadcast_to(held.reshape(1, -1, TAPS, 8, 128), (4, held.size // (TAPS * 1024), TAPS, 8, 128))
+        held = exchange(spread, groups)
+    own = held
     far = lax.ppermute(own, "co", across)
 
     (decoded,) = convolution(decoded_kernel, (block,))(

time: 214 us -> 222 us (1.037)
  blocking collectives: 86.8 us -> 95.5 us
    all_to_all x4 -> x6, blocking collectives: 86.8 us -> 95.5 us  [exchange(): lax.all_to_all(value, ALL, 0, 0, axis_index_groups=groups, tiled=False)]
    pallas_call x8 -> x9, Pallas kernels: 32.2 us -> 32.2 us  [call(): pl.pallas_call(kernel, out_shape=outs, in_specs=[pl.BlockSpec(memory_spac...]
where the time goes in v4:
time: 222 us; the launch traced here: 221 us
  blocking collectives  95.5 us (43%)
  waiting for transfers between devices  50.2 us (23%)
  Pallas kernels  38.4 us (17%)
  starting transfers between devices  28.2 us (13%)
  local copies, waits for them, and re-layouts  3.96 us (2%)
  other arithmetic  3.9 us (2%)
    all_to_all x6, blocking collectives, exchange(): lax.all_to_all(value, ALL, 0, 0, axis_index_groups=groups, tiled=False)  95.5 us
    ppermute x8, waiting for transfers between devices, swap(): return lax.ppermute(value, axis, pairs)  47.3 us
    pallas_call x9, Pallas kernels, call(): pl.pallas_call(kernel, out_shape=outs, in_specs=[pl.BlockSpec(memory_spac...  32.2 us
    ppermute x8, starting transfers between devices, swap(): return lax.ppermute(value, axis, pairs)  27.6 us
    pallas_call x1, Pallas kernels, assemble(): pl.pallas_call(assemble_kernel, out_shape=(shape, shape), grid=(TAPS // S...  6.22 us
  transfers between devices with their start and end apart: 11, of which 7 were waited for; matrix products, arithmetic and copies ran while one was open for 1% of the time, Pallas kernels for 10%

profile of v4, /device:TPU:96, one launch (start us, length us, event | category | flops | bytes accessed | tf_op | source)
XLA Modules:
  0.0 221.2 jit_solution(13318407677908970061)
XLA Ops:
  3.2 7.1 %collective-permute-start.1 = (bf16[2,4,128,256]{3,2,1,0:T(8,128)(2,1)S(1)}, bf16[2,4,128,256]{3,2,1,0:T(8,128)(2,1)S(1)}, u32[]{:S(2)}, u32[]{:S(2)}) collective-permute-start(bf16[2,4,128,256]{3,2,1,0:T(8,128)(2,1)S(1)} %pad_maximum_fusion.4), channel_id=1, source_target_pairs={{1,0},{2,1},{3,2},{4,3},{5,4},{6,5},{7,6},{8,7},{9,8},{10,9},{11,1... | collective-permute-start | bytes 1572872 | tf_op jit(solution)/shard_map/ppermute | solution.py:321
  12.3 9.2 %collective-permute-done.1 = bf16[2,4,128,256]{3,2,1,0:T(8,128)(2,1)S(1)} collective-permute-done((bf16[2,4,128,256]{3,2,1,0:T(8,128)(2,1)S(1)}, bf16[2,4,128,256]{3,2,1,0:T(8,128)(2,1)S(1)}, u32[]{:S(2)}, u32[]{:S(2)}) %collective-permute-start.1) | collective-permute-done | bytes 524320 | tf_op jit(solution)/shard_map/ppermute | solution.py:321
  21.5 10.0 %collective-permute-done = bf16[2,4,128,256]{3,2,1,0:T(8,128)(2,1)S(1)} collective-permute-done((bf16[2,4,128,256]{3,2,1,0:T(8,128)(2,1)S(1)}, bf16[2,4,128,256]{3,2,1,0:T(8,128)(2,1)S(1)}, u32[]{:S(2)}, u32[]{:S(2)}) %collective-permute-start) | collective-permute-done | bytes 524320 | tf_op jit(solution)/shard_map/ppermute | solution.py:321
  34.3 3.6 %collective-permute-start.3 = (bf16[2,4,128,256]{3,2,1,0:T(8,128)(2,1)}, bf16[2,4,128,256]{3,2,1,0:T(8,128)(2,1)S(1)}, u32[]{:S(2)}, u32[]{:S(2)}) collective-permute-start(bf16[2,4,128,256]{3,2,1,0:T(8,128)(2,1)} %pad_maximum_fusion.6), channel_id=1, source_target_pairs={{32,0},{64,32},{96,64},{33,1},{65,33},{97,65},{34,2},{66,34},{98,6... | collective-permute-start | bytes 1572872 | tf_op jit(solution)/shard_map/ppermute | solution.py:321
  38.1 3.9 %collective-permute-done.2.time_ref = bf16[2,4,128,256]{3,2,1,0:T(8,128)(2,1)S(1)} collective-permute-done((bf16[2,4,128,256]{3,2,1,0:T(8,128)(2,1)S(1)}, bf16[2,4,128,256]{3,2,1,0:T(8,128)(2,1)S(1)}, u32[]{:S(2)}, u32[]{:S(2)}) %collective-permute-start.2) | collective-permute-done | bytes 524320 | tf_op jit(solution)/shard_map/ppermute | solution.py:321
  44.0 4.8 %shard_map.75 = (f32[4,256,256]{2,1,0:T(8,128)S(1)}, bf16[4,2,128,256]{3,2,1,0:T(8,128)(2,1)S(1)}) custom-call(bf16[4,2,128,256]{3,2,1,0:T(8,128)(2,1)S(1)} %copy.13.own_ref, bf16[2,2,4,128,256]{4,3,2,1,0:T(8,128)(2,1)S(1)} %pad_maximum_fusion.1.rows_ref, bf16[2,4,128,256]{3,2,1,0:T(8,128)(2,1)S(1)} %collective-permute-done.2.time_ref, ...), custom_call_target="tpu_custom_call" | custom-call | flops 3623878656 | bytes 7208960 | tf_op jit(solution)/shard_map/pallas_call | solution.py:222
  48.9 4.9 %shard_map.76.own_ref.grad_ref = bf16[4,2,128,256]{3,2,1,0:T(8,128)(2,1)S(1)} custom-call(bf16[4,2,128,256]{3,2,1,0:T(8,128)(2,1)S(1)} %copy-done, bf16[2,2,4,128,256]{4,3,2,1,0:T(8,128)(2,1)S(1)} %pad_maximum_fusion.1.rows_ref, bf16[2,4,128,256]{3,2,1,0:T(8,128)(2,1)S(1)} %collective-permute-done.3.time_ref, bf16[9,3,256,256]{3,2,1,0:T(8,128)(2,1)S(1)} %bitcast.76, ...), custom_call_target="tpu_custom_call" | custom-call | flops 3623878656 | bytes 7208960 | tf_op jit(solution)/shard_map/pallas_call | solution.py:222
  53.8 5.0 %shard_map.80 = (f32[16,2,27,8,128]{4,3,2,1,0:T(8,128)S(1)}, bf16[16,2,27,8,128]{4,3,2,1,0:T(8,128)(2,1)S(1)}) custom-call(s32[1]{0:T(128)} %bitcast.28.core_ref, bf16[4,2,128,256]{3,2,1,0:T(8,128)(2,1)S(1)} %shard_map.76.own_ref.grad_ref, bf16[4,2,128,256]{3,2,1,0:T(8,128)(2,1)S(1)} %copy.13.own_ref, ...), custom_call_target="tpu_custom_call" | custom-call | flops 3623878656 | bytes 7929860 | tf_op jit(solution)/shard_map/pallas_call | solution.py:222
  58.8 5.6 %shard_map.79 = (f32[16,2,27,8,128]{4,3,2,1,0:T(8,128)S(1)}, bf16[16,2,27,8,128]{4,3,2,1,0:T(8,128)(2,1)S(1)}) custom-call(s32[1]{0:T(128)} %bitcast.28.core_ref, bf16[4,2,128,256]{3,2,1,0:T(8,128)(2,1)S(1)} %get-tuple-element.12.own_ref.active_ref, bf16[4,2,128,256]{3,2,1,0:T(8,128)(2,1)S(1)} %copy-done, ...), custom_call_target="tpu_custom_call" | custom-call | flops 3623878656 | bytes 7929860 | tf_op jit(solution)/shard_map/pallas_call | solution.py:222
  65.4 2.9 %collective-permute-done.8 = bf16[16,2,27,8,128]{4,3,2,1,0:T(8,128)(2,1)S(1)} collective-permute-done((bf16[16,2,27,8,128]{4,3,2,1,0:T(8,128)(2,1)S(1)}, bf16[16,2,27,8,128]{4,3,2,1,0:T(8,128)(2,1)S(1)}, u32[]{:S(2)}, u32[]{:S(2)}) %collective-permute-start.8) | collective-permute-done | bytes 1769504 | tf_op jit(solution)/shard_map/ppermute | solution.py:372
  69.0 26.8 %all_to_all.30.parts_ref = bf16[4,16,27,8,128]{4,3,2,1,0:T(8,128)(2,1)S(1)} all-to-all(bf16[4,16,27,8,128]{4,3,2,1,0:T(8,128)(2,1)S(1)} %bitcast.80), channel_id=1, replica_groups={{0,1,2,3},{4,5,6,7},{8,9,10,11},{12,13,14,15},{16,17,18,19},{20,21,22,2..., dimensions={0} | all-to-all | bytes 7077888 | tf_op jit(solution)/shard_map/all_to_all | solution.py:315
  96.3 12.4 %all_to_all.31.parts_ref = bf16[4,4,27,8,128]{4,3,2,1,0:T(8,128)(2,1)S(1)} all-to-all(bf16[4,4,27,8,128]{4,3,2,1,0:T(8,128)(2,1)S(1)} %bitcast.74), channel_id=1, replica_groups={{0,4,8,12},{1,5,9,13},{2,6,10,14},{3,7,11,15},{16,20,24,28},{17,21,25,2..., dimensions={0} | all-to-all | bytes 1769472 | tf_op jit(solution)/shard_map/all_to_all | solution.py:315
  108.9 8.5 %all_to_all.32.parts_ref = bf16[4,1,27,8,128]{4,3,2,1,0:T(8,128)(2,1)S(1)} all-to-all(bf16[4,1,27,8,128]{4,3,2,1,0:T(8,128)(2,1)S(1)} %bitcast.75), channel_id=1, replica_groups={{0,16,64,80},{1,17,65,81},{2,18,66,82},{3,19,67,83},{4,20,68,84},{5,21,..., dimensions={0} | all-to-all | bytes 442368 | tf_op jit(solution)/shard_map/all_to_all | solution.py:315
  117.4 8.7 %all_to_all.33 = bf16[4,1,27,8,128]{4,3,2,1,0:T(8,128)(2,1)S(1)} all-to-all(bf16[4,1,27,8,128]{4,3,2,1,0:T(8,128)(2,1)S(1)} %shard_map.83), channel_id=1, replica_groups={{0,16,64,80},{1,17,65,81},{2,18,66,82},{3,19,67,83},{4,20,68,84},{5,21,..., dimensions={0} | all-to-all | bytes 442368 | tf_op jit(solution)/shard_map/all_to_all | solution.py:315
  126.2 12.4 %all_to_all.34 = bf16[4,4,27,8,128]{4,3,2,1,0:T(8,128)(2,1)S(1)} all-to-all(bf16[4,4,27,8,128]{4,3,2,1,0:T(8,128)(2,1)S(1)} %broadcast_in_dim.15), channel_id=1, replica_groups={{0,4,8,12},{1,5,9,13},{2,6,10,14},{3,7,11,15},{16,20,24,28},{17,21,25,2..., dimensions={0} | all-to-all | bytes 1769472 | tf_op jit(solution)/shard_map/all_to_all | solution.py:315
  139.1 26.8 %all_to_all.35 = bf16[4,16,27,8,128]{4,3,2,1,0:T(8,128)(2,1)S(1)} all-to-all(bf16[4,16,27,8,128]{4,3,2,1,0:T(8,128)(2,1)S(1)} %broadcast_in_dim.17), channel_id=1, replica_groups={{0,1,2,3},{4,5,6,7},{8,9,10,11},{12,13,14,15},{16,17,18,19},{20,21,22,2..., dimensions={0} | all-to-all | bytes 7077888 | tf_op jit(solution)/shard_map/all_to_all | solution.py:315
  166.0 5.2 %collective-permute-start.5 = (bf16[2,4,128,256]{3,2,1,0:T(8,128)(2,1)S(1)}, bf16[2,4,128,256]{3,2,1,0:T(8,128)(2,1)S(1)}, u32[]{:S(2)}, u32[]{:S(2)}) collective-permute-start(bf16[2,4,128,256]{3,2,1,0:T(8,128)(2,1)S(1)} %pad_maximum_fusion.8), channel_id=1, source_target_pairs={{1,0},{2,1},{3,2},{4,3},{5,4},{6,5},{7,6},{8,7},{9,8},{10,9},{11,1... | collective-permute-start | bytes 1572872 | tf_op jit(solution)/shard_map/ppermute | solution.py:321
  173.3 9.7 %collective-permute-done.5 = bf16[2,4,128,256]{3,2,1,0:T(8,128)(2,1)S(1)} collective-permute-done((bf16[2,4,128,256]{3,2,1,0:T(8,128)(2,1)S(1)}, bf16[2,4,128,256]{3,2,1,0:T(8,128)(2,1)S(1)}, u32[]{:S(2)}, u32[]{:S(2)}) %collective-permute-start.5) | collective-permute-done | bytes 524320 | tf_op jit(solution)/shard_map/ppermute | solution.py:321
  183.0 10.0 %collective-permute-done.4 = bf16[2,4,128,256]{3,2,1,0:T(8,128)(2,1)S(1)} collective-permute-done((bf16[2,4,128,256]{3,2,1,0:T(8,128)(2,1)S(1)}, bf16[2,4,128,256]{3,2,1,0:T(8,128)(2,1)S(1)}, u32[]{:S(2)}, u32[]{:S(2)}) %collective-permute-start.4) | collective-permute-done | bytes 524320 | tf_op jit(solution)/shard_map/ppermute | solution.py:321
  195.4 3.6 %collective-permute-start.7 = (bf16[2,4,128,256]{3,2,1,0:T(8,128)(2,1)S(1)}, bf16[2,4,128,256]{3,2,1,0:T(8,128)(2,1)S(1)}, u32[]{:S(2)}, u32[]{:S(2)}) collective-permute-start(bf16[2,4,128,256]{3,2,1,0:T(8,128)(2,1)S(1)} %pad_maximum_fusion.10), channel_id=1, source_target_pairs={{32,0},{64,32},{96,64},{33,1},{65,33},{97,65},{34,2},{66,34},{98,6... | collective-permute-start | bytes 1572872 | tf_op jit(solution)/shard_map/ppermute | solution.py:321
  199.1 4.5 %collective-permute-done.6.time_ref = bf16[2,4,128,256]{3,2,1,0:T(8,128)(2,1)S(1)} collective-permute-done((bf16[2,4,128,256]{3,2,1,0:T(8,128)(2,1)S(1)}, bf16[2,4,128,256]{3,2,1,0:T(8,128)(2,1)S(1)}, u32[]{:S(2)}, u32[]{:S(2)}) %collective-permute-start.6) | collective-permute-done | bytes 524320 | tf_op jit(solution)/shard_map/ppermute | solution.py:321
  203.6 5.5 %shard_map.77 = bf16[4,2,128,256]{3,2,1,0:T(8,128)(2,1)} custom-call(bf16[4,2,128,256]{3,2,1,0:T(8,128)(2,1)S(1)} %get-tuple-element.12.own_ref.active_ref, bf16[2,2,4,128,256]{4,3,2,1,0:T(8,128)(2,1)S(1)} %pad_maximum_fusion.2.rows_ref, bf16[2,4,128,256]{3,2,1,0:T(8,128)(2,1)S(1)} %collective-permute-done.6.time_ref, bf16[9,3,256,256]{3,2,1,0:T(8,128)(2,1)S(1)} %bitcast.77, ...), custom_call_target="tpu_custom_call" | custom-call | flops 3623878656 | bytes 6684672 | tf_op jit(solution)/shard_map/pallas_call | solution.py:222
  209.2 5.8 %shard_map.78 = bf16[4,2,128,256]{3,2,1,0:T(8,128)(2,1)} custom-call(bf16[4,2,128,256]{3,2,1,0:T(8,128)(2,1)S(1)} %shard_map.76.own_ref.grad_ref, bf16[2,2,4,128,256]{4,3,2,1,0:T(8,128)(2,1)S(1)} %pad_maximum_fusion.2.rows_ref, bf16[2,4,128,256]{3,2,1,0:T(8,128)(2,1)S(1)} %collective-permute-done.7.time_ref, bf16[9,3,256,256]{3,2,1,0:T(8,128)(2,1)S(1)} %bitcast.79, ...), custom_call_target="tpu_custom_call" | custom-call | flops 3623878656 | bytes 7208960 | tf_op jit(solution)/shard_map/pallas_call | solution.py:222
  215.0 6.2 %assemble.1 = (f32[27,256,256]{2,1,0:T(8,128)}, f32[27,256,256]{2,1,0:T(8,128)}) custom-call(s32[1]{0:T(128)} %bitcast.28.core_ref, bf16[2,16,2,27,8,128]{5,4,3,2,1,0:T(8,128)(2,1)S(1)} %bitcast.72, bf16[2,16,2,27,8,128]{5,4,3,2,1,0:T(8,128)(2,1)S(1)} %bitcast.73), custom_call_target="tpu_custom_call" | custom-call | flops 16777216 | bytes 29360128 | tf_op jit(solution)/shard_map/assemble/pallas_call | solution.py:266
  (53 shorter events, 17.2 us)
Async XLA Ops:
  2.0 31.5 %slice-start = ((bf16[4,2,128,256]{3,2,1,0:T(8,128)(2,1)}), bf16[2,2,128,256]{3,2,1,0:T(8,128)(2,1)S(1)}, s32[]{:S(2)}) async-start(bf16[4,2,128,256]{3,2,1,0:T(8,128)(2,1)} %own_ref.3), calls=%async_computation.6 | async-start | bytes 524288 | tf_op jit(solution)/shard_map/slice | solution.py:335
  3.2 18.3 %collective-permute-start.1 = (bf16[2,4,128,256]{3,2,1,0:T(8,128)(2,1)S(1)}, bf16[2,4,128,256]{3,2,1,0:T(8,128)(2,1)S(1)}, u32[]{:S(2)}, u32[]{:S(2)}) collective-permute-start(bf16[2,4,128,256]{3,2,1,0:T(8,128)(2,1)S(1)} %pad_maximum_fusion.4), channel_id=1, source_target_pairs={{1,0},{2,1},{3,2},{4,3},{5,4},{6,5},{7,6},{8,7},{9,8},{10,9},{11,1... | collective-permute-start | bytes 1572872 | tf_op jit(solution)/shard_map/ppermute | solution.py:321
  10.4 21.1 %collective-permute-start = (bf16[2,4,128,256]{3,2,1,0:T(8,128)(2,1)S(1)}, bf16[2,4,128,256]{3,2,1,0:T(8,128)(2,1)S(1)}, u32[]{:S(2)}, u32[]{:S(2)}) collective-permute-start(bf16[2,4,128,256]{3,2,1,0:T(8,128)(2,1)S(1)} %pad_maximum_fusion.3), channel_id=1, source_target_pairs={{0,1},{1,2},{2,3},{3,4},{4,5},{5,6},{6,7},{7,8},{8,9},{9,10},{10,1... | collective-permute-start | bytes 1572872 | tf_op jit(solution)/shard_map/ppermute | solution.py:321
  31.5 10.5 %collective-permute-start.2 = (bf16[2,4,128,256]{3,2,1,0:T(8,128)(2,1)S(1)}, bf16[2,4,128,256]{3,2,1,0:T(8,128)(2,1)S(1)}, u32[]{:S(2)}, u32[]{:S(2)}) collective-permute-start(bf16[2,4,128,256]{3,2,1,0:T(8,128)(2,1)S(1)} %pad_maximum_fusion.5), channel_id=1, source_target_pairs={{0,32},{32,64},{64,96},{1,33},{33,65},{65,97},{2,34},{34,66},{66,9... | collective-permute-start | bytes 1572872 | tf_op jit(solution)/shard_map/ppermute | solution.py:321
  34.3 14.5 %collective-permute-start.3 = (bf16[2,4,128,256]{3,2,1,0:T(8,128)(2,1)}, bf16[2,4,128,256]{3,2,1,0:T(8,128)(2,1)S(1)}, u32[]{:S(2)}, u32[]{:S(2)}) collective-permute-start(bf16[2,4,128,256]{3,2,1,0:T(8,128)(2,1)} %pad_maximum_fusion.6), channel_id=1, source_target_pairs={{32,0},{64,32},{96,64},{33,1},{65,33},{97,65},{34,2},{66,34},{98,6... | collective-permute-start | bytes 1572872 | tf_op jit(solution)/shard_map/ppermute | solution.py:321
  42.0 2.0 copy-start.3
  44.0 4.8 %copy-start = (bf16[4,2,128,256]{3,2,1,0:T(8,128)(2,1)S(1)}, bf16[4,2,128,256]{3,2,1,0:T(8,128)(2,1)}, u32[]{:S(2)}) copy-start(bf16[4,2,128,256]{3,2,1,0:T(8,128)(2,1)} %own_ref.3) | copy-start | bytes 1572868
  44.0 4.8 %copy-start.2 = (bf16[3,3,3,256,256]{4,3,2,1,0:T(8,128)(2,1)S(1)}, bf16[3,3,3,256,256]{4,3,2,1,0:T(8,128)(2,1)}, u32[]{:S(2)}) copy-start(bf16[3,3,3,256,256]{4,3,2,1,0:T(8,128)(2,1)} %param.6) | copy-start | bytes 10616836
  58.7 6.2 %collective-permute-start.9 = (bf16[16,2,27,8,128]{4,3,2,1,0:T(8,128)(2,1)S(1)}, bf16[16,2,27,8,128]{4,3,2,1,0:T(8,128)(2,1)S(1)}, u32[]{:S(2)}, u32[]{:S(2)}) collective-permute-start(bf16[16,2,27,8,128]{4,3,2,1,0:T(8,128)(2,1)S(1)} %get-tuple-element.17), channel_id=1, source_target_pairs={{0,32},{32,0},{1,33},{33,1},{2,34},{34,2},{3,35},{35,3},{4,36},{36... | collective-permute-start | bytes 5308424 | tf_op jit(solution)/shard_map/ppermute | solution.py:373
  64.4 3.9 %collective-permute-start.8 = (bf16[16,2,27,8,128]{4,3,2,1,0:T(8,128)(2,1)S(1)}, bf16[16,2,27,8,128]{4,3,2,1,0:T(8,128)(2,1)S(1)}, u32[]{:S(2)}, u32[]{:S(2)}) collective-permute-start(bf16[16,2,27,8,128]{4,3,2,1,0:T(8,128)(2,1)S(1)} %get-tuple-element.15), channel_id=1, source_target_pairs={{0,32},{32,0},{1,33},{33,1},{2,34},{34,2},{3,35},{35,3},{4,36},{36... | collective-permute-start | bytes 5308424 | tf_op jit(solution)/shard_map/ppermute | solution.py:372
  165.8 49.2 %collective-permute-start.10 = (bf16[4,16,27,8,128]{4,3,2,1,0:T(8,128)(2,1)S(1)}, bf16[4,16,27,8,128]{4,3,2,1,0:T(8,128)(2,1)S(1)}, u32[]{:S(2)}, u32[]{:S(2)}) collective-permute-start(bf16[4,16,27,8,128]{4,3,2,1,0:T(8,128)(2,1)S(1)} %all_to_all.35), channel_id=1, source_target_pairs={{0,32},{32,0},{1,33},{33,1},{2,34},{34,2},{3,35},{35,3},{4,36},{36... | collective-permute-start | bytes 10616840 | tf_op jit(solution)/shard_map/ppermute | solution.py:385
  166.0 17.0 %collective-permute-start.5 = (bf16[2,4,128,256]{3,2,1,0:T(8,128)(2,1)S(1)}, bf16[2,4,128,256]{3,2,1,0:T(8,128)(2,1)S(1)}, u32[]{:S(2)}, u32[]{:S(2)}) collective-permute-start(bf16[2,4,128,256]{3,2,1,0:T(8,128)(2,1)S(1)} %pad_maximum_fusion.8), channel_id=1, source_target_pairs={{1,0},{2,1},{3,2},{4,3},{5,4},{6,5},{7,6},{8,7},{9,8},{10,9},{11,1... | collective-permute-start | bytes 1572872 | tf_op jit(solution)/shard_map/ppermute | solution.py:321
  171.2 32.5 %copy-start.1 = (bf16[4,2,128,256]{3,2,1,0:T(8,128)(2,1)S(1)}, bf16[4,2,128,256]{3,2,1,0:T(8,128)(2,1)}, u32[]{:S(2)}) copy-start(bf16[4,2,128,256]{3,2,1,0:T(8,128)(2,1)} %latents_ref.3) | copy-start | bytes 1572868
  171.2 21.8 %collective-permute-start.4 = (bf16[2,4,128,256]{3,2,1,0:T(8,128)(2,1)S(1)}, bf16[2,4,128,256]{3,2,1,0:T(8,128)(2,1)S(1)}, u32[]{:S(2)}, u32[]{:S(2)}) collective-permute-start(bf16[2,4,128,256]{3,2,1,0:T(8,128)(2,1)S(1)} %pad_maximum_fusion.7), channel_id=1, source_target_pairs={{0,1},{1,2},{2,3},{3,4},{4,5},{5,6},{6,7},{7,8},{8,9},{9,10},{10,1... | collective-permute-start | bytes 1572872 | tf_op jit(solution)/shard_map/ppermute | solution.py:321
  193.1 10.5 %collective-permute-start.6 = (bf16[2,4,128,256]{3,2,1,0:T(8,128)(2,1)S(1)}, bf16[2,4,128,256]{3,2,1,0:T(8,128)(2,1)S(1)}, u32[]{:S(2)}, u32[]{:S(2)}) collective-permute-start(bf16[2,4,128,256]{3,2,1,0:T(8,128)(2,1)S(1)} %pad_maximum_fusion.9), channel_id=1, source_target_pairs={{0,32},{32,64},{64,96},{1,33},{33,65},{65,97},{2,34},{34,66},{66,9... | collective-permute-start | bytes 1572872 | tf_op jit(solution)/shard_map/ppermute | solution.py:321
  195.4 13.8 %collective-permute-start.7 = (bf16[2,4,128,256]{3,2,1,0:T(8,128)(2,1)S(1)}, bf16[2,4,128,256]{3,2,1,0:T(8,128)(2,1)S(1)}, u32[]{:S(2)}, u32[]{:S(2)}) collective-permute-start(bf16[2,4,128,256]{3,2,1,0:T(8,128)(2,1)S(1)} %pad_maximum_fusion.10), channel_id=1, source_target_pairs={{32,0},{64,32},{96,64},{33,1},{65,33},{97,65},{34,2},{66,34},{98,6... | collective-permute-start | bytes 1572872 | tf_op jit(solution)/shard_map/ppermute | solution.py:321
  199.1 10.1 %copy-start.4 = (bf16[3,3,3,256,256]{4,3,2,1,0:T(8,128)(2,1)S(1)}, bf16[3,3,3,256,256]{4,3,2,1,0:T(8,128)(2,1)}, u32[]{:S(2)}) copy-start(bf16[3,3,3,256,256]{4,3,2,1,0:T(8,128)(2,1)} %param.5) | copy-start | bytes 10616836

commit v5 on v3

--- a/solution.py
+++ b/solution.py
@@ -22,13 +22,13 @@
 PASS_FLOPS = 2 * FRAMES * 2 * W * TAPS * C * C
 
 
-def fill_ext(ext_ref, own_ref, rows_ref, time_ref, first, which):
+def fill_ext(ext_ref, own_ref, above_ref, below_ref, time_ref, first, which=0):
     other = 0 if first == 2 else FRAMES
     for f in range(FRAMES):
-        ext_ref[first + f, 0:W] = rows_ref[0, which, f]
+        ext_ref[first + f, 0:W] = above_ref[which, f]
         for r in range(2):
             ext_ref[first + f, (r + 1) * W : (r + 2) * W] = own_ref[f, r]
-        ext_ref[first + f, 3 * W : 4 * W] = rows_ref[1, which, f]
+        ext_ref[first + f, 3 * W : 4 * W] = below_ref[which, f]
     for f in range(2):
         for r in range(4):
             ext_ref[other + f, r * W : (r + 1) * W] = time_ref[f, r]
@@ -83,9 +83,9 @@
     return value.reshape(2, W, C)
 
 
-def hidden_kernel(own_ref, rows_ref, time_ref, source_ref, hidden_ref, active_ref, ext_ref, kernel_ref, sem):
+def hidden_kernel(own_ref, above_ref, below_ref, time_ref, source_ref, hidden_ref, active_ref, ext_ref, kernel_ref, sem):
     copies = load_taps(source_ref, kernel_ref, sem)
-    fill_ext(ext_ref, own_ref, rows_ref, time_ref, 2, 0)
+    fill_ext(ext_ref, own_ref, above_ref, below_ref, time_ref, 2)
     for copy in copies:
         copy.wait()
 
@@ -98,9 +98,9 @@
     lax.fori_loop(0, FRAMES, body, 0)
 
 
-def hidden_grad_kernel(own_ref, rows_ref, time_ref, source_ref, hidden_ref, out_ref, ext_ref, kernel_ref, sem):
+def hidden_grad_kernel(own_ref, above_ref, below_ref, time_ref, source_ref, hidden_ref, out_ref, ext_ref, kernel_ref, sem):
     copies = load_taps(source_ref, kernel_ref, sem)
-    fill_ext(ext_ref, own_ref, rows_ref, time_ref, 0, 1)
+    fill_ext(ext_ref, own_ref, above_ref, below_ref, time_ref, 0)
     for copy in copies:
         copy.wait()
 
@@ -112,9 +112,9 @@
     lax.fori_loop(0, FRAMES, body, 0)
 
 
-def decoded_kernel(own_ref, rows_ref, time_ref, source_ref, latents_ref, out_ref, ext_ref, kernel_ref, sem):
+def decoded_kernel(own_ref, above_ref, below_ref, time_ref, source_ref, latents_ref, out_ref, ext_ref, kernel_ref, sem):
     copies = load_taps(source_ref, kernel_ref, sem)
-    fill_ext(ext_ref, own_ref, rows_ref, time_ref, 2, 0)
+    fill_ext(ext_ref, own_ref, above_ref, below_ref, time_ref, 2, 0)
     for copy in copies:
         copy.wait()
 
@@ -127,10 +127,10 @@
 
 
 def latent_grad_kernel(
-    own_ref, rows_ref, time_ref, source_ref, latents_ref, upstream_ref, out_ref, ext_ref, kernel_ref, sem
+    own_ref, above_ref, below_ref, time_ref, source_ref, latents_ref, upstream_ref, out_ref, ext_ref, kernel_ref, sem
 ):
     copies = load_taps(source_ref, kernel_ref, sem)
-    fill_ext(ext_ref, own_ref, rows_ref, time_ref, 0, 1)
+    fill_ext(ext_ref, own_ref, above_ref, below_ref, time_ref, 0, 1)
     for copy in copies:
         copy.wait()
 
@@ -160,10 +160,10 @@
 
 
 def second_grad_kernel(
-    core_ref, active_ref, own_ref, rows_ref, time_ref, keep_ref, send_ref, ext_ref, across_ref, turn_ref
+    core_ref, active_ref, own_ref, above_ref, below_ref, time_ref, keep_ref, send_ref, ext_ref, across_ref, turn_ref
 ):
     core = core_ref[0]
-    fill_ext(ext_ref, own_ref, rows_ref, time_ref, 0, 1)
+    fill_ext(ext_ref, own_ref, above_ref, below_ref, time_ref, 0)
     for f in range(EXT):
         for k, copy in enumerate(shift_copies(ext_ref[f])):
             across_ref[k, f] = copy
@@ -185,10 +185,10 @@
 
 
 def first_grad_kernel(
-    core_ref, grad_ref, own_ref, rows_ref, time_ref, keep_ref, send_ref, ext_ref, across_ref, turn_ref
+    core_ref, grad_ref, own_ref, above_ref, below_ref, time_ref, keep_ref, send_ref, ext_ref, across_ref, turn_ref
 ):
     core = core_ref[0]
-    fill_ext(ext_ref, own_ref, rows_ref, time_ref, 2, 0)
+    fill_ext(ext_ref, own_ref, above_ref, below_ref, time_ref, 2)
     for t in range(FRAMES):
         for k, copy in enumerate(shift_copies(grad_ref[t].reshape(2 * W, C))):
             across_ref[k, t * 2 * W : (t + 1) * 2 * W] = copy
@@ -238,41 +238,41 @@
         pltpu.VMEM((3, 9, C, C), BF),
         pltpu.SemaphoreType.DMA((3,)),
     ]
-    return whole(kernel, outs, scratch, 24, hbm=(3,))
+    return whole(kernel, outs, scratch, 24, hbm=(4,))
 
 
 STEP = 3
 
 
-def assemble_kernel(core_ref, own2_ref, own1_ref, far2_ref, far1_ref, first_ref, second_ref):
+def assemble_kernel(core_ref, own_ref, far_ref, first_ref, second_ref):
     core = core_ref[0]
+    start = pl.program_id(0) * STEP
     mine = pl.multiple_of(core * 128, 128)
     theirs = pl.multiple_of((1 - core) * 128, 128)
-    for out, own, far in ((second_ref, own2_ref, far2_ref), (first_ref, own1_ref, far1_ref)):
+    for grad, out in ((0, second_ref), (1, first_ref)):
         for p in range(STEP):
             for b in range(2):
                 lanes = slice(b * 128, (b + 1) * 128)
-                out[p, pl.ds(mine, 128), lanes] = own[0, :, b, p].astype(F32).reshape(128, 128)
-                out[p, pl.ds(theirs, 128), lanes] = far[0, :, b, p].astype(F32).reshape(128, 128)
+                for rows, ref in ((mine, own_ref), (theirs, far_ref)):
+                    half = ref[grad, :, b, start + p].astype(F32)
+                    out[p, pl.ds(rows, 128), lanes] = half.reshape(128, 128)
 
 
 def assemble(core, own, far):
     own, far = (v.reshape(2, 16, 2, TAPS, 8, 128) for v in (own, far))
-    block = (1, 16, 2, STEP, 8, 128)
-    second = pl.BlockSpec(block, lambda p: (0, 0, 0, p, 0, 0))
-    first = pl.BlockSpec(block, lambda p: (1, 0, 0, p, 0, 0))
     out = pl.BlockSpec((STEP, C, C), lambda p: (p, 0, 0))
     shape = jax.ShapeDtypeStruct((TAPS, C, C), F32)
+    whole_array = pl.BlockSpec(memory_space=pltpu.VMEM)
     return pl.pallas_call(
         assemble_kernel,
         out_shape=(shape, shape),
         grid=(TAPS // STEP,),
-        in_specs=[pl.BlockSpec(memory_space=pltpu.SMEM), second, first, second, first],
+        in_specs=[pl.BlockSpec(memory_space=pltpu.SMEM), whole_array, whole_array],
         out_specs=(out, out),
-        compiler_params=pltpu.CompilerParams(vmem_limit_bytes=16 << 20),
+        compiler_params=pltpu.CompilerParams(vmem_limit_bytes=24 << 20),
         cost_estimate=cost(1 << 24, 28 << 20),
         name="assemble",
-    )(core, own, own, far, far)
+    )(core, own, far)
 
 
 def total_kernel(parts_ref, out_ref):
@@ -315,18 +315,17 @@
     return lax.ppermute(value, axis, pairs)
 
 
-def edge_rows(one, two):
-    to_above = jnp.stack([one[:, 0], two[:, 0]])
-    to_below = jnp.stack([one[:, 1], two[:, 1]])
-    above = swap(to_below, SPACE, 1)
-    below = swap(to_above, SPACE, -1)
-    return jnp.stack([above, below])
+def edge_rows(arrays):
+    above = swap(jnp.stack([value[:, 1] for value in arrays]), SPACE, 1)
+    below = swap(jnp.stack([value[:, 0] for value in arrays]), SPACE, -1)
+    return above, below
 
 
 def two_frames(own, rows, which, start):
     frames = slice(start, start + 2)
+    above, below = rows
     return jnp.concatenate(
-        [rows[0, which, frames][:, None], own[frames], rows[1, which, frames][:, None]], axis=1
+        [above[which, frames][:, None], own[frames], below[which, frames][:, None]], axis=1
     )
 
 
@@ -339,28 +338,26 @@
     block = jax.ShapeDtypeStruct((FRAMES, 2, W, C), BF)
     ext = pltpu.VMEM((EXT, 4 * W, C), BF)
 
-    rows = edge_rows(smooth, upstream)
+    rows = edge_rows((smooth,))
+    up_rows = edge_rows((upstream,))
     smooth_time = swap(two_frames(smooth, rows, 0, 2), GROUP, 1)
-    up_time = swap(two_frames(upstream, rows, 1, 0), GROUP, -1)
+    up_time = swap(two_frames(upstream, up_rows, 0, 0), GROUP, -1)
     hidden, active = convolution(
         hidden_kernel, (jax.ShapeDtypeStruct((FRAMES, 2 * W, C), F32), block)
-    )(smooth, rows, smooth_time, k1)
+    )(smooth, *rows, smooth_time, k1)
     (hidden_grad,) = convolution(hidden_grad_kernel, (block,))(
-        upstream, rows, up_time, k2, hidden
+        upstream, *up_rows, up_time, k2, hidden
     )
 
-    late = edge_rows(active, hidden_grad)
-    active_time = swap(two_frames(active, late, 0, 2), GROUP, 1)
-    grad_time = swap(two_frames(hidden_grad, late, 1, 0), GROUP, -1)
-
+    late = edge_rows((active, hidden_grad))
     half = (16, 2, TAPS, 8, 128)
     pair = (jax.ShapeDtypeStruct(half, F32), jax.ShapeDtypeStruct(half, BF))
     keep2, send2 = whole(
         second_grad_kernel, pair, [ext, pltpu.VMEM((3, EXT, 4 * W, C), BF), pltpu.VMEM((C, FRAMES * 2 * W), BF)], 40, 1
-    )(core, active, upstream, rows, up_time)
+    )(core, active, upstream, *up_rows, up_time)
     keep1, send1 = whole(
         first_grad_kernel, pair, [ext, pltpu.VMEM((3, FRAMES * 2 * W, C), BF), pltpu.VMEM((EXT, C, 4 * W), BF)], 40, 1
-    )(core, hidden_grad, smooth, rows, smooth_time)
+    )(core, hidden_grad, smooth, *rows, smooth_time)
 
     across = [(0, 1), (1, 0)]
     got2 = lax.ppermute(send2, "co", across)
@@ -371,6 +368,9 @@
     block_rows = 64 // (first * second) * TAPS
     parts = exchange(mine.reshape(first, second, block_rows, 8, 128), near)
     quarter = total(parts, 1)
+    active_own, grad_own, _ = lax.optimization_barrier((active, hidden_grad, quarter))
+    active_time = swap(two_frames(active_own, late, 0, 2), GROUP, 1)
+    grad_time = swap(two_frames(grad_own, late, 1, 0), GROUP, -1)
     parts = exchange(quarter.reshape(second, block_rows, 8, 128), rest)
     spread = total(parts[:, None], second)
     quarter = exchange(spread.reshape(second, block_rows, 8, 128), rest)
@@ -378,9 +378,9 @@
     far = lax.ppermute(own, "co", across)
 
     (decoded,) = convolution(decoded_kernel, (block,))(
-        active, late, active_time, k2, latents
+        active, *late, active_time, k2, latents
     )
-    (latent_grad,) = convolution(latent_grad_kernel, (block,))(hidden_grad, late, grad_time, k1, latents, upstream)
+    (latent_grad,) = convolution(latent_grad_kernel, (block,))(hidden_grad, *late, grad_time, k1, latents, upstream)
     first_grad, second_grad = assemble(core, own, far)
     shape = first_kernel.shape
     return (decoded, latent_grad, first_grad.reshape(shape), second_grad.reshape(shape))

time: 214 us -> 212 us (level)
  the two profiles are of different devices: /device:TPU:96 before, /device:TPU:31 now
where the time goes in v5:
time: 212 us; the launch traced here: 211 us
  blocking collectives  90.4 us (43%)
  starting transfers between devices  45.4 us (21%)
  Pallas kernels  38.4 us (18%)
  waiting for transfers between devices  28.7 us (14%)
  local copies, waits for them, and re-layouts  3.81 us (2%)
  other arithmetic  3.64 us (2%)
    all_to_all x4, blocking collectives, exchange(): lax.all_to_all(value, ALL, 0, 0, axis_index_groups=groups, tiled=False)  90.4 us
    ppermute x10, starting transfers between devices, swap(): return lax.ppermute(value, axis, pairs)  43.6 us
    pallas_call x8, Pallas kernels, call(): pl.pallas_call(kernel, out_shape=outs, in_specs=[pl.BlockSpec(memory_spac...  32.2 us
    ppermute x10, waiting for transfers between devices, swap(): return lax.ppermute(value, axis, pairs)  25.8 us
    pallas_call x1, Pallas kernels, assemble(): pl.pallas_call(assemble_kernel, out_shape=(shape, shape), grid=(TAPS // S...  6.22 us
  transfers between devices with their start and end apart: 13, of which 5 were waited for; matrix products, arithmetic and copies ran while one was open for 1% of the time, Pallas kernels for 10%

profile of v5, /device:TPU:31, one launch (start us, length us, event | category | flops | bytes accessed | tf_op | source)
XLA Modules:
  0.0 211.4 jit_solution(13351368439661445595)
XLA Ops:
  2.1 2.5 %collective-permute-start.1 = (bf16[1,4,128,256]{3,2,1,0:T(8,128)(2,1)S(1)}, bf16[1,4,128,256]{3,2,1,0:T(8,128)(2,1)S(1)}, u32[]{:S(2)}, u32[]{:S(2)}) collective-permute-start(bf16[1,4,128,256]{3,2,1,0:T(8,128)(2,1)S(1)} %get-tuple-element.34), channel_id=1, source_target_pairs={{1,0},{2,1},{3,2},{4,3},{5,4},{6,5},{7,6},{8,7},{9,8},{10,9},{11,1... | collective-permute-start | bytes 786440 | tf_op jit(solution)/shard_map/ppermute | solution.py:315
  4.5 8.5 %collective-permute-start = (bf16[1,4,128,256]{3,2,1,0:T(8,128)(2,1)S(1)}, bf16[1,4,128,256]{3,2,1,0:T(8,128)(2,1)S(1)}, u32[]{:S(2)}, u32[]{:S(2)}) collective-permute-start(bf16[1,4,128,256]{3,2,1,0:T(8,128)(2,1)S(1)} %get-tuple-element.35), channel_id=1, source_target_pairs={{0,1},{1,2},{2,3},{3,4},{4,5},{5,6},{6,7},{7,8},{8,9},{9,10},{10,1... | collective-permute-start | bytes 786440 | tf_op jit(solution)/shard_map/ppermute | solution.py:315
  16.1 9.1 %collective-permute-start.3 = (bf16[1,4,128,256]{3,2,1,0:T(8,128)(2,1)S(1)}, bf16[1,4,128,256]{3,2,1,0:T(8,128)(2,1)S(1)}, u32[]{:S(2)}, u32[]{:S(2)}) collective-permute-start(bf16[1,4,128,256]{3,2,1,0:T(8,128)(2,1)S(1)} %get-tuple-element.33), channel_id=1, source_target_pairs={{0,1},{1,2},{2,3},{3,4},{4,5},{5,6},{6,7},{7,8},{8,9},{9,10},{10,1... | collective-permute-start | bytes 786440 | tf_op jit(solution)/shard_map/ppermute | solution.py:315
  25.3 5.2 %collective-permute-start.2 = (bf16[2,4,128,256]{3,2,1,0:T(8,128)(2,1)S(1)}, bf16[2,4,128,256]{3,2,1,0:T(8,128)(2,1)S(1)}, u32[]{:S(2)}, u32[]{:S(2)}) collective-permute-start(bf16[2,4,128,256]{3,2,1,0:T(8,128)(2,1)S(1)} %pad_maximum_fusion.1), channel_id=1, source_target_pairs={{0,32},{32,64},{64,96},{1,33},{33,65},{65,97},{2,34},{34,66},{66,9... | collective-permute-start | bytes 1572872 | tf_op jit(solution)/shard_map/ppermute | solution.py:315
  31.5 3.0 %collective-permute-start.5 = (bf16[2,4,128,256]{3,2,1,0:T(8,128)(2,1)}, bf16[2,4,128,256]{3,2,1,0:T(8,128)(2,1)S(1)}, u32[]{:S(2)}, u32[]{:S(2)}) collective-permute-start(bf16[2,4,128,256]{3,2,1,0:T(8,128)(2,1)} %pad_maximum_fusion.2), channel_id=1, source_target_pairs={{32,0},{64,32},{96,64},{33,1},{65,33},{97,65},{34,2},{66,34},{98,6... | collective-permute-start | bytes 1572872 | tf_op jit(solution)/shard_map/ppermute | solution.py:315
  34.5 2.1 collective-permute-done.2.time_ref
  38.6 4.8 %shard_map.75 = (f32[4,256,256]{2,1,0:T(8,128)S(1)}, bf16[4,2,128,256]{3,2,1,0:T(8,128)(2,1)S(1)}) custom-call(bf16[4,2,128,256]{3,2,1,0:T(8,128)(2,1)S(1)} %copy.11.own_ref, bf16[1,4,128,256]{3,2,1,0:T(8,128)(2,1)S(1)} %collective-permute-done.above_ref, bf16[1,4,128,256]{3,2,1,0:T(8,128)(2,1)S(1)} %collective-permute-done.1.below_ref, ...), custom_call_target="tpu_custom_call" | custom-call | flops 3623878656 | bytes 6684672 | tf_op jit(solution)/shard_map/pallas_call | solution.py:222
  43.4 4.9 %shard_map.76.grad_ref.own_ref = bf16[4,2,128,256]{3,2,1,0:T(8,128)(2,1)S(1)} custom-call(bf16[4,2,128,256]{3,2,1,0:T(8,128)(2,1)S(1)} %copy-done, bf16[1,4,128,256]{3,2,1,0:T(8,128)(2,1)S(1)} %collective-permute-done.3.above_ref, bf16[1,4,128,256]{3,2,1,0:T(8,128)(2,1)S(1)} %collective-permute-done.4.below_ref, ...), custom_call_target="tpu_custom_call" | custom-call | flops 3623878656 | bytes 6684672 | tf_op jit(solution)/shard_map/pallas_call | solution.py:222
  48.3 5.0 %shard_map.78 = (f32[16,2,27,8,128]{4,3,2,1,0:T(8,128)S(1)}, bf16[16,2,27,8,128]{4,3,2,1,0:T(8,128)(2,1)S(1)}) custom-call(s32[1]{0:T(128)} %bitcast.17.core_ref, bf16[4,2,128,256]{3,2,1,0:T(8,128)(2,1)S(1)} %shard_map.76.grad_ref.own_ref, bf16[4,2,128,256]{3,2,1,0:T(8,128)(2,1)S(1)} %copy.11.own_ref, ...), custom_call_target="tpu_custom_call" | custom-call | flops 3623878656 | bytes 7405572 | tf_op jit(solution)/shard_map/pallas_call | solution.py:222
  53.4 5.6 %shard_map.77 = (f32[16,2,27,8,128]{4,3,2,1,0:T(8,128)S(1)}, bf16[16,2,27,8,128]{4,3,2,1,0:T(8,128)(2,1)S(1)}) custom-call(s32[1]{0:T(128)} %bitcast.17.core_ref, bf16[4,2,128,256]{3,2,1,0:T(8,128)(2,1)S(1)} %get-tuple-element.20.active_ref.own_ref, bf16[4,2,128,256]{3,2,1,0:T(8,128)(2,1)S(1)} %copy-done, ...), custom_call_target="tpu_custom_call" | custom-call | flops 3623878656 | bytes 7405572 | tf_op jit(solution)/shard_map/pallas_call | solution.py:222
  59.9 2.9 %collective-permute-done.8 = bf16[16,2,27,8,128]{4,3,2,1,0:T(8,128)(2,1)S(1)} collective-permute-done((bf16[16,2,27,8,128]{4,3,2,1,0:T(8,128)(2,1)S(1)}, bf16[16,2,27,8,128]{4,3,2,1,0:T(8,128)(2,1)S(1)}, u32[]{:S(2)}, u32[]{:S(2)}) %collective-permute-start.8) | collective-permute-done | bytes 1769504 | tf_op jit(solution)/shard_map/ppermute | solution.py:363
  63.6 25.0 %all_to_all.20.parts_ref = bf16[4,16,27,8,128]{4,3,2,1,0:T(8,128)(2,1)S(1)} all-to-all(bf16[4,16,27,8,128]{4,3,2,1,0:T(8,128)(2,1)S(1)} %bitcast.70), channel_id=1, replica_groups={{0,1,2,3},{4,5,6,7},{8,9,10,11},{12,13,14,15},{16,17,18,19},{20,21,22,2..., dimensions={0} | all-to-all | bytes 7077888 | tf_op jit(solution)/shard_map/all_to_all | solution.py:309
  89.2 20.9 %all_to_all.21 = bf16[16,27,8,128]{3,2,1,0:T(8,128)(2,1)S(1)} all-to-all(bf16[16,27,8,128]{3,2,1,0:T(8,128)(2,1)S(1)} %bitcast.65), channel_id=1, replica_groups={{0,4,8,12,16,20,24,28,64,68,72,76,80,84,88,92},{1,5,9,13,17,21,25,29,65..., dimensions={0} | all-to-all | bytes 1769472 | tf_op jit(solution)/shard_map/all_to_all | solution.py:309
  110.2 17.1 %all_to_all.22 = bf16[16,27,8,128]{3,2,1,0:T(8,128)(2,1)S(1)} all-to-all(bf16[16,27,8,128]{3,2,1,0:T(8,128)(2,1)S(1)} %bitcast.64), channel_id=1, replica_groups={{0,4,8,12,16,20,24,28,64,68,72,76,80,84,88,92},{1,5,9,13,17,21,25,29,65..., dimensions={0} | all-to-all | bytes 1769472 | tf_op jit(solution)/shard_map/all_to_all | solution.py:309
  127.7 27.4 %all_to_all.23 = bf16[4,16,27,8,128]{4,3,2,1,0:T(8,128)(2,1)S(1)} all-to-all(bf16[4,16,27,8,128]{4,3,2,1,0:T(8,128)(2,1)S(1)} %broadcast_in_dim.10), channel_id=1, replica_groups={{0,1,2,3},{4,5,6,7},{8,9,10,11},{12,13,14,15},{16,17,18,19},{20,21,22,2..., dimensions={0} | all-to-all | bytes 7077888 | tf_op jit(solution)/shard_map/all_to_all | solution.py:309
  156.4 5.6 %collective-permute-start.6 = (bf16[2,4,128,256]{3,2,1,0:T(8,128)(2,1)S(1)}, bf16[2,4,128,256]{3,2,1,0:T(8,128)(2,1)S(1)}, u32[]{:S(2)}, u32[]{:S(2)}) collective-permute-start(bf16[2,4,128,256]{3,2,1,0:T(8,128)(2,1)S(1)} %pad_maximum_fusion.3), channel_id=1, source_target_pairs={{0,1},{1,2},{2,3},{3,4},{4,5},{5,6},{6,7},{7,8},{8,9},{9,10},{10,1... | collective-permute-start | bytes 1572872 | tf_op jit(solution)/shard_map/ppermute | solution.py:315
  164.0 9.3 %collective-permute-done.6.above_ref = bf16[2,4,128,256]{3,2,1,0:T(8,128)(2,1)S(1)} collective-permute-done((bf16[2,4,128,256]{3,2,1,0:T(8,128)(2,1)S(1)}, bf16[2,4,128,256]{3,2,1,0:T(8,128)(2,1)S(1)}, u32[]{:S(2)}, u32[]{:S(2)}) %collective-permute-start.6) | collective-permute-done | bytes 524320 | tf_op jit(solution)/shard_map/ppermute | solution.py:315
  173.3 9.6 %collective-permute-done.7.below_ref = bf16[2,4,128,256]{3,2,1,0:T(8,128)(2,1)S(1)} collective-permute-done((bf16[2,4,128,256]{3,2,1,0:T(8,128)(2,1)S(1)}, bf16[2,4,128,256]{3,2,1,0:T(8,128)(2,1)S(1)}, u32[]{:S(2)}, u32[]{:S(2)}) %collective-permute-start.7) | collective-permute-done | bytes 524320 | tf_op jit(solution)/shard_map/ppermute | solution.py:315
  183.0 3.1 %collective-permute-start.11 = (bf16[2,4,128,256]{3,2,1,0:T(8,128)(2,1)S(1)}, bf16[2,4,128,256]{3,2,1,0:T(8,128)(2,1)S(1)}, u32[]{:S(2)}, u32[]{:S(2)}) collective-permute-start(bf16[2,4,128,256]{3,2,1,0:T(8,128)(2,1)S(1)} %pad_maximum_fusion.6), channel_id=1, source_target_pairs={{32,0},{64,32},{96,64},{33,1},{65,33},{97,65},{34,2},{66,34},{98,6... | collective-permute-start | bytes 1572872 | tf_op jit(solution)/shard_map/ppermute | solution.py:315
  186.3 2.7 %collective-permute-start.10 = (bf16[2,4,128,256]{3,2,1,0:T(8,128)(2,1)S(1)}, bf16[2,4,128,256]{3,2,1,0:T(8,128)(2,1)S(1)}, u32[]{:S(2)}, u32[]{:S(2)}) collective-permute-start(bf16[2,4,128,256]{3,2,1,0:T(8,128)(2,1)S(1)} %pad_maximum_fusion.5), channel_id=1, source_target_pairs={{0,32},{32,64},{64,96},{1,33},{33,65},{65,97},{2,34},{34,66},{66,9... | collective-permute-start | bytes 1572872 | tf_op jit(solution)/shard_map/ppermute | solution.py:315
  189.0 4.8 %collective-permute-done.11.time_ref = bf16[2,4,128,256]{3,2,1,0:T(8,128)(2,1)S(1)} collective-permute-done((bf16[2,4,128,256]{3,2,1,0:T(8,128)(2,1)S(1)}, bf16[2,4,128,256]{3,2,1,0:T(8,128)(2,1)S(1)}, u32[]{:S(2)}, u32[]{:S(2)}) %collective-permute-start.11) | collective-permute-done | bytes 524320 | tf_op jit(solution)/shard_map/ppermute | solution.py:315
  193.8 5.8 %shard_map.81 = bf16[4,2,128,256]{3,2,1,0:T(8,128)(2,1)} custom-call(bf16[4,2,128,256]{3,2,1,0:T(8,128)(2,1)S(1)} %shard_map.76.grad_ref.own_ref, bf16[2,4,128,256]{3,2,1,0:T(8,128)(2,1)S(1)} %collective-permute-done.6.above_ref, bf16[2,4,128,256]{3,2,1,0:T(8,128)(2,1)S(1)} %collective-permute-done.7.below_ref, ...), custom_call_target="tpu_custom_call" | custom-call | flops 3623878656 | bytes 7208960 | tf_op jit(solution)/shard_map/pallas_call | solution.py:222
  199.6 5.5 %shard_map.80 = bf16[4,2,128,256]{3,2,1,0:T(8,128)(2,1)} custom-call(bf16[4,2,128,256]{3,2,1,0:T(8,128)(2,1)S(1)} %get-tuple-element.20.active_ref.own_ref, bf16[2,4,128,256]{3,2,1,0:T(8,128)(2,1)S(1)} %collective-permute-done.6.above_ref, bf16[2,4,128,256]{3,2,1,0:T(8,128)(2,1)S(1)} %collective-permute-done.7.below_ref, ...), custom_call_target="tpu_custom_call" | custom-call | flops 3623878656 | bytes 6684672 | tf_op jit(solution)/shard_map/pallas_call | solution.py:222
  205.2 6.2 %assemble.1 = (f32[27,256,256]{2,1,0:T(8,128)}, f32[27,256,256]{2,1,0:T(8,128)}) custom-call(s32[1]{0:T(128)} %bitcast.17.core_ref, bf16[2,16,2,27,8,128]{5,4,3,2,1,0:T(8,128)(2,1)S(1)} %bitcast.61, bf16[2,16,2,27,8,128]{5,4,3,2,1,0:T(8,128)(2,1)S(1)} %bitcast.62), custom_call_target="tpu_custom_call" | custom-call | flops 16777216 | bytes 29360128 | tf_op jit(solution)/shard_map/assemble/pallas_call | solution.py:266
  (51 shorter events, 13.8 us)
Async XLA Ops:
  0.6 30.0 %slice-start = ((bf16[4,2,128,256]{3,2,1,0:T(8,128)(2,1)}), bf16[2,2,128,256]{3,2,1,0:T(8,128)(2,1)S(1)}, s32[]{:S(2)}) async-start(bf16[4,2,128,256]{3,2,1,0:T(8,128)(2,1)} %upstream_ref.1), calls=%async_computation.4 | async-start | bytes 524288 | tf_op jit(solution)/shard_map/slice | solution.py:328
  2.1 23.1 %collective-permute-start.1 = (bf16[1,4,128,256]{3,2,1,0:T(8,128)(2,1)S(1)}, bf16[1,4,128,256]{3,2,1,0:T(8,128)(2,1)S(1)}, u32[]{:S(2)}, u32[]{:S(2)}) collective-permute-start(bf16[1,4,128,256]{3,2,1,0:T(8,128)(2,1)S(1)} %get-tuple-element.34), channel_id=1, source_target_pairs={{1,0},{2,1},{3,2},{4,3},{5,4},{6,5},{7,6},{8,7},{9,8},{10,9},{11,1... | collective-permute-start | bytes 786440 | tf_op jit(solution)/shard_map/ppermute | solution.py:315
  4.5 20.7 %collective-permute-start = (bf16[1,4,128,256]{3,2,1,0:T(8,128)(2,1)S(1)}, bf16[1,4,128,256]{3,2,1,0:T(8,128)(2,1)S(1)}, u32[]{:S(2)}, u32[]{:S(2)}) collective-permute-start(bf16[1,4,128,256]{3,2,1,0:T(8,128)(2,1)S(1)} %get-tuple-element.35), channel_id=1, source_target_pairs={{0,1},{1,2},{2,3},{3,4},{4,5},{5,6},{6,7},{7,8},{8,9},{9,10},{10,1... | collective-permute-start | bytes 786440 | tf_op jit(solution)/shard_map/ppermute | solution.py:315
  14.2 16.4 %collective-permute-start.4 = (bf16[1,4,128,256]{3,2,1,0:T(8,128)(2,1)S(1)}, bf16[1,4,128,256]{3,2,1,0:T(8,128)(2,1)S(1)}, u32[]{:S(2)}, u32[]{:S(2)}) collective-permute-start(bf16[1,4,128,256]{3,2,1,0:T(8,128)(2,1)S(1)} %get-tuple-element.32), channel_id=1, source_target_pairs={{1,0},{2,1},{3,2},{4,3},{5,4},{6,5},{7,6},{8,7},{9,8},{10,9},{11,1... | collective-permute-start | bytes 786440 | tf_op jit(solution)/shard_map/ppermute | solution.py:315
  16.1 14.5 %collective-permute-start.3 = (bf16[1,4,128,256]{3,2,1,0:T(8,128)(2,1)S(1)}, bf16[1,4,128,256]{3,2,1,0:T(8,128)(2,1)S(1)}, u32[]{:S(2)}, u32[]{:S(2)}) collective-permute-start(bf16[1,4,128,256]{3,2,1,0:T(8,128)(2,1)S(1)} %get-tuple-element.33), channel_id=1, source_target_pairs={{0,1},{1,2},{2,3},{3,4},{4,5},{5,6},{6,7},{7,8},{8,9},{9,10},{10,1... | collective-permute-start | bytes 786440 | tf_op jit(solution)/shard_map/ppermute | solution.py:315
  25.3 11.3 %collective-permute-start.2 = (bf16[2,4,128,256]{3,2,1,0:T(8,128)(2,1)S(1)}, bf16[2,4,128,256]{3,2,1,0:T(8,128)(2,1)S(1)}, u32[]{:S(2)}, u32[]{:S(2)}) collective-permute-start(bf16[2,4,128,256]{3,2,1,0:T(8,128)(2,1)S(1)} %pad_maximum_fusion.1), channel_id=1, source_target_pairs={{0,32},{32,64},{64,96},{1,33},{33,65},{65,97},{2,34},{34,66},{66,9... | collective-permute-start | bytes 1572872 | tf_op jit(solution)/shard_map/ppermute | solution.py:315
  31.5 12.0 %collective-permute-start.5 = (bf16[2,4,128,256]{3,2,1,0:T(8,128)(2,1)}, bf16[2,4,128,256]{3,2,1,0:T(8,128)(2,1)S(1)}, u32[]{:S(2)}, u32[]{:S(2)}) collective-permute-start(bf16[2,4,128,256]{3,2,1,0:T(8,128)(2,1)} %pad_maximum_fusion.2), channel_id=1, source_target_pairs={{32,0},{64,32},{96,64},{33,1},{65,33},{97,65},{34,2},{66,34},{98,6... | collective-permute-start | bytes 1572872 | tf_op jit(solution)/shard_map/ppermute | solution.py:315
  36.6 2.0 copy-start.2
  38.6 4.8 %copy-start = (bf16[4,2,128,256]{3,2,1,0:T(8,128)(2,1)S(1)}, bf16[4,2,128,256]{3,2,1,0:T(8,128)(2,1)}, u32[]{:S(2)}) copy-start(bf16[4,2,128,256]{3,2,1,0:T(8,128)(2,1)} %upstream_ref.1) | copy-start | bytes 1572868
  38.6 4.8 %copy-start.4 = (bf16[3,3,3,256,256]{4,3,2,1,0:T(8,128)(2,1)S(1)}, bf16[3,3,3,256,256]{4,3,2,1,0:T(8,128)(2,1)}, u32[]{:S(2)}) copy-start(bf16[3,3,3,256,256]{4,3,2,1,0:T(8,128)(2,1)} %param.6) | copy-start | bytes 10616836
  53.3 6.2 %collective-permute-start.9 = (bf16[16,2,27,8,128]{4,3,2,1,0:T(8,128)(2,1)S(1)}, bf16[16,2,27,8,128]{4,3,2,1,0:T(8,128)(2,1)S(1)}, u32[]{:S(2)}, u32[]{:S(2)}) collective-permute-start(bf16[16,2,27,8,128]{4,3,2,1,0:T(8,128)(2,1)S(1)} %get-tuple-element.19), channel_id=1, source_target_pairs={{0,32},{32,0},{1,33},{33,1},{2,34},{34,2},{3,35},{35,3},{4,36},{36... | collective-permute-start | bytes 5308424 | tf_op jit(solution)/shard_map/ppermute | solution.py:364
  59.0 3.9 %collective-permute-start.8 = (bf16[16,2,27,8,128]{4,3,2,1,0:T(8,128)(2,1)S(1)}, bf16[16,2,27,8,128]{4,3,2,1,0:T(8,128)(2,1)S(1)}, u32[]{:S(2)}, u32[]{:S(2)}) collective-permute-start(bf16[16,2,27,8,128]{4,3,2,1,0:T(8,128)(2,1)S(1)} %get-tuple-element.17), channel_id=1, source_target_pairs={{0,32},{32,0},{1,33},{33,1},{2,34},{34,2},{3,35},{35,3},{4,36},{36... | collective-permute-start | bytes 5308424 | tf_op jit(solution)/shard_map/ppermute | solution.py:363
  155.1 50.1 %collective-permute-start.12 = (bf16[4,16,27,8,128]{4,3,2,1,0:T(8,128)(2,1)S(1)}, bf16[4,16,27,8,128]{4,3,2,1,0:T(8,128)(2,1)S(1)}, u32[]{:S(2)}, u32[]{:S(2)}) collective-permute-start(bf16[4,16,27,8,128]{4,3,2,1,0:T(8,128)(2,1)S(1)} %all_to_all.23), channel_id=1, source_target_pairs={{0,32},{32,0},{1,33},{33,1},{2,34},{34,2},{3,35},{35,3},{4,36},{36... | collective-permute-start | bytes 10616840 | tf_op jit(solution)/shard_map/ppermute | solution.py:378
  156.3 37.5 %copy-start.1 = (bf16[4,2,128,256]{3,2,1,0:T(8,128)(2,1)S(1)}, bf16[4,2,128,256]{3,2,1,0:T(8,128)(2,1)}, u32[]{:S(2)}) copy-start(bf16[4,2,128,256]{3,2,1,0:T(8,128)(2,1)} %latents_ref.3) | copy-start | bytes 1572868
  156.3 37.5 %copy-start.3 = (bf16[3,3,3,256,256]{4,3,2,1,0:T(8,128)(2,1)S(1)}, bf16[3,3,3,256,256]{4,3,2,1,0:T(8,128)(2,1)}, u32[]{:S(2)}) copy-start(bf16[3,3,3,256,256]{4,3,2,1,0:T(8,128)(2,1)} %param.5) | copy-start | bytes 10616836
  156.4 16.9 %collective-permute-start.6 = (bf16[2,4,128,256]{3,2,1,0:T(8,128)(2,1)S(1)}, bf16[2,4,128,256]{3,2,1,0:T(8,128)(2,1)S(1)}, u32[]{:S(2)}, u32[]{:S(2)}) collective-permute-start(bf16[2,4,128,256]{3,2,1,0:T(8,128)(2,1)S(1)} %pad_maximum_fusion.3), channel_id=1, source_target_pairs={{0,1},{1,2},{2,3},{3,4},{4,5},{5,6},{6,7},{7,8},{8,9},{9,10},{10,1... | collective-permute-start | bytes 1572872 | tf_op jit(solution)/shard_map/ppermute | solution.py:315
  162.1 20.8 %collective-permute-start.7 = (bf16[2,4,128,256]{3,2,1,0:T(8,128)(2,1)S(1)}, bf16[2,4,128,256]{3,2,1,0:T(8,128)(2,1)S(1)}, u32[]{:S(2)}, u32[]{:S(2)}) collective-permute-start(bf16[2,4,128,256]{3,2,1,0:T(8,128)(2,1)S(1)} %pad_maximum_fusion.4), channel_id=1, source_target_pairs={{1,0},{2,1},{3,2},{4,3},{5,4},{6,5},{7,6},{8,7},{9,8},{10,9},{11,1... | collective-permute-start | bytes 1572872 | tf_op jit(solution)/shard_map/ppermute | solution.py:315
  183.0 10.8 %collective-permute-start.11 = (bf16[2,4,128,256]{3,2,1,0:T(8,128)(2,1)S(1)}, bf16[2,4,128,256]{3,2,1,0:T(8,128)(2,1)S(1)}, u32[]{:S(2)}, u32[]{:S(2)}) collective-permute-start(bf16[2,4,128,256]{3,2,1,0:T(8,128)(2,1)S(1)} %pad_maximum_fusion.6), channel_id=1, source_target_pairs={{32,0},{64,32},{96,64},{33,1},{65,33},{97,65},{34,2},{66,34},{98,6... | collective-permute-start | bytes 1572872 | tf_op jit(solution)/shard_map/ppermute | solution.py:315
  186.3 13.3 %collective-permute-start.10 = (bf16[2,4,128,256]{3,2,1,0:T(8,128)(2,1)S(1)}, bf16[2,4,128,256]{3,2,1,0:T(8,128)(2,1)S(1)}, u32[]{:S(2)}, u32[]{:S(2)}) collective-permute-start(bf16[2,4,128,256]{3,2,1,0:T(8,128)(2,1)S(1)} %pad_maximum_fusion.5), channel_id=1, source_target_pairs={{0,32},{32,64},{64,96},{1,33},{33,65},{65,97},{2,34},{34,66},{66,9... | collective-permute-start | bytes 1572872 | tf_op jit(solution)/shard_map/ppermute | solution.py:315

commit v6 on v3

--- a/solution.py
+++ b/solution.py
@@ -244,35 +244,35 @@
 STEP = 3
 
 
-def assemble_kernel(core_ref, own2_ref, own1_ref, far2_ref, far1_ref, first_ref, second_ref):
+def assemble_kernel(core_ref, own_ref, far_ref, first_ref, second_ref):
     core = core_ref[0]
+    start = pl.program_id(0) * STEP
     mine = pl.multiple_of(core * 128, 128)
     theirs = pl.multiple_of((1 - core) * 128, 128)
-    for out, own, far in ((second_ref, own2_ref, far2_ref), (first_ref, own1_ref, far1_ref)):
+    for grad, out in ((0, second_ref), (1, first_ref)):
         for p in range(STEP):
             for b in range(2):
                 lanes = slice(b * 128, (b + 1) * 128)
-                out[p, pl.ds(mine, 128), lanes] = own[0, :, b, p].astype(F32).reshape(128, 128)
-                out[p, pl.ds(theirs, 128), lanes] = far[0, :, b, p].astype(F32).reshape(128, 128)
+                for rows, ref in ((mine, own_ref), (theirs, far_ref)):
+                    half = ref[grad, :, b, start + p].astype(F32)
+                    out[p, pl.ds(rows, 128), lanes] = half.reshape(128, 128)
 
 
 def assemble(core, own, far):
     own, far = (v.reshape(2, 16, 2, TAPS, 8, 128) for v in (own, far))
-    block = (1, 16, 2, STEP, 8, 128)
-    second = pl.BlockSpec(block, lambda p: (0, 0, 0, p, 0, 0))
-    first = pl.BlockSpec(block, lambda p: (1, 0, 0, p, 0, 0))
     out = pl.BlockSpec((STEP, C, C), lambda p: (p, 0, 0))
     shape = jax.ShapeDtypeStruct((TAPS, C, C), F32)
+    whole_array = pl.BlockSpec(memory_space=pltpu.VMEM)
     return pl.pallas_call(
         assemble_kernel,
         out_shape=(shape, shape),
         grid=(TAPS // STEP,),
-        in_specs=[pl.BlockSpec(memory_space=pltpu.SMEM), second, first, second, first],
+        in_specs=[pl.BlockSpec(memory_space=pltpu.SMEM), whole_array, whole_array],
         out_specs=(out, out),
-        compiler_params=pltpu.CompilerParams(vmem_limit_bytes=16 << 20),
+        compiler_params=pltpu.CompilerParams(vmem_limit_bytes=24 << 20),
         cost_estimate=cost(1 << 24, 28 << 20),
         name="assemble",
-    )(core, own, own, far, far)
+    )(core, own, far)
 
 
 def total_kernel(parts_ref, out_ref):
@@ -344,7 +344,7 @@
     up_time = swap(two_frames(upstream, rows, 1, 0), GROUP, -1)
     hidden, active = convolution(
         hidden_kernel, (jax.ShapeDtypeStruct((FRAMES, 2 * W, C), F32), block)
-    )(smooth, rows, smooth_time, k1)
+    )(smooth, rows, smooth_time, pltpu.with_memory_space_constraint(k1, pltpu.HBM))
     (hidden_grad,) = convolution(hidden_grad_kernel, (block,))(
         upstream, rows, up_time, k2, hidden
     )

time: 214 us -> 213 us (level)
  transfers between devices with their start and end apart: 11 -> 11, of which waited for: 7 -> 7; matrix products, arithmetic and copies ran while one was open for 1% -> 1% of each run, Pallas kernels for 10% -> 11%
where the time goes in v6:
time: 213 us
  blocking collectives  86.8 us (41%)
  waiting for transfers between devices  50.4 us (24%)
  Pallas kernels  40.2 us (19%)
  starting transfers between devices  28.4 us (13%)
  other arithmetic  3.9 us (2%)
    all_to_all x4, blocking collectives, exchange(): lax.all_to_all(value, ALL, 0, 0, axis_index_groups=groups, tiled=False)  86.8 us
    ppermute x8, waiting for transfers between devices, swap(): return lax.ppermute(value, axis, pairs)  47.5 us
    pallas_call x8, Pallas kernels, call(): pl.pallas_call(kernel, out_shape=outs, in_specs=[pl.BlockSpec(memory_spac...  34 us
    ppermute x8, starting transfers between devices, swap(): return lax.ppermute(value, axis, pairs)  27.7 us
    pallas_call x1, Pallas kernels, assemble(): pl.pallas_call(assemble_kernel, out_shape=(shape, shape), grid=(TAPS // S...  6.22 us
  transfers between devices with their start and end apart: 11, of which 7 were waited for; matrix products, arithmetic and copies ran while one was open for 1% of the time, Pallas kernels for 11%

profile of v6, /device:TPU:96, one launch (start us, length us, event | category | flops | bytes accessed | tf_op | source)
XLA Modules:
  0.0 212.5 jit_solution(15351811074236166304)
XLA Ops:
  3.2 7.1 %collective-permute-start.1 = (bf16[2,4,128,256]{3,2,1,0:T(8,128)(2,1)S(1)}, bf16[2,4,128,256]{3,2,1,0:T(8,128)(2,1)S(1)}, u32[]{:S(2)}, u32[]{:S(2)}) collective-permute-start(bf16[2,4,128,256]{3,2,1,0:T(8,128)(2,1)S(1)} %pad_maximum_fusion.4), channel_id=1, source_target_pairs={{1,0},{2,1},{3,2},{4,3},{5,4},{6,5},{7,6},{8,7},{9,8},{10,9},{11,1... | collective-permute-start | bytes 1572872 | tf_op jit(solution)/shard_map/ppermute | solution.py:315
  10.4 1.9 collective-permute-start
  12.3 9.2 %collective-permute-done.1 = bf16[2,4,128,256]{3,2,1,0:T(8,128)(2,1)S(1)} collective-permute-done((bf16[2,4,128,256]{3,2,1,0:T(8,128)(2,1)S(1)}, bf16[2,4,128,256]{3,2,1,0:T(8,128)(2,1)S(1)}, u32[]{:S(2)}, u32[]{:S(2)}) %collective-permute-start.1) | collective-permute-done | bytes 524320 | tf_op jit(solution)/shard_map/ppermute | solution.py:315
  21.5 10.0 %collective-permute-done = bf16[2,4,128,256]{3,2,1,0:T(8,128)(2,1)S(1)} collective-permute-done((bf16[2,4,128,256]{3,2,1,0:T(8,128)(2,1)S(1)}, bf16[2,4,128,256]{3,2,1,0:T(8,128)(2,1)S(1)}, u32[]{:S(2)}, u32[]{:S(2)}) %collective-permute-start) | collective-permute-done | bytes 524320 | tf_op jit(solution)/shard_map/ppermute | solution.py:315
  34.3 3.6 %collective-permute-start.3 = (bf16[2,4,128,256]{3,2,1,0:T(8,128)(2,1)}, bf16[2,4,128,256]{3,2,1,0:T(8,128)(2,1)S(1)}, u32[]{:S(2)}, u32[]{:S(2)}) collective-permute-start(bf16[2,4,128,256]{3,2,1,0:T(8,128)(2,1)} %pad_maximum_fusion.6), channel_id=1, source_target_pairs={{32,0},{64,32},{96,64},{33,1},{65,33},{97,65},{34,2},{66,34},{98,6... | collective-permute-start | bytes 1572872 | tf_op jit(solution)/shard_map/ppermute | solution.py:315
  38.1 3.9 %collective-permute-done.2.time_ref = bf16[2,4,128,256]{3,2,1,0:T(8,128)(2,1)S(1)} collective-permute-done((bf16[2,4,128,256]{3,2,1,0:T(8,128)(2,1)S(1)}, bf16[2,4,128,256]{3,2,1,0:T(8,128)(2,1)S(1)}, u32[]{:S(2)}, u32[]{:S(2)}) %collective-permute-start.2) | collective-permute-done | bytes 524320 | tf_op jit(solution)/shard_map/ppermute | solution.py:315
  42.0 6.6 %shard_map.75 = (f32[4,256,256]{2,1,0:T(8,128)S(1)}, bf16[4,2,128,256]{3,2,1,0:T(8,128)(2,1)S(1)}) custom-call(bf16[4,2,128,256]{3,2,1,0:T(8,128)(2,1)S(1)} %copy.13.own_ref, bf16[2,2,4,128,256]{4,3,2,1,0:T(8,128)(2,1)S(1)} %pad_maximum_fusion.1.rows_ref, bf16[2,4,128,256]{3,2,1,0:T(8,128)(2,1)S(1)} %collective-permute-done.2.time_ref, ...), custom_call_target="tpu_custom_call" | custom-call | flops 3623878656 | bytes 7208960 | tf_op jit(solution)/shard_map/pallas_call | solution.py:222
  48.6 4.9 %shard_map.76.own_ref.grad_ref = bf16[4,2,128,256]{3,2,1,0:T(8,128)(2,1)S(1)} custom-call(bf16[4,2,128,256]{3,2,1,0:T(8,128)(2,1)S(1)} %copy-done, bf16[2,2,4,128,256]{4,3,2,1,0:T(8,128)(2,1)S(1)} %pad_maximum_fusion.1.rows_ref, bf16[2,4,128,256]{3,2,1,0:T(8,128)(2,1)S(1)} %collective-permute-done.3.time_ref, bf16[9,3,256,256]{3,2,1,0:T(8,128)(2,1)S(1)} %bitcast.76, ...), custom_call_target="tpu_custom_call" | custom-call | flops 3623878656 | bytes 7208960 | tf_op jit(solution)/shard_map/pallas_call | solution.py:222
  53.5 5.0 %shard_map.80 = (f32[16,2,27,8,128]{4,3,2,1,0:T(8,128)S(1)}, bf16[16,2,27,8,128]{4,3,2,1,0:T(8,128)(2,1)S(1)}) custom-call(s32[1]{0:T(128)} %bitcast.28.core_ref, bf16[4,2,128,256]{3,2,1,0:T(8,128)(2,1)S(1)} %shard_map.76.own_ref.grad_ref, bf16[4,2,128,256]{3,2,1,0:T(8,128)(2,1)S(1)} %copy.13.own_ref, ...), custom_call_target="tpu_custom_call" | custom-call | flops 3623878656 | bytes 7929860 | tf_op jit(solution)/shard_map/pallas_call | solution.py:222
  58.6 5.6 %shard_map.79 = (f32[16,2,27,8,128]{4,3,2,1,0:T(8,128)S(1)}, bf16[16,2,27,8,128]{4,3,2,1,0:T(8,128)(2,1)S(1)}) custom-call(s32[1]{0:T(128)} %bitcast.28.core_ref, bf16[4,2,128,256]{3,2,1,0:T(8,128)(2,1)S(1)} %get-tuple-element.12.own_ref.active_ref, bf16[4,2,128,256]{3,2,1,0:T(8,128)(2,1)S(1)} %copy-done, ...), custom_call_target="tpu_custom_call" | custom-call | flops 3623878656 | bytes 7929860 | tf_op jit(solution)/shard_map/pallas_call | solution.py:222
  65.2 2.9 %collective-permute-done.8 = bf16[16,2,27,8,128]{4,3,2,1,0:T(8,128)(2,1)S(1)} collective-permute-done((bf16[16,2,27,8,128]{4,3,2,1,0:T(8,128)(2,1)S(1)}, bf16[16,2,27,8,128]{4,3,2,1,0:T(8,128)(2,1)S(1)}, u32[]{:S(2)}, u32[]{:S(2)}) %collective-permute-start.8) | collective-permute-done | bytes 1769504 | tf_op jit(solution)/shard_map/ppermute | solution.py:366
  68.8 26.8 %all_to_all.20.parts_ref = bf16[4,16,27,8,128]{4,3,2,1,0:T(8,128)(2,1)S(1)} all-to-all(bf16[4,16,27,8,128]{4,3,2,1,0:T(8,128)(2,1)S(1)} %bitcast.80), channel_id=1, replica_groups={{0,1,2,3},{4,5,6,7},{8,9,10,11},{12,13,14,15},{16,17,18,19},{20,21,22,2..., dimensions={0} | all-to-all | bytes 7077888 | tf_op jit(solution)/shard_map/all_to_all | solution.py:309
  96.1 15.6 %all_to_all.21 = bf16[16,27,8,128]{3,2,1,0:T(8,128)(2,1)S(1)} all-to-all(bf16[16,27,8,128]{3,2,1,0:T(8,128)(2,1)S(1)} %bitcast.75), channel_id=1, replica_groups={{0,4,8,12,16,20,24,28,64,68,72,76,80,84,88,92},{1,5,9,13,17,21,25,29,65..., dimensions={0} | all-to-all | bytes 1769472 | tf_op jit(solution)/shard_map/all_to_all | solution.py:309
  111.8 17.2 %all_to_all.22 = bf16[16,27,8,128]{3,2,1,0:T(8,128)(2,1)S(1)} all-to-all(bf16[16,27,8,128]{3,2,1,0:T(8,128)(2,1)S(1)} %bitcast.74), channel_id=1, replica_groups={{0,4,8,12,16,20,24,28,64,68,72,76,80,84,88,92},{1,5,9,13,17,21,25,29,65..., dimensions={0} | all-to-all | bytes 1769472 | tf_op jit(solution)/shard_map/all_to_all | solution.py:309
  129.5 27.2 %all_to_all.23 = bf16[4,16,27,8,128]{4,3,2,1,0:T(8,128)(2,1)S(1)} all-to-all(bf16[4,16,27,8,128]{4,3,2,1,0:T(8,128)(2,1)S(1)} %broadcast_in_dim.10), channel_id=1, replica_groups={{0,1,2,3},{4,5,6,7},{8,9,10,11},{12,13,14,15},{16,17,18,19},{20,21,22,2..., dimensions={0} | all-to-all | bytes 7077888 | tf_op jit(solution)/shard_map/all_to_all | solution.py:309
  156.9 5.5 %collective-permute-start.5 = (bf16[2,4,128,256]{3,2,1,0:T(8,128)(2,1)S(1)}, bf16[2,4,128,256]{3,2,1,0:T(8,128)(2,1)S(1)}, u32[]{:S(2)}, u32[]{:S(2)}) collective-permute-start(bf16[2,4,128,256]{3,2,1,0:T(8,128)(2,1)S(1)} %pad_maximum_fusion.8), channel_id=1, source_target_pairs={{1,0},{2,1},{3,2},{4,3},{5,4},{6,5},{7,6},{8,7},{9,8},{10,9},{11,1... | collective-permute-start | bytes 1572872 | tf_op jit(solution)/shard_map/ppermute | solution.py:315
  162.5 2.1 collective-permute-start.4
  164.6 9.7 %collective-permute-done.5 = bf16[2,4,128,256]{3,2,1,0:T(8,128)(2,1)S(1)} collective-permute-done((bf16[2,4,128,256]{3,2,1,0:T(8,128)(2,1)S(1)}, bf16[2,4,128,256]{3,2,1,0:T(8,128)(2,1)S(1)}, u32[]{:S(2)}, u32[]{:S(2)}) %collective-permute-start.5) | collective-permute-done | bytes 524320 | tf_op jit(solution)/shard_map/ppermute | solution.py:315
  174.3 10.1 %collective-permute-done.4 = bf16[2,4,128,256]{3,2,1,0:T(8,128)(2,1)S(1)} collective-permute-done((bf16[2,4,128,256]{3,2,1,0:T(8,128)(2,1)S(1)}, bf16[2,4,128,256]{3,2,1,0:T(8,128)(2,1)S(1)}, u32[]{:S(2)}, u32[]{:S(2)}) %collective-permute-start.4) | collective-permute-done | bytes 524320 | tf_op jit(solution)/shard_map/ppermute | solution.py:315
  186.4 3.6 %collective-permute-start.7 = (bf16[2,4,128,256]{3,2,1,0:T(8,128)(2,1)S(1)}, bf16[2,4,128,256]{3,2,1,0:T(8,128)(2,1)S(1)}, u32[]{:S(2)}, u32[]{:S(2)}) collective-permute-start(bf16[2,4,128,256]{3,2,1,0:T(8,128)(2,1)S(1)} %pad_maximum_fusion.10), channel_id=1, source_target_pairs={{32,0},{64,32},{96,64},{33,1},{65,33},{97,65},{34,2},{66,34},{98,6... | collective-permute-start | bytes 1572872 | tf_op jit(solution)/shard_map/ppermute | solution.py:315
  190.2 4.7 %collective-permute-done.6.time_ref = bf16[2,4,128,256]{3,2,1,0:T(8,128)(2,1)S(1)} collective-permute-done((bf16[2,4,128,256]{3,2,1,0:T(8,128)(2,1)S(1)}, bf16[2,4,128,256]{3,2,1,0:T(8,128)(2,1)S(1)}, u32[]{:S(2)}, u32[]{:S(2)}) %collective-permute-start.6) | collective-permute-done | bytes 524320 | tf_op jit(solution)/shard_map/ppermute | solution.py:315
  194.9 5.5 %shard_map.77 = bf16[4,2,128,256]{3,2,1,0:T(8,128)(2,1)} custom-call(bf16[4,2,128,256]{3,2,1,0:T(8,128)(2,1)S(1)} %get-tuple-element.12.own_ref.active_ref, bf16[2,2,4,128,256]{4,3,2,1,0:T(8,128)(2,1)S(1)} %pad_maximum_fusion.2.rows_ref, bf16[2,4,128,256]{3,2,1,0:T(8,128)(2,1)S(1)} %collective-permute-done.6.time_ref, bf16[9,3,256,256]{3,2,1,0:T(8,128)(2,1)S(1)} %bitcast.77, ...), custom_call_target="tpu_custom_call" | custom-call | flops 3623878656 | bytes 6684672 | tf_op jit(solution)/shard_map/pallas_call | solution.py:222
  200.5 5.8 %shard_map.78 = bf16[4,2,128,256]{3,2,1,0:T(8,128)(2,1)} custom-call(bf16[4,2,128,256]{3,2,1,0:T(8,128)(2,1)S(1)} %shard_map.76.own_ref.grad_ref, bf16[2,2,4,128,256]{4,3,2,1,0:T(8,128)(2,1)S(1)} %pad_maximum_fusion.2.rows_ref, bf16[2,4,128,256]{3,2,1,0:T(8,128)(2,1)S(1)} %collective-permute-done.7.time_ref, bf16[9,3,256,256]{3,2,1,0:T(8,128)(2,1)S(1)} %bitcast.79, ...), custom_call_target="tpu_custom_call" | custom-call | flops 3623878656 | bytes 7208960 | tf_op jit(solution)/shard_map/pallas_call | solution.py:222
  206.3 6.2 %assemble.1 = (f32[27,256,256]{2,1,0:T(8,128)}, f32[27,256,256]{2,1,0:T(8,128)}) custom-call(s32[1]{0:T(128)} %bitcast.28.core_ref, bf16[2,16,2,27,8,128]{5,4,3,2,1,0:T(8,128)(2,1)S(1)} %bitcast.71, bf16[2,16,2,27,8,128]{5,4,3,2,1,0:T(8,128)(2,1)S(1)} %bitcast.72), custom_call_target="tpu_custom_call" | custom-call | flops 16777216 | bytes 29360128 | tf_op jit(solution)/shard_map/assemble/pallas_call | solution.py:266
  (47 shorter events, 10.9 us)
Async XLA Ops:
  2.0 31.5 %slice-start = ((bf16[4,2,128,256]{3,2,1,0:T(8,128)(2,1)}), bf16[2,2,128,256]{3,2,1,0:T(8,128)(2,1)S(1)}, s32[]{:S(2)}) async-start(bf16[4,2,128,256]{3,2,1,0:T(8,128)(2,1)} %own_ref.3), calls=%async_computation.4 | async-start | bytes 524288 | tf_op jit(solution)/shard_map/slice | solution.py:329
  3.2 18.3 %collective-permute-start.1 = (bf16[2,4,128,256]{3,2,1,0:T(8,128)(2,1)S(1)}, bf16[2,4,128,256]{3,2,1,0:T(8,128)(2,1)S(1)}, u32[]{:S(2)}, u32[]{:S(2)}) collective-permute-start(bf16[2,4,128,256]{3,2,1,0:T(8,128)(2,1)S(1)} %pad_maximum_fusion.4), channel_id=1, source_target_pairs={{1,0},{2,1},{3,2},{4,3},{5,4},{6,5},{7,6},{8,7},{9,8},{10,9},{11,1... | collective-permute-start | bytes 1572872 | tf_op jit(solution)/shard_map/ppermute | solution.py:315
  10.4 21.1 %collective-permute-start = (bf16[2,4,128,256]{3,2,1,0:T(8,128)(2,1)S(1)}, bf16[2,4,128,256]{3,2,1,0:T(8,128)(2,1)S(1)}, u32[]{:S(2)}, u32[]{:S(2)}) collective-permute-start(bf16[2,4,128,256]{3,2,1,0:T(8,128)(2,1)S(1)} %pad_maximum_fusion.3), channel_id=1, source_target_pairs={{0,1},{1,2},{2,3},{3,4},{4,5},{5,6},{6,7},{7,8},{8,9},{9,10},{10,1... | collective-permute-start | bytes 1572872 | tf_op jit(solution)/shard_map/ppermute | solution.py:315
  31.5 10.5 %collective-permute-start.2 = (bf16[2,4,128,256]{3,2,1,0:T(8,128)(2,1)S(1)}, bf16[2,4,128,256]{3,2,1,0:T(8,128)(2,1)S(1)}, u32[]{:S(2)}, u32[]{:S(2)}) collective-permute-start(bf16[2,4,128,256]{3,2,1,0:T(8,128)(2,1)S(1)} %pad_maximum_fusion.5), channel_id=1, source_target_pairs={{0,32},{32,64},{64,96},{1,33},{33,65},{65,97},{2,34},{34,66},{66,9... | collective-permute-start | bytes 1572872 | tf_op jit(solution)/shard_map/ppermute | solution.py:315
  34.3 14.3 %collective-permute-start.3 = (bf16[2,4,128,256]{3,2,1,0:T(8,128)(2,1)}, bf16[2,4,128,256]{3,2,1,0:T(8,128)(2,1)S(1)}, u32[]{:S(2)}, u32[]{:S(2)}) collective-permute-start(bf16[2,4,128,256]{3,2,1,0:T(8,128)(2,1)} %pad_maximum_fusion.6), channel_id=1, source_target_pairs={{32,0},{64,32},{96,64},{33,1},{65,33},{97,65},{34,2},{66,34},{98,6... | collective-permute-start | bytes 1572872 | tf_op jit(solution)/shard_map/ppermute | solution.py:315
  42.0 6.6 %copy-start = (bf16[4,2,128,256]{3,2,1,0:T(8,128)(2,1)S(1)}, bf16[4,2,128,256]{3,2,1,0:T(8,128)(2,1)}, u32[]{:S(2)}) copy-start(bf16[4,2,128,256]{3,2,1,0:T(8,128)(2,1)} %own_ref.3) | copy-start | bytes 1572868
  42.0 6.6 %copy-start.2 = (bf16[3,3,3,256,256]{4,3,2,1,0:T(8,128)(2,1)S(1)}, bf16[3,3,3,256,256]{4,3,2,1,0:T(8,128)(2,1)}, u32[]{:S(2)}) copy-start(bf16[3,3,3,256,256]{4,3,2,1,0:T(8,128)(2,1)} %param.6) | copy-start | bytes 10616836
  58.5 6.2 %collective-permute-start.9 = (bf16[16,2,27,8,128]{4,3,2,1,0:T(8,128)(2,1)S(1)}, bf16[16,2,27,8,128]{4,3,2,1,0:T(8,128)(2,1)S(1)}, u32[]{:S(2)}, u32[]{:S(2)}) collective-permute-start(bf16[16,2,27,8,128]{4,3,2,1,0:T(8,128)(2,1)S(1)} %get-tuple-element.17), channel_id=1, source_target_pairs={{0,32},{32,0},{1,33},{33,1},{2,34},{34,2},{3,35},{35,3},{4,36},{36... | collective-permute-start | bytes 5308424 | tf_op jit(solution)/shard_map/ppermute | solution.py:367
  64.2 3.9 %collective-permute-start.8 = (bf16[16,2,27,8,128]{4,3,2,1,0:T(8,128)(2,1)S(1)}, bf16[16,2,27,8,128]{4,3,2,1,0:T(8,128)(2,1)S(1)}, u32[]{:S(2)}, u32[]{:S(2)}) collective-permute-start(bf16[16,2,27,8,128]{4,3,2,1,0:T(8,128)(2,1)S(1)} %get-tuple-element.15), channel_id=1, source_target_pairs={{0,32},{32,0},{1,33},{33,1},{2,34},{34,2},{3,35},{35,3},{4,36},{36... | collective-permute-start | bytes 5308424 | tf_op jit(solution)/shard_map/ppermute | solution.py:366
  156.7 49.6 %collective-permute-start.10 = (bf16[4,16,27,8,128]{4,3,2,1,0:T(8,128)(2,1)S(1)}, bf16[4,16,27,8,128]{4,3,2,1,0:T(8,128)(2,1)S(1)}, u32[]{:S(2)}, u32[]{:S(2)}) collective-permute-start(bf16[4,16,27,8,128]{4,3,2,1,0:T(8,128)(2,1)S(1)} %all_to_all.23), channel_id=1, source_target_pairs={{0,32},{32,0},{1,33},{33,1},{2,34},{34,2},{3,35},{35,3},{4,36},{36... | collective-permute-start | bytes 10616840 | tf_op jit(solution)/shard_map/ppermute | solution.py:378
  156.9 17.4 %collective-permute-start.5 = (bf16[2,4,128,256]{3,2,1,0:T(8,128)(2,1)S(1)}, bf16[2,4,128,256]{3,2,1,0:T(8,128)(2,1)S(1)}, u32[]{:S(2)}, u32[]{:S(2)}) collective-permute-start(bf16[2,4,128,256]{3,2,1,0:T(8,128)(2,1)S(1)} %pad_maximum_fusion.8), channel_id=1, source_target_pairs={{1,0},{2,1},{3,2},{4,3},{5,4},{6,5},{7,6},{8,7},{9,8},{10,9},{11,1... | collective-permute-start | bytes 1572872 | tf_op jit(solution)/shard_map/ppermute | solution.py:315
  162.4 32.5 %copy-start.1 = (bf16[4,2,128,256]{3,2,1,0:T(8,128)(2,1)S(1)}, bf16[4,2,128,256]{3,2,1,0:T(8,128)(2,1)}, u32[]{:S(2)}) copy-start(bf16[4,2,128,256]{3,2,1,0:T(8,128)(2,1)} %latents_ref.3) | copy-start | bytes 1572868
  162.5 21.8 %collective-permute-start.4 = (bf16[2,4,128,256]{3,2,1,0:T(8,128)(2,1)S(1)}, bf16[2,4,128,256]{3,2,1,0:T(8,128)(2,1)S(1)}, u32[]{:S(2)}, u32[]{:S(2)}) collective-permute-start(bf16[2,4,128,256]{3,2,1,0:T(8,128)(2,1)S(1)} %pad_maximum_fusion.7), channel_id=1, source_target_pairs={{0,1},{1,2},{2,3},{3,4},{4,5},{5,6},{6,7},{7,8},{8,9},{9,10},{10,1... | collective-permute-start | bytes 1572872 | tf_op jit(solution)/shard_map/ppermute | solution.py:315
  184.4 10.5 %collective-permute-start.6 = (bf16[2,4,128,256]{3,2,1,0:T(8,128)(2,1)S(1)}, bf16[2,4,128,256]{3,2,1,0:T(8,128)(2,1)S(1)}, u32[]{:S(2)}, u32[]{:S(2)}) collective-permute-start(bf16[2,4,128,256]{3,2,1,0:T(8,128)(2,1)S(1)} %pad_maximum_fusion.9), channel_id=1, source_target_pairs={{0,32},{32,64},{64,96},{1,33},{33,65},{65,97},{2,34},{34,66},{66,9... | collective-permute-start | bytes 1572872 | tf_op jit(solution)/shard_map/ppermute | solution.py:315
  186.4 14.0 %collective-permute-start.7 = (bf16[2,4,128,256]{3,2,1,0:T(8,128)(2,1)S(1)}, bf16[2,4,128,256]{3,2,1,0:T(8,128)(2,1)S(1)}, u32[]{:S(2)}, u32[]{:S(2)}) collective-permute-start(bf16[2,4,128,256]{3,2,1,0:T(8,128)(2,1)S(1)} %pad_maximum_fusion.10), channel_id=1, source_target_pairs={{32,0},{64,32},{96,64},{33,1},{65,33},{97,65},{34,2},{66,34},{98,6... | collective-permute-start | bytes 1572872 | tf_op jit(solution)/shard_map/ppermute | solution.py:315
  190.2 10.3 %copy-start.3 = (bf16[3,3,3,256,256]{4,3,2,1,0:T(8,128)(2,1)S(1)}, bf16[3,3,3,256,256]{4,3,2,1,0:T(8,128)(2,1)}, u32[]{:S(2)}) copy-start(bf16[3,3,3,256,256]{4,3,2,1,0:T(8,128)(2,1)} %param.5) | copy-start | bytes 10616836

commit v7 on v6

--- a/solution.py
+++ b/solution.py
@@ -42,7 +42,7 @@
     return jnp.where(column == edge, 0.0, turned)
 
 
-def conv_frame(ext_ref, kernel_ref, t, transposed):
+def conv_frame(ext_ref, kernel_ref, t, transposed, copies):
     parts = []
     for i in range(3):
         for j in range(3):
@@ -52,6 +52,7 @@
     lhs = jnp.concatenate(parts, axis=1)
     sums = []
     for k in range(3):
+        pl.when(t == 0)(copies[k].wait)
         taps = [kernel_ref[k, n] for n in range(9)]
         if transposed:
             rhs = jnp.concatenate(taps, axis=1)
@@ -86,11 +87,9 @@
 def hidden_kernel(own_ref, rows_ref, time_ref, source_ref, hidden_ref, active_ref, ext_ref, kernel_ref, sem):
     copies = load_taps(source_ref, kernel_ref, sem)
     fill_ext(ext_ref, own_ref, rows_ref, time_ref, 2, 0)
-    for copy in copies:
-        copy.wait()
 
     def body(t, carry):
-        hidden = conv_frame(ext_ref, kernel_ref, t, False)
+        hidden = conv_frame(ext_ref, kernel_ref, t, False, copies)
         hidden_ref[t] = hidden
         active_ref[t] = split_rows((hidden * jax.nn.sigmoid(hidden)).astype(BF))
         return carry
@@ -101,11 +100,9 @@
 def hidden_grad_kernel(own_ref, rows_ref, time_ref, source_ref, hidden_ref, out_ref, ext_ref, kernel_ref, sem):
     copies = load_taps(source_ref, kernel_ref, sem)
     fill_ext(ext_ref, own_ref, rows_ref, time_ref, 0, 1)
-    for copy in copies:
-        copy.wait()
 
     def body(t, carry):
-        grad = conv_frame(ext_ref, kernel_ref, t, True)
+        grad = conv_frame(ext_ref, kernel_ref, t, True, copies)
         out_ref[t] = split_rows((grad * gate_grad(hidden_ref[t])).astype(BF))
         return carry
 
@@ -115,11 +112,9 @@
 def decoded_kernel(own_ref, rows_ref, time_ref, source_ref, latents_ref, out_ref, ext_ref, kernel_ref, sem):
     copies = load_taps(source_ref, kernel_ref, sem)
     fill_ext(ext_ref, own_ref, rows_ref, time_ref, 2, 0)
-    for copy in copies:
-        copy.wait()
 
     def body(t, carry):
-        branch = split_rows(conv_frame(ext_ref, kernel_ref, t, False))
+        branch = split_rows(conv_frame(ext_ref, kernel_ref, t, False, copies))
         out_ref[t] = (latents_ref[t].astype(F32) + branch).astype(BF)
         return carry
 
@@ -131,11 +126,9 @@
 ):
     copies = load_taps(source_ref, kernel_ref, sem)
     fill_ext(ext_ref, own_ref, rows_ref, time_ref, 0, 1)
-    for copy in copies:
-        copy.wait()
 
     def body(t, carry):
-        inner = split_rows(conv_frame(ext_ref, kernel_ref, t, True))
+        inner = split_rows(conv_frame(ext_ref, kernel_ref, t, True, copies))
         gate = gate_grad(latents_ref[t].astype(F32))
         out_ref[t] = (upstream_ref[t].astype(F32) + inner * gate).astype(BF)
         return carry

time: 213 us -> 218 us (1.023)
  Pallas kernels: 40.2 us -> 44.9 us
    pallas_call x8, Pallas kernels: 34 us -> 38.7 us  [call(): pl.pallas_call(kernel, out_shape=outs, in_specs=[pl.BlockSpec(memory_spac...]
  transfers between devices with their start and end apart: 11 -> 11, of which waited for: 7 -> 7; matrix products, arithmetic and copies ran while one was open for 1% -> 1% of each run, Pallas kernels for 11% -> 12%
where the time goes in v7:
time: 218 us; the launch traced here: 217 us
  blocking collectives  86.8 us (40%)
  waiting for transfers between devices  50.2 us (23%)
  Pallas kernels  44.9 us (21%)
  starting transfers between devices  28.6 us (13%)
  other arithmetic  3.9 us (2%)
    all_to_all x4, blocking collectives, exchange(): lax.all_to_all(value, ALL, 0, 0, axis_index_groups=groups, tiled=False)  86.8 us
    ppermute x8, waiting for transfers between devices, swap(): return lax.ppermute(value, axis, pairs)  47.3 us
    pallas_call x8, Pallas kernels, call(): pl.pallas_call(kernel, out_shape=outs, in_specs=[pl.BlockSpec(memory_spac...  38.7 us
    ppermute x8, starting transfers between devices, swap(): return lax.ppermute(value, axis, pairs)  27.9 us
    pallas_call x1, Pallas kernels, assemble(): pl.pallas_call(assemble_kernel, out_shape=(shape, shape), grid=(TAPS // S...  6.22 us
  transfers between devices with their start and end apart: 11, of which 7 were waited for; matrix products, arithmetic and copies ran while one was open for 1% of the time, Pallas kernels for 12%

profile of v7, /device:TPU:96, one launch (start us, length us, event | category | flops | bytes accessed | tf_op | source)
XLA Modules:
  0.0 217.2 jit_solution(11827879283601123950)
XLA Ops:
  3.2 7.1 %collective-permute-start.1 = (bf16[2,4,128,256]{3,2,1,0:T(8,128)(2,1)S(1)}, bf16[2,4,128,256]{3,2,1,0:T(8,128)(2,1)S(1)}, u32[]{:S(2)}, u32[]{:S(2)}) collective-permute-start(bf16[2,4,128,256]{3,2,1,0:T(8,128)(2,1)S(1)} %pad_maximum_fusion.4), channel_id=1, source_target_pairs={{1,0},{2,1},{3,2},{4,3},{5,4},{6,5},{7,6},{8,7},{9,8},{10,9},{11,1... | collective-permute-start | bytes 1572872 | tf_op jit(solution)/shard_map/ppermute | solution.py:308
  10.4 1.9 collective-permute-start
  12.3 9.2 %collective-permute-done.1 = bf16[2,4,128,256]{3,2,1,0:T(8,128)(2,1)S(1)} collective-permute-done((bf16[2,4,128,256]{3,2,1,0:T(8,128)(2,1)S(1)}, bf16[2,4,128,256]{3,2,1,0:T(8,128)(2,1)S(1)}, u32[]{:S(2)}, u32[]{:S(2)}) %collective-permute-start.1) | collective-permute-done | bytes 524320 | tf_op jit(solution)/shard_map/ppermute | solution.py:308
  21.5 10.0 %collective-permute-done = bf16[2,4,128,256]{3,2,1,0:T(8,128)(2,1)S(1)} collective-permute-done((bf16[2,4,128,256]{3,2,1,0:T(8,128)(2,1)S(1)}, bf16[2,4,128,256]{3,2,1,0:T(8,128)(2,1)S(1)}, u32[]{:S(2)}, u32[]{:S(2)}) %collective-permute-start) | collective-permute-done | bytes 524320 | tf_op jit(solution)/shard_map/ppermute | solution.py:308
  34.3 3.6 %collective-permute-start.3 = (bf16[2,4,128,256]{3,2,1,0:T(8,128)(2,1)}, bf16[2,4,128,256]{3,2,1,0:T(8,128)(2,1)S(1)}, u32[]{:S(2)}, u32[]{:S(2)}) collective-permute-start(bf16[2,4,128,256]{3,2,1,0:T(8,128)(2,1)} %pad_maximum_fusion.6), channel_id=1, source_target_pairs={{32,0},{64,32},{96,64},{33,1},{65,33},{97,65},{34,2},{66,34},{98,6... | collective-permute-start | bytes 1572872 | tf_op jit(solution)/shard_map/ppermute | solution.py:308
  38.1 3.9 %collective-permute-done.2.time_ref = bf16[2,4,128,256]{3,2,1,0:T(8,128)(2,1)S(1)} collective-permute-done((bf16[2,4,128,256]{3,2,1,0:T(8,128)(2,1)S(1)}, bf16[2,4,128,256]{3,2,1,0:T(8,128)(2,1)S(1)}, u32[]{:S(2)}, u32[]{:S(2)}) %collective-permute-start.2) | collective-permute-done | bytes 524320 | tf_op jit(solution)/shard_map/ppermute | solution.py:308
  42.0 7.1 %shard_map.75 = (f32[4,256,256]{2,1,0:T(8,128)S(1)}, bf16[4,2,128,256]{3,2,1,0:T(8,128)(2,1)S(1)}) custom-call(bf16[4,2,128,256]{3,2,1,0:T(8,128)(2,1)S(1)} %copy.13.own_ref, bf16[2,2,4,128,256]{4,3,2,1,0:T(8,128)(2,1)S(1)} %pad_maximum_fusion.1.rows_ref, bf16[2,4,128,256]{3,2,1,0:T(8,128)(2,1)S(1)} %collective-permute-done.2.time_ref, ...), custom_call_target="tpu_custom_call" | custom-call | flops 3623878656 | bytes 7208960 | tf_op jit(solution)/shard_map/pallas_call | solution.py:215
  49.2 6.4 %shard_map.76.own_ref.grad_ref = bf16[4,2,128,256]{3,2,1,0:T(8,128)(2,1)S(1)} custom-call(bf16[4,2,128,256]{3,2,1,0:T(8,128)(2,1)S(1)} %copy-done, bf16[2,2,4,128,256]{4,3,2,1,0:T(8,128)(2,1)S(1)} %pad_maximum_fusion.1.rows_ref, bf16[2,4,128,256]{3,2,1,0:T(8,128)(2,1)S(1)} %collective-permute-done.3.time_ref, bf16[9,3,256,256]{3,2,1,0:T(8,128)(2,1)S(1)} %bitcast.76, ...), custom_call_target="tpu_custom_call" | custom-call | flops 3623878656 | bytes 7208960 | tf_op jit(solution)/shard_map/pallas_call | solution.py:215
  55.6 5.0 %shard_map.80 = (f32[16,2,27,8,128]{4,3,2,1,0:T(8,128)S(1)}, bf16[16,2,27,8,128]{4,3,2,1,0:T(8,128)(2,1)S(1)}) custom-call(s32[1]{0:T(128)} %bitcast.28.core_ref, bf16[4,2,128,256]{3,2,1,0:T(8,128)(2,1)S(1)} %shard_map.76.own_ref.grad_ref, bf16[4,2,128,256]{3,2,1,0:T(8,128)(2,1)S(1)} %copy.13.own_ref, ...), custom_call_target="tpu_custom_call" | custom-call | flops 3623878656 | bytes 7929860 | tf_op jit(solution)/shard_map/pallas_call | solution.py:215
  60.7 5.6 %shard_map.79 = (f32[16,2,27,8,128]{4,3,2,1,0:T(8,128)S(1)}, bf16[16,2,27,8,128]{4,3,2,1,0:T(8,128)(2,1)S(1)}) custom-call(s32[1]{0:T(128)} %bitcast.28.core_ref, bf16[4,2,128,256]{3,2,1,0:T(8,128)(2,1)S(1)} %get-tuple-element.12.own_ref.active_ref, bf16[4,2,128,256]{3,2,1,0:T(8,128)(2,1)S(1)} %copy-done, ...), custom_call_target="tpu_custom_call" | custom-call | flops 3623878656 | bytes 7929860 | tf_op jit(solution)/shard_map/pallas_call | solution.py:215
  67.2 2.9 %collective-permute-done.8 = bf16[16,2,27,8,128]{4,3,2,1,0:T(8,128)(2,1)S(1)} collective-permute-done((bf16[16,2,27,8,128]{4,3,2,1,0:T(8,128)(2,1)S(1)}, bf16[16,2,27,8,128]{4,3,2,1,0:T(8,128)(2,1)S(1)}, u32[]{:S(2)}, u32[]{:S(2)}) %collective-permute-start.8) | collective-permute-done | bytes 1769504 | tf_op jit(solution)/shard_map/ppermute | solution.py:359
  70.9 26.8 %all_to_all.20.parts_ref = bf16[4,16,27,8,128]{4,3,2,1,0:T(8,128)(2,1)S(1)} all-to-all(bf16[4,16,27,8,128]{4,3,2,1,0:T(8,128)(2,1)S(1)} %bitcast.80), channel_id=1, replica_groups={{0,1,2,3},{4,5,6,7},{8,9,10,11},{12,13,14,15},{16,17,18,19},{20,21,22,2..., dimensions={0} | all-to-all | bytes 7077888 | tf_op jit(solution)/shard_map/all_to_all | solution.py:302
  98.2 15.6 %all_to_all.21 = bf16[16,27,8,128]{3,2,1,0:T(8,128)(2,1)S(1)} all-to-all(bf16[16,27,8,128]{3,2,1,0:T(8,128)(2,1)S(1)} %bitcast.75), channel_id=1, replica_groups={{0,4,8,12,16,20,24,28,64,68,72,76,80,84,88,92},{1,5,9,13,17,21,25,29,65..., dimensions={0} | all-to-all | bytes 1769472 | tf_op jit(solution)/shard_map/all_to_all | solution.py:302
  113.9 17.2 %all_to_all.22 = bf16[16,27,8,128]{3,2,1,0:T(8,128)(2,1)S(1)} all-to-all(bf16[16,27,8,128]{3,2,1,0:T(8,128)(2,1)S(1)} %bitcast.74), channel_id=1, replica_groups={{0,4,8,12,16,20,24,28,64,68,72,76,80,84,88,92},{1,5,9,13,17,21,25,29,65..., dimensions={0} | all-to-all | bytes 1769472 | tf_op jit(solution)/shard_map/all_to_all | solution.py:302
  131.6 27.2 %all_to_all.23 = bf16[4,16,27,8,128]{4,3,2,1,0:T(8,128)(2,1)S(1)} all-to-all(bf16[4,16,27,8,128]{4,3,2,1,0:T(8,128)(2,1)S(1)} %broadcast_in_dim.10), channel_id=1, replica_groups={{0,1,2,3},{4,5,6,7},{8,9,10,11},{12,13,14,15},{16,17,18,19},{20,21,22,2..., dimensions={0} | all-to-all | bytes 7077888 | tf_op jit(solution)/shard_map/all_to_all | solution.py:302
  159.0 5.5 %collective-permute-start.5 = (bf16[2,4,128,256]{3,2,1,0:T(8,128)(2,1)S(1)}, bf16[2,4,128,256]{3,2,1,0:T(8,128)(2,1)S(1)}, u32[]{:S(2)}, u32[]{:S(2)}) collective-permute-start(bf16[2,4,128,256]{3,2,1,0:T(8,128)(2,1)S(1)} %pad_maximum_fusion.8), channel_id=1, source_target_pairs={{1,0},{2,1},{3,2},{4,3},{5,4},{6,5},{7,6},{8,7},{9,8},{10,9},{11,1... | collective-permute-start | bytes 1572872 | tf_op jit(solution)/shard_map/ppermute | solution.py:308
  164.6 2.2 %collective-permute-start.4 = (bf16[2,4,128,256]{3,2,1,0:T(8,128)(2,1)S(1)}, bf16[2,4,128,256]{3,2,1,0:T(8,128)(2,1)S(1)}, u32[]{:S(2)}, u32[]{:S(2)}) collective-permute-start(bf16[2,4,128,256]{3,2,1,0:T(8,128)(2,1)S(1)} %pad_maximum_fusion.7), channel_id=1, source_target_pairs={{0,1},{1,2},{2,3},{3,4},{4,5},{5,6},{6,7},{7,8},{8,9},{9,10},{10,1... | collective-permute-start | bytes 1572872 | tf_op jit(solution)/shard_map/ppermute | solution.py:308
  166.8 9.5 %collective-permute-done.5 = bf16[2,4,128,256]{3,2,1,0:T(8,128)(2,1)S(1)} collective-permute-done((bf16[2,4,128,256]{3,2,1,0:T(8,128)(2,1)S(1)}, bf16[2,4,128,256]{3,2,1,0:T(8,128)(2,1)S(1)}, u32[]{:S(2)}, u32[]{:S(2)}) %collective-permute-start.5) | collective-permute-done | bytes 524320 | tf_op jit(solution)/shard_map/ppermute | solution.py:308
  176.4 10.1 %collective-permute-done.4 = bf16[2,4,128,256]{3,2,1,0:T(8,128)(2,1)S(1)} collective-permute-done((bf16[2,4,128,256]{3,2,1,0:T(8,128)(2,1)S(1)}, bf16[2,4,128,256]{3,2,1,0:T(8,128)(2,1)S(1)}, u32[]{:S(2)}, u32[]{:S(2)}) %collective-permute-start.4) | collective-permute-done | bytes 524320 | tf_op jit(solution)/shard_map/ppermute | solution.py:308
  188.5 3.6 %collective-permute-start.7 = (bf16[2,4,128,256]{3,2,1,0:T(8,128)(2,1)S(1)}, bf16[2,4,128,256]{3,2,1,0:T(8,128)(2,1)S(1)}, u32[]{:S(2)}, u32[]{:S(2)}) collective-permute-start(bf16[2,4,128,256]{3,2,1,0:T(8,128)(2,1)S(1)} %pad_maximum_fusion.10), channel_id=1, source_target_pairs={{32,0},{64,32},{96,64},{33,1},{65,33},{97,65},{34,2},{66,34},{98,6... | collective-permute-start | bytes 1572872 | tf_op jit(solution)/shard_map/ppermute | solution.py:308
  192.3 4.7 %collective-permute-done.6.time_ref = bf16[2,4,128,256]{3,2,1,0:T(8,128)(2,1)S(1)} collective-permute-done((bf16[2,4,128,256]{3,2,1,0:T(8,128)(2,1)S(1)}, bf16[2,4,128,256]{3,2,1,0:T(8,128)(2,1)S(1)}, u32[]{:S(2)}, u32[]{:S(2)}) %collective-permute-start.6) | collective-permute-done | bytes 524320 | tf_op jit(solution)/shard_map/ppermute | solution.py:308
  197.0 6.7 %shard_map.77 = bf16[4,2,128,256]{3,2,1,0:T(8,128)(2,1)} custom-call(bf16[4,2,128,256]{3,2,1,0:T(8,128)(2,1)S(1)} %get-tuple-element.12.own_ref.active_ref, bf16[2,2,4,128,256]{4,3,2,1,0:T(8,128)(2,1)S(1)} %pad_maximum_fusion.2.rows_ref, bf16[2,4,128,256]{3,2,1,0:T(8,128)(2,1)S(1)} %collective-permute-done.6.time_ref, bf16[9,3,256,256]{3,2,1,0:T(8,128)(2,1)S(1)} %bitcast.77, ...), custom_call_target="tpu_custom_call" | custom-call | flops 3623878656 | bytes 6684672 | tf_op jit(solution)/shard_map/pallas_call | solution.py:215
  203.7 7.3 %shard_map.78 = bf16[4,2,128,256]{3,2,1,0:T(8,128)(2,1)} custom-call(bf16[4,2,128,256]{3,2,1,0:T(8,128)(2,1)S(1)} %shard_map.76.own_ref.grad_ref, bf16[2,2,4,128,256]{4,3,2,1,0:T(8,128)(2,1)S(1)} %pad_maximum_fusion.2.rows_ref, bf16[2,4,128,256]{3,2,1,0:T(8,128)(2,1)S(1)} %collective-permute-done.7.time_ref, bf16[9,3,256,256]{3,2,1,0:T(8,128)(2,1)S(1)} %bitcast.79, ...), custom_call_target="tpu_custom_call" | custom-call | flops 3623878656 | bytes 7208960 | tf_op jit(solution)/shard_map/pallas_call | solution.py:215
  211.0 6.2 %assemble.1 = (f32[27,256,256]{2,1,0:T(8,128)}, f32[27,256,256]{2,1,0:T(8,128)}) custom-call(s32[1]{0:T(128)} %bitcast.28.core_ref, bf16[2,16,2,27,8,128]{5,4,3,2,1,0:T(8,128)(2,1)S(1)} %bitcast.71, bf16[2,16,2,27,8,128]{5,4,3,2,1,0:T(8,128)(2,1)S(1)} %bitcast.72), custom_call_target="tpu_custom_call" | custom-call | flops 16777216 | bytes 29360128 | tf_op jit(solution)/shard_map/assemble/pallas_call | solution.py:259
  (47 shorter events, 10.9 us)
Async XLA Ops:
  2.0 31.5 %slice-start = ((bf16[4,2,128,256]{3,2,1,0:T(8,128)(2,1)}), bf16[2,2,128,256]{3,2,1,0:T(8,128)(2,1)S(1)}, s32[]{:S(2)}) async-start(bf16[4,2,128,256]{3,2,1,0:T(8,128)(2,1)} %own_ref.3), calls=%async_computation.4 | async-start | bytes 524288 | tf_op jit(solution)/shard_map/slice | solution.py:322
  3.2 18.3 %collective-permute-start.1 = (bf16[2,4,128,256]{3,2,1,0:T(8,128)(2,1)S(1)}, bf16[2,4,128,256]{3,2,1,0:T(8,128)(2,1)S(1)}, u32[]{:S(2)}, u32[]{:S(2)}) collective-permute-start(bf16[2,4,128,256]{3,2,1,0:T(8,128)(2,1)S(1)} %pad_maximum_fusion.4), channel_id=1, source_target_pairs={{1,0},{2,1},{3,2},{4,3},{5,4},{6,5},{7,6},{8,7},{9,8},{10,9},{11,1... | collective-permute-start | bytes 1572872 | tf_op jit(solution)/shard_map/ppermute | solution.py:308
  10.4 21.1 %collective-permute-start = (bf16[2,4,128,256]{3,2,1,0:T(8,128)(2,1)S(1)}, bf16[2,4,128,256]{3,2,1,0:T(8,128)(2,1)S(1)}, u32[]{:S(2)}, u32[]{:S(2)}) collective-permute-start(bf16[2,4,128,256]{3,2,1,0:T(8,128)(2,1)S(1)} %pad_maximum_fusion.3), channel_id=1, source_target_pairs={{0,1},{1,2},{2,3},{3,4},{4,5},{5,6},{6,7},{7,8},{8,9},{9,10},{10,1... | collective-permute-start | bytes 1572872 | tf_op jit(solution)/shard_map/ppermute | solution.py:308
  31.5 10.5 %collective-permute-start.2 = (bf16[2,4,128,256]{3,2,1,0:T(8,128)(2,1)S(1)}, bf16[2,4,128,256]{3,2,1,0:T(8,128)(2,1)S(1)}, u32[]{:S(2)}, u32[]{:S(2)}) collective-permute-start(bf16[2,4,128,256]{3,2,1,0:T(8,128)(2,1)S(1)} %pad_maximum_fusion.5), channel_id=1, source_target_pairs={{0,32},{32,64},{64,96},{1,33},{33,65},{65,97},{2,34},{34,66},{66,9... | collective-permute-start | bytes 1572872 | tf_op jit(solution)/shard_map/ppermute | solution.py:308
  34.3 14.8 %collective-permute-start.3 = (bf16[2,4,128,256]{3,2,1,0:T(8,128)(2,1)}, bf16[2,4,128,256]{3,2,1,0:T(8,128)(2,1)S(1)}, u32[]{:S(2)}, u32[]{:S(2)}) collective-permute-start(bf16[2,4,128,256]{3,2,1,0:T(8,128)(2,1)} %pad_maximum_fusion.6), channel_id=1, source_target_pairs={{32,0},{64,32},{96,64},{33,1},{65,33},{97,65},{34,2},{66,34},{98,6... | collective-permute-start | bytes 1572872 | tf_op jit(solution)/shard_map/ppermute | solution.py:308
  42.0 7.1 %copy-start = (bf16[4,2,128,256]{3,2,1,0:T(8,128)(2,1)S(1)}, bf16[4,2,128,256]{3,2,1,0:T(8,128)(2,1)}, u32[]{:S(2)}) copy-start(bf16[4,2,128,256]{3,2,1,0:T(8,128)(2,1)} %own_ref.3) | copy-start | bytes 1572868
  42.0 7.1 %copy-start.2 = (bf16[3,3,3,256,256]{4,3,2,1,0:T(8,128)(2,1)S(1)}, bf16[3,3,3,256,256]{4,3,2,1,0:T(8,128)(2,1)}, u32[]{:S(2)}) copy-start(bf16[3,3,3,256,256]{4,3,2,1,0:T(8,128)(2,1)} %param.6) | copy-start | bytes 10616836
  60.6 6.2 %collective-permute-start.9 = (bf16[16,2,27,8,128]{4,3,2,1,0:T(8,128)(2,1)S(1)}, bf16[16,2,27,8,128]{4,3,2,1,0:T(8,128)(2,1)S(1)}, u32[]{:S(2)}, u32[]{:S(2)}) collective-permute-start(bf16[16,2,27,8,128]{4,3,2,1,0:T(8,128)(2,1)S(1)} %get-tuple-element.17), channel_id=1, source_target_pairs={{0,32},{32,0},{1,33},{33,1},{2,34},{34,2},{3,35},{35,3},{4,36},{36... | collective-permute-start | bytes 5308424 | tf_op jit(solution)/shard_map/ppermute | solution.py:360
  66.3 3.9 %collective-permute-start.8 = (bf16[16,2,27,8,128]{4,3,2,1,0:T(8,128)(2,1)S(1)}, bf16[16,2,27,8,128]{4,3,2,1,0:T(8,128)(2,1)S(1)}, u32[]{:S(2)}, u32[]{:S(2)}) collective-permute-start(bf16[16,2,27,8,128]{4,3,2,1,0:T(8,128)(2,1)S(1)} %get-tuple-element.15), channel_id=1, source_target_pairs={{0,32},{32,0},{1,33},{33,1},{2,34},{34,2},{3,35},{35,3},{4,36},{36... | collective-permute-start | bytes 5308424 | tf_op jit(solution)/shard_map/ppermute | solution.py:359
  158.8 52.2 %collective-permute-start.10 = (bf16[4,16,27,8,128]{4,3,2,1,0:T(8,128)(2,1)S(1)}, bf16[4,16,27,8,128]{4,3,2,1,0:T(8,128)(2,1)S(1)}, u32[]{:S(2)}, u32[]{:S(2)}) collective-permute-start(bf16[4,16,27,8,128]{4,3,2,1,0:T(8,128)(2,1)S(1)} %all_to_all.23), channel_id=1, source_target_pairs={{0,32},{32,0},{1,33},{33,1},{2,34},{34,2},{3,35},{35,3},{4,36},{36... | collective-permute-start | bytes 10616840 | tf_op jit(solution)/shard_map/ppermute | solution.py:371
  159.0 17.4 %collective-permute-start.5 = (bf16[2,4,128,256]{3,2,1,0:T(8,128)(2,1)S(1)}, bf16[2,4,128,256]{3,2,1,0:T(8,128)(2,1)S(1)}, u32[]{:S(2)}, u32[]{:S(2)}) collective-permute-start(bf16[2,4,128,256]{3,2,1,0:T(8,128)(2,1)S(1)} %pad_maximum_fusion.8), channel_id=1, source_target_pairs={{1,0},{2,1},{3,2},{4,3},{5,4},{6,5},{7,6},{8,7},{9,8},{10,9},{11,1... | collective-permute-start | bytes 1572872 | tf_op jit(solution)/shard_map/ppermute | solution.py:308
  164.5 32.5 %copy-start.1 = (bf16[4,2,128,256]{3,2,1,0:T(8,128)(2,1)S(1)}, bf16[4,2,128,256]{3,2,1,0:T(8,128)(2,1)}, u32[]{:S(2)}) copy-start(bf16[4,2,128,256]{3,2,1,0:T(8,128)(2,1)} %latents_ref.3) | copy-start | bytes 1572868
  164.6 21.8 %collective-permute-start.4 = (bf16[2,4,128,256]{3,2,1,0:T(8,128)(2,1)S(1)}, bf16[2,4,128,256]{3,2,1,0:T(8,128)(2,1)S(1)}, u32[]{:S(2)}, u32[]{:S(2)}) collective-permute-start(bf16[2,4,128,256]{3,2,1,0:T(8,128)(2,1)S(1)} %pad_maximum_fusion.7), channel_id=1, source_target_pairs={{0,1},{1,2},{2,3},{3,4},{4,5},{5,6},{6,7},{7,8},{8,9},{9,10},{10,1... | collective-permute-start | bytes 1572872 | tf_op jit(solution)/shard_map/ppermute | solution.py:308
  186.5 10.5 %collective-permute-start.6 = (bf16[2,4,128,256]{3,2,1,0:T(8,128)(2,1)S(1)}, bf16[2,4,128,256]{3,2,1,0:T(8,128)(2,1)S(1)}, u32[]{:S(2)}, u32[]{:S(2)}) collective-permute-start(bf16[2,4,128,256]{3,2,1,0:T(8,128)(2,1)S(1)} %pad_maximum_fusion.9), channel_id=1, source_target_pairs={{0,32},{32,64},{64,96},{1,33},{33,65},{65,97},{2,34},{34,66},{66,9... | collective-permute-start | bytes 1572872 | tf_op jit(solution)/shard_map/ppermute | solution.py:308
  188.5 15.2 %collective-permute-start.7 = (bf16[2,4,128,256]{3,2,1,0:T(8,128)(2,1)S(1)}, bf16[2,4,128,256]{3,2,1,0:T(8,128)(2,1)S(1)}, u32[]{:S(2)}, u32[]{:S(2)}) collective-permute-start(bf16[2,4,128,256]{3,2,1,0:T(8,128)(2,1)S(1)} %pad_maximum_fusion.10), channel_id=1, source_target_pairs={{32,0},{64,32},{96,64},{33,1},{65,33},{97,65},{34,2},{66,34},{98,6... | collective-permute-start | bytes 1572872 | tf_op jit(solution)/shard_map/ppermute | solution.py:308
  192.3 11.4 %copy-start.3 = (bf16[3,3,3,256,256]{4,3,2,1,0:T(8,128)(2,1)S(1)}, bf16[3,3,3,256,256]{4,3,2,1,0:T(8,128)(2,1)}, u32[]{:S(2)}) copy-start(bf16[3,3,3,256,256]{4,3,2,1,0:T(8,128)(2,1)} %param.5) | copy-start | bytes 10616836
